TPU v7x, 512 devices: a whole 4x4x16 slice. The times are simulated.
512 devices in a mesh: layer: 8 (over x, y_lo), trow: 2 (over y_hi), tcol: 32 (over z, core).
Axes of the slice: x: 4, y: 4 (y_hi: 2, y_lo: 2; y = y_hi * 2 + y_lo), z: 16, core: 2. Of those that a mesh axis runs over, the one named last changes fastest.
Arguments:
- act_rows: bfloat16 [8, 1024, 4096], P('layer', ('trow', 'tcol')), may hold values from -6 to 6
- back_rows: bfloat16 [8, 1024, 4096], P('layer', ('trow', 'tcol')), may hold values from -6 to 6
- act_cols: bfloat16 [8, 8192, 4096], P('layer', ('tcol', 'trow')), may hold values from -6 to 6
- back_cols: bfloat16 [8, 8192, 4096], P('layer', ('tcol', 'trow')), may hold values from -6 to 6
Outputs:
- kernel: float32 [1024, 8192], P(('trow', 'layer'), 'tcol')
All inputs are finite; a program needn't handle non-finite values.
Results may differ from a plain program's by a relative error of at most 0.0003.
Values may be sent and summed in bfloat16 or wider, within the bound.
No kernel may reach another device: no remote copies, remote signals or barrier semaphores. Data moves between devices by JAX's collectives and lax.ppermute only.
A program may use at most 64 MiB of HBM per device.

v0:
```python
import jax
import jax.numpy as jnp
from jax import lax
from jax.sharding import PartitionSpec as P


def in_one_piece(arrays, axis, dim, along):
    ends, at = ([], 0)
    for a in arrays[:-1]:
        at += a.shape[along]
        ends.append(at)
    both = jnp.concatenate(arrays, axis=along)
    return tuple(jnp.split(lax.all_gather(both, axis, axis=dim, tiled=True), ends, axis=along))


def in_blocks(value, dim, peers):
    before, after = (value.shape[:dim], value.shape[dim + 1 :])
    return jnp.moveaxis(value.reshape(*before, peers, -1, *after), dim, 0)


def summed_on_arrival(value, axis, dim):
    peers = lax.axis_size(axis)
    blocks = lax.all_to_all(in_blocks(value, dim, peers), axis, 0, 0, tiled=True)
    return jnp.sum(blocks, axis=0)


def kernel_terms(row_act, row_back, col_act, col_back):
    gram_act = jnp.einsum("lrd,lcd->lrc", row_act, col_act, preferred_element_type=jnp.float32)
    gram_back = jnp.einsum("lrd,lcd->lrc", row_back, col_back, preferred_element_type=jnp.float32)
    return jnp.sum(gram_act * gram_back, axis=0) / row_act.shape[2]


def local(act_rows, back_rows, act_cols, back_cols):
    row_act, row_back = in_one_piece((act_rows, back_rows), "tcol", 1, 0)
    col_act, col_back = in_one_piece((act_cols, back_cols), "trow", 1, 0)
    return summed_on_arrival(kernel_terms(row_act, row_back, col_act, col_back), "layer", 0)


def solution(mesh):
    in_specs = (
        P("layer", ("trow", "tcol"), None),
        P("layer", ("trow", "tcol"), None),
        P("layer", ("tcol", "trow"), None),
        P("layer", ("tcol", "trow"), None),
    )
    out_specs = P(("trow", "layer"), "tcol")
    return jax.shard_map(local, mesh=mesh, in_specs=in_specs, out_specs=out_specs, check_vma=False)
```

profile of v0, /device:TPU:24, one launch (start us, length us, event | category | flops | bytes accessed | tf_op | source)
XLA Modules:
  0.0 193.7 jit_solution(17718104956702732244)
XLA Ops:
  6.5 0.0 copy-start.1
  6.5 0.0 copy-start
  6.5 0.0 all-gather.5.cloned.1.call-start
  6.5 3.1 %pad_maximum_fusion = bf16[2,128,4096]{2,1,0:T(8,128)(2,1)} fusion(bf16[1,128,4096]{2,1,0:T(8,128)(2,1)} %param.7, bf16[1,128,4096]{2,1,0:T(8,128)(2,1)} %param.6), kind=kLoop, calls=%fused_computation.6 | loop fusion | flops 1048576 | bytes 4194304 | tf_op jit(solution)/shard_map/concatenate | solution.py:12
  9.7 0.0 all-gather.5.cloned.1.call-update
  9.7 0.0 all-gather.3.cloned.1.call-start
  9.7 0.0 copy-done.1
  9.7 0.0 copy-done
  9.7 0.7 pad_maximum_fusion.1
  10.5 0.0 all-gather.3.cloned.1.call-update
  10.5 70.4 %all-gather.5.cloned.1.call-done = bf16[2,256,4096]{2,1,0:T(8,128)(2,1)} async-done(((bf16[2,128,4096]{2,1,0:T(8,128)(2,1)}), bf16[2,256,4096]{2,1,0:T(8,128)(2,1)}) %all-gather.5.cloned.1.call-update) | async-done | bytes 4194320 | tf_op jit(solution)/shard_map/all_gather | solution.py:13
  80.9 82.1 %all-gather.3.cloned.1.call-done = bf16[2,512,4096]{2,1,0:T(8,128)(2,1)} async-done(((bf16[2,16,4096]{2,1,0:T(8,128)(2,1)}), bf16[2,512,4096]{2,1,0:T(8,128)(2,1)}) %all-gather.3.cloned.1.call-update) | async-done | bytes 8388624 | tf_op jit(solution)/shard_map/all_gather | solution.py:13
  163.0 0.0 copy-start.2
  163.0 4.3 %fusion = f32[512,256]{1,0:T(8,128)S(1)} fusion(bf16[2,512,4096]{2,1,0:T(8,128)(2,1)} %all-gather.3.cloned.1.call-done, bf16[2,256,4096]{2,1,0:T(8,128)(2,1)} %all-gather.5.cloned.1.call-done), kind=kOutput, calls=%fused_computation.1 | convolution fusion | flops 1073741824 | bytes 6815744 | tf_op jit(solution)/shard_map/lrd,lcd->lrc/dot_general | solution.py:29
  167.3 1.0 copy-done.2
  168.3 3.0 %fusion.3 = f32[512,256]{1,0:T(8,128)S(1)} fusion(f32[512,256]{1,0:T(8,128)S(1)} %fusion, bf16[2,256,4096]{2,1,0:T(8,128)(2,1)} %all-gather.5.cloned.1.call-done, bf16[2,512,4096]{2,1,0:T(8,128)(2,1)S(1)} %copy-done.2), kind=kOutput, calls=%fused_computation.8 | convolution fusion | flops 1074003968 | bytes 7340032 | tf_op jit(solution)/shard_map/lrd,lcd->lrc/dot_general | solution.py:28
  171.3 14.9 %all_to_all.5 = f32[8,64,256]{2,1,0:T(8,128)S(1)} all-to-all(f32[8,64,256]{2,1,0:T(8,128)S(1)} %bitcast.21), channel_id=1, replica_groups=mesh['layer'=8,'trow'=2,'tcol'=32] {'layer'}, dimensions={0} | all-to-all | bytes 1048576 | tf_op jit(solution)/shard_map/all_to_all | solution.py:23
  186.2 0.7 reduce_sum.8
Async XLA Ops:
  6.5 3.2 %copy-start.1 = (bf16[1,16,4096]{2,1,0:T(8,128)(2,1)S(1)}, bf16[1,16,4096]{2,1,0:T(8,128)(2,1)}, u32[]{:S(2)}) copy-start(bf16[1,16,4096]{2,1,0:T(8,128)(2,1)} %param.4) | copy-start | bytes 393220
  6.5 3.2 %copy-start = (bf16[1,16,4096]{2,1,0:T(8,128)(2,1)S(1)}, bf16[1,16,4096]{2,1,0:T(8,128)(2,1)}, u32[]{:S(2)}) copy-start(bf16[1,16,4096]{2,1,0:T(8,128)(2,1)} %param.5) | copy-start | bytes 393220
  6.5 74.4 %all-gather.5.cloned.1.call-start = ((), (), s32[]{:S(2)}) async-start(), calls=%async_computation.2 | async-start | bytes 6291456 | tf_op jit(solution)/shard_map/all_gather | solution.py:13
  9.7 153.4 %all-gather.3.cloned.1.call-start = ((), (), s32[]{:S(2)}) async-start(), calls=%async_computation.1 | async-start | bytes 8650752 | tf_op jit(solution)/shard_map/all_gather | solution.py:13
  163.0 5.2 %copy-start.2 = (bf16[2,512,4096]{2,1,0:T(8,128)(2,1)S(1)}, bf16[2,512,4096]{2,1,0:T(8,128)(2,1)}, u32[]{:S(2)}) copy-start(bf16[2,512,4096]{2,1,0:T(8,128)(2,1)} %all-gather.3.cloned.1.call-done) | copy-start | bytes 25165828
Sparse Core Ops, SparseCore 0:
  9.8 71.0 all-gather.4
  83.0 79.9 all-gather.2
where the time goes:
time: 194 us
  waiting for transfers between devices  153 us (79%)
  blocking collectives  14.9 us (8%)
  between operations  13.4 us (7%)
  matrix products  7.32 us (4%)
  other arithmetic  4.52 us (2%)
    all_gather x2, waiting for transfers between devices, in_one_piece(): lax.all_gather(both, axis, axis=dim, tiled=True)  153 us
    all_to_all x1, blocking collectives, summed_on_arrival(): lax.all_to_all(in_blocks(value, dim, peers), axis, 0, 0, tiled=True)  14.9 us
    dot_general x1, matrix products, kernel_terms(): jnp.einsum('lrd,lcd->lrc', row_back, col_back, preferred_element_type=jnp...  4.29 us
  transfers between devices with their start and end apart: 2, of which 2 were waited for; matrix products, arithmetic and copies ran while one was open for 0% of the time, Pallas kernels for 0%

commit v1 on v0

v1 whole, which is shorter than its diff:
```python
import functools

import jax
import jax.numpy as jnp
from jax import lax
from jax.experimental import pallas as pl
from jax.experimental.pallas import tpu as pltpu
from jax.sharding import PartitionSpec as P


MIB = 1 << 20
ANY = pl.BlockSpec(memory_space=pl.ANY)


def stack_kernel(*refs):
    *parts, out, sem = refs
    height = parts[0].shape[0]
    for i, part in enumerate(parts):
        pltpu.make_async_copy(part, out.at[i * height : (i + 1) * height], sem).start()
    pltpu.make_async_copy(out, out, sem).wait()


def stack(parts):
    height, depth = parts[0].shape
    return pl.pallas_call(
        stack_kernel,
        out_shape=jax.ShapeDtypeStruct((len(parts) * height, depth), parts[0].dtype),
        in_specs=[ANY] * len(parts),
        out_specs=ANY,
        scratch_shapes=[pltpu.SemaphoreType.DMA],
        compiler_params=pltpu.CompilerParams(vmem_limit_bytes=MIB),
        cost_estimate=pl.CostEstimate(flops=200_000_000, bytes_accessed=0, transcendentals=0),
        name="stack",
    )(*parts)


def terms_kernel(half, groups, *refs):
    n_mine, n_next = half + 1, half
    mine, next_ = refs[:n_mine], refs[n_mine : n_mine + n_next]
    given = refs[n_mine + n_next : n_mine + n_next + len(groups)]
    own_act, other_act, own_back, other_back, out, act, back, cols_act, cols_back, sems = refs[n_mine + n_next + len(groups) :]
    tcol, trow = lax.axis_index("tcol"), lax.axis_index("trow")
    z, core = lax.shift_right_logical(tcol, 1), lax.rem(tcol, 2)
    planes = 2 * half
    height, depth = mine[0].shape[0] // 2, mine[0].shape[1]
    width = own_act.shape[0]
    sign = 1 - 2 * core

    def put(ref, first, plane, on):
        at = pl.multiple_of((lax.rem(plane + planes, planes) * 2 + on) * height, height)
        pltpu.make_async_copy(ref.at[first : first + height], act.at[pl.ds(at, height)], sems.at[0]).start()
        pltpu.make_async_copy(ref.at[first + height : first + 2 * height], back.at[pl.ds(at, height)], sems.at[1]).start()

    own_at = pl.multiple_of(trow * width, width)
    other_at = pl.multiple_of((1 - trow) * width, width)
    pltpu.make_async_copy(own_act, cols_act.at[pl.ds(own_at, width)], sems.at[2]).start()
    pltpu.make_async_copy(other_act, cols_act.at[pl.ds(other_at, width)], sems.at[2]).start()
    for step in range(n_mine):
        put(mine[step], 0, z - sign * step, core)
    for step in range(n_next):
        put(next_[step], 0, z - sign * step, 1 - core)
    for ref, group in zip(given, groups):
        for i, (stream, step) in enumerate(group):
            put(ref, 2 * height * i, z + sign * step, 1 - core if stream == 0 else core)
    pltpu.make_async_copy(own_back, cols_back.at[pl.ds(own_at, width)], sems.at[3]).start()
    pltpu.make_async_copy(other_back, cols_back.at[pl.ds(other_at, width)], sems.at[3]).start()

    dims = (((1,), (1,)), ((), ()))
    block = 128

    def at(i):
        return pl.ds(pl.multiple_of(i * block, block), block)

    pltpu.make_async_copy(cols_act, cols_act, sems.at[2]).wait()
    pltpu.make_async_copy(act, act, sems.at[0]).wait()

    def first(i, carry):
        out[at(i), :] = lax.dot_general(act[at(i), :], cols_act[...], dims, preferred_element_type=jnp.float32)
        return carry

    lax.fori_loop(0, act.shape[0] // block, first, 0)
    pltpu.make_async_copy(cols_back, cols_back, sems.at[3]).wait()
    pltpu.make_async_copy(back, back, sems.at[1]).wait()

    def second(i, carry):
        gram = lax.dot_general(back[at(i), :], cols_back[...], dims, preferred_element_type=jnp.float32)
        out[at(i), :] = out[at(i), :] * gram * (1.0 / depth)
        return carry

    lax.fori_loop(0, act.shape[0] // block, second, 0)


def terms_of(mine, next_, given, groups, cols):
    half = len(next_)
    height, depth = mine[0].shape
    rows, width = 2 * half * height, 2 * cols[0].shape[0]
    dtype = mine[0].dtype
    return pl.pallas_call(
        functools.partial(terms_kernel, half, groups),
        out_shape=jax.ShapeDtypeStruct((rows, width), jnp.float32),
        in_specs=[ANY] * (len(mine) + len(next_) + len(given) + len(cols)),
        out_specs=pl.BlockSpec(memory_space=pltpu.VMEM),
        scratch_shapes=[
            pltpu.VMEM((rows, depth), dtype),
            pltpu.VMEM((rows, depth), dtype),
            pltpu.VMEM((width, depth), dtype),
            pltpu.VMEM((width, depth), dtype),
            pltpu.SemaphoreType.DMA((4,)),
        ],
        compiler_params=pltpu.CompilerParams(vmem_limit_bytes=20 * MIB),
        cost_estimate=pl.CostEstimate(flops=4 * rows * width * depth, bytes_accessed=0, transcendentals=0),
        name="terms",
    )(*mine, *next_, *given, *cols)


def local(act_rows, back_rows, act_cols, back_cols):
    layers, tcols = lax.axis_size("layer"), lax.axis_size("tcol")
    planes = tcols // 2
    half = planes // 2
    cores = [(t, t ^ 1) for t in range(tcols)]
    along = [(2 * p + c, 2 * ((p + (1, -1)[c]) % planes) + c) for p in range(planes) for c in range(2)]

    mine = [jnp.concatenate((act_rows[0], back_rows[0]), axis=0)]
    next_ = [lax.ppermute(mine[0], "tcol", cores)]
    other_act = lax.ppermute(act_cols[0], "trow", [(0, 1), (1, 0)])
    other_back = lax.ppermute(back_cols[0], "trow", [(0, 1), (1, 0)])
    for step in range(1, half + 1):
        mine.append(lax.ppermute(mine[-1], "tcol", along))
        if step < half:
            next_.append(lax.ppermute(next_[-1], "tcol", along))

    order = [(stream, step) for step in range(1, half) for stream in range(2)] + [(0, half)]
    cut = len(order) // 5 * 2
    groups = (order[:cut], order[cut : 2 * cut], order[2 * cut :])
    given = []
    for group in groups:
        parts = [(mine, next_)[stream][step] for stream, step in group]
        given.append(lax.ppermute(stack(parts), "tcol", cores))

    cols = (act_cols[0], other_act, back_cols[0], other_back)
    terms = terms_of(mine, next_, given, groups, cols)
    got = lax.all_to_all(terms.reshape(layers, -1, terms.shape[-1]), "layer", 0, 0, tiled=True)
    return jnp.sum(got, axis=0)


def solution(mesh):
    in_specs = (
        P("layer", ("trow", "tcol"), None),
        P("layer", ("trow", "tcol"), None),
        P("layer", ("tcol", "trow"), None),
        P("layer", ("tcol", "trow"), None),
    )
    out_specs = P(("trow", "layer"), "tcol")
    return jax.shard_map(local, mesh=mesh, in_specs=in_specs, out_specs=out_specs, check_vma=False)
```

time: 194 us -> 165 us (0.85)
  waiting for transfers between devices: 153 us -> 81.9 us
  starting transfers between devices: 0.04 us -> 46.6 us
  Pallas kernels: 0 us -> 20.1 us
  between operations: 13.4 us -> 0.26 us
  matrix products: 7.32 us -> 0 us
  other arithmetic: 4.52 us -> 1.65 us
    all_gather x2 -> x0, waiting for transfers between devices: 153 us -> none  [in_one_piece(): lax.all_gather(both, axis, axis=dim, tiled=True)]
    ppermute x0 -> x21, waiting for transfers between devices: none -> 81.9 us  [the longest x8 36.6 us: local(): mine.append(lax.ppermute(mine[-1], 'tcol', along))]
    ppermute x0 -> x21, starting transfers between devices: none -> 46.6 us  [the longest x8 17.2 us: local(): mine.append(lax.ppermute(mine[-1], 'tcol', along))]
    pallas_call x0 -> x4, Pallas kernels: none -> 20.1 us  [the longest x1 19.8 us: terms_of(): pl.pallas_call(functools.partial(terms_kernel, half, groups), out_shape=j...]
    dot_general x2 -> x0, matrix products: 7.32 us -> none  [the longest x1 4.29 us: kernel_terms(): jnp.einsum('lrd,lcd->lrc', row_back, col_back, preferred_element_type=jnp...]
    concatenate x2 -> x1, other arithmetic: 3.85 us -> 0.99 us  [local(): mine = [jnp.concatenate((act_rows[0], back_rows[0]), axis=0)]]
  transfers between devices with their start and end apart: 2 -> 21, of which waited for: 2 -> 16; matrix products, arithmetic and copies ran while one was open for 0% -> 0% of each run, Pallas kernels for 0% -> 0%
where the time goes in v1:
time: 165 us; the launch traced here: 164 us
  waiting for transfers between devices  81.9 us (50%)
  starting transfers between devices  46.6 us (28%)
  Pallas kernels  20.1 us (12%)
  blocking collectives  13.6 us (8%)
    ppermute x8, waiting for transfers between devices, local(): mine.append(lax.ppermute(mine[-1], 'tcol', along))  36.6 us
    ppermute x1, waiting for transfers between devices, local(): other_back = lax.ppermute(back_cols[0], 'trow', [(0, 1), (1, 0)])  21.3 us
    pallas_call x1, Pallas kernels, terms_of(): pl.pallas_call(functools.partial(terms_kernel, half, groups), out_shape=j...  19.8 us
    ppermute x1, waiting for transfers between devices, local(): other_act = lax.ppermute(act_cols[0], 'trow', [(0, 1), (1, 0)])  18.7 us
    ppermute x8, starting transfers between devices, local(): mine.append(lax.ppermute(mine[-1], 'tcol', along))  17.2 us
    ppermute x7, starting transfers between devices, local(): next_.append(lax.ppermute(next_[-1], 'tcol', along))  15.3 us
    all_to_all x1, blocking collectives, local(): lax.all_to_all(terms.reshape(layers, -1, terms.shape[-1]), 'layer', 0, 0,...  13.6 us
    ppermute x3, starting transfers between devices, local(): given.append(lax.ppermute(stack(parts), 'tcol', cores))  5.93 us
  transfers between devices with their start and end apart: 21, of which 16 were waited for; matrix products, arithmetic and copies ran while one was open for 0% of the time, Pallas kernels for 0%

profile of v1, /device:TPU:24, one launch (start us, length us, event | category | flops | bytes accessed | tf_op | source)
XLA Modules:
  0.0 164.1 jit_solution(2096180408231965360)
XLA Ops:
  0.0 1.0 pad_maximum_fusion.refs_0_
  1.0 1.9 %collective-permute-start.8 = (bf16[32,4096]{1,0:T(8,128)(2,1)S(1)}, bf16[32,4096]{1,0:T(8,128)(2,1)S(1)}, u32[]{:S(2)}, u32[]{:S(2)}) collective-permute-start(bf16[32,4096]{1,0:T(8,128)(2,1)S(1)} %pad_maximum_fusion.refs_0_), channel_id=1, source_target_pairs={{0,1},{1,0},{2,3},{3,2},{4,5},{5,4},{6,7},{7,6},{8,9},{9,8},{10,11... | collective-permute-start | bytes 786440 | tf_op jit(solution)/shard_map/ppermute | solution.py:124
  2.9 3.8 %collective-permute-start = (bf16[32,4096]{1,0:T(8,128)(2,1)S(1)}, bf16[32,4096]{1,0:T(8,128)(2,1)S(1)}, u32[]{:S(2)}, u32[]{:S(2)}) collective-permute-start(bf16[32,4096]{1,0:T(8,128)(2,1)S(1)} %pad_maximum_fusion.refs_0_), channel_id=1, source_target_pairs={{0,2},{1,31},{2,4},{3,1},{4,6},{5,3},{6,8},{7,5},{8,10},{9,7},{10,... | collective-permute-start | bytes 786440 | tf_op jit(solution)/shard_map/ppermute | solution.py:128
  6.8 3.8 %collective-permute-start.9 = (bf16[32,4096]{1,0:T(8,128)(2,1)S(1)}, bf16[32,4096]{1,0:T(8,128)(2,1)S(1)}, u32[]{:S(2)}, u32[]{:S(2)}) collective-permute-start(bf16[32,4096]{1,0:T(8,128)(2,1)S(1)} %collective-permute-done.8.refs_9_), channel_id=1, source_target_pairs={{0,2},{1,31},{2,4},{3,1},{4,6},{5,3},{6,8},{7,5},{8,10},{9,7},{10,... | collective-permute-start | bytes 786440 | tf_op jit(solution)/shard_map/ppermute | solution.py:130
  10.6 8.1 %collective-permute-done.refs_0_.refs_1_ = bf16[32,4096]{1,0:T(8,128)(2,1)S(1)} collective-permute-done((bf16[32,4096]{1,0:T(8,128)(2,1)S(1)}, bf16[32,4096]{1,0:T(8,128)(2,1)S(1)}, u32[]{:S(2)}, u32[]{:S(2)}) %collective-permute-start) | collective-permute-done | bytes 262176 | tf_op jit(solution)/shard_map/ppermute | solution.py:128
  18.7 1.9 %collective-permute-start.1 = (bf16[32,4096]{1,0:T(8,128)(2,1)S(1)}, bf16[32,4096]{1,0:T(8,128)(2,1)S(1)}, u32[]{:S(2)}, u32[]{:S(2)}) collective-permute-start(bf16[32,4096]{1,0:T(8,128)(2,1)S(1)} %collective-permute-done.refs_0_.refs_1_), channel_id=1, source_target_pairs={{0,2},{1,31},{2,4},{3,1},{4,6},{5,3},{6,8},{7,5},{8,10},{9,7},{10,... | collective-permute-start | bytes 786440 | tf_op jit(solution)/shard_map/ppermute | solution.py:128
  20.6 0.9 collective-permute-done.9.refs_1_.refs_10_
  21.5 1.9 %collective-permute-start.10 = (bf16[32,4096]{1,0:T(8,128)(2,1)S(1)}, bf16[32,4096]{1,0:T(8,128)(2,1)S(1)}, u32[]{:S(2)}, u32[]{:S(2)}) collective-permute-start(bf16[32,4096]{1,0:T(8,128)(2,1)S(1)} %collective-permute-done.9.refs_1_.refs_10_), channel_id=1, source_target_pairs={{0,2},{1,31},{2,4},{3,1},{4,6},{5,3},{6,8},{7,5},{8,10},{9,7},{10,... | collective-permute-start | bytes 786440 | tf_op jit(solution)/shard_map/ppermute | solution.py:130
  23.4 4.7 %collective-permute-done.1.refs_2_ = bf16[32,4096]{1,0:T(8,128)(2,1)S(1)} collective-permute-done((bf16[32,4096]{1,0:T(8,128)(2,1)S(1)}, bf16[32,4096]{1,0:T(8,128)(2,1)S(1)}, u32[]{:S(2)}, u32[]{:S(2)}) %collective-permute-start.1) | collective-permute-done | bytes 262176 | tf_op jit(solution)/shard_map/ppermute | solution.py:128
  28.1 1.9 %collective-permute-start.2 = (bf16[32,4096]{1,0:T(8,128)(2,1)S(1)}, bf16[32,4096]{1,0:T(8,128)(2,1)S(1)}, u32[]{:S(2)}, u32[]{:S(2)}) collective-permute-start(bf16[32,4096]{1,0:T(8,128)(2,1)S(1)} %collective-permute-done.1.refs_2_), channel_id=1, source_target_pairs={{0,2},{1,31},{2,4},{3,1},{4,6},{5,3},{6,8},{7,5},{8,10},{9,7},{10,... | collective-permute-start | bytes 786440 | tf_op jit(solution)/shard_map/ppermute | solution.py:128
  30.0 0.9 collective-permute-done.10.refs_3_.refs_11_
  30.9 1.9 %collective-permute-start.11 = (bf16[32,4096]{1,0:T(8,128)(2,1)S(1)}, bf16[32,4096]{1,0:T(8,128)(2,1)S(1)}, u32[]{:S(2)}, u32[]{:S(2)}) collective-permute-start(bf16[32,4096]{1,0:T(8,128)(2,1)S(1)} %collective-permute-done.10.refs_3_.refs_11_), channel_id=1, source_target_pairs={{0,2},{1,31},{2,4},{3,1},{4,6},{5,3},{6,8},{7,5},{8,10},{9,7},{10,... | collective-permute-start | bytes 786440 | tf_op jit(solution)/shard_map/ppermute | solution.py:130
  32.9 4.7 %collective-permute-done.2.refs_4_.refs_3_ = bf16[32,4096]{1,0:T(8,128)(2,1)S(1)} collective-permute-done((bf16[32,4096]{1,0:T(8,128)(2,1)S(1)}, bf16[32,4096]{1,0:T(8,128)(2,1)S(1)}, u32[]{:S(2)}, u32[]{:S(2)}) %collective-permute-start.2) | collective-permute-done | bytes 262176 | tf_op jit(solution)/shard_map/ppermute | solution.py:128
  37.6 1.9 %collective-permute-start.3 = (bf16[32,4096]{1,0:T(8,128)(2,1)S(1)}, bf16[32,4096]{1,0:T(8,128)(2,1)S(1)}, u32[]{:S(2)}, u32[]{:S(2)}) collective-permute-start(bf16[32,4096]{1,0:T(8,128)(2,1)S(1)} %collective-permute-done.2.refs_4_.refs_3_), channel_id=1, source_target_pairs={{0,2},{1,31},{2,4},{3,1},{4,6},{5,3},{6,8},{7,5},{8,10},{9,7},{10,... | collective-permute-start | bytes 786440 | tf_op jit(solution)/shard_map/ppermute | solution.py:128
  39.5 0.9 collective-permute-done.11.refs_5_.refs_12_
  40.4 1.9 %collective-permute-start.12 = (bf16[32,4096]{1,0:T(8,128)(2,1)S(1)}, bf16[32,4096]{1,0:T(8,128)(2,1)S(1)}, u32[]{:S(2)}, u32[]{:S(2)}) collective-permute-start(bf16[32,4096]{1,0:T(8,128)(2,1)S(1)} %collective-permute-done.11.refs_5_.refs_12_), channel_id=1, source_target_pairs={{0,2},{1,31},{2,4},{3,1},{4,6},{5,3},{6,8},{7,5},{8,10},{9,7},{10,... | collective-permute-start | bytes 786440 | tf_op jit(solution)/shard_map/ppermute | solution.py:130
  42.3 4.7 %collective-permute-done.3.refs_0_.refs_4_ = bf16[32,4096]{1,0:T(8,128)(2,1)S(1)} collective-permute-done((bf16[32,4096]{1,0:T(8,128)(2,1)S(1)}, bf16[32,4096]{1,0:T(8,128)(2,1)S(1)}, u32[]{:S(2)}, u32[]{:S(2)}) %collective-permute-start.3) | collective-permute-done | bytes 262176 | tf_op jit(solution)/shard_map/ppermute | solution.py:128
  47.1 1.9 %collective-permute-start.4 = (bf16[32,4096]{1,0:T(8,128)(2,1)S(1)}, bf16[32,4096]{1,0:T(8,128)(2,1)S(1)}, u32[]{:S(2)}, u32[]{:S(2)}) collective-permute-start(bf16[32,4096]{1,0:T(8,128)(2,1)S(1)} %collective-permute-done.3.refs_0_.refs_4_), channel_id=1, source_target_pairs={{0,2},{1,31},{2,4},{3,1},{4,6},{5,3},{6,8},{7,5},{8,10},{9,7},{10,... | collective-permute-start | bytes 786440 | tf_op jit(solution)/shard_map/ppermute | solution.py:128
  49.0 0.9 collective-permute-done.12.refs_1_.refs_13_
  49.9 1.9 %collective-permute-start.13 = (bf16[32,4096]{1,0:T(8,128)(2,1)S(1)}, bf16[32,4096]{1,0:T(8,128)(2,1)S(1)}, u32[]{:S(2)}, u32[]{:S(2)}) collective-permute-start(bf16[32,4096]{1,0:T(8,128)(2,1)S(1)} %collective-permute-done.12.refs_1_.refs_13_), channel_id=1, source_target_pairs={{0,2},{1,31},{2,4},{3,1},{4,6},{5,3},{6,8},{7,5},{8,10},{9,7},{10,... | collective-permute-start | bytes 786440 | tf_op jit(solution)/shard_map/ppermute | solution.py:130
  51.8 4.7 %collective-permute-done.4.refs_2_.refs_5_ = bf16[32,4096]{1,0:T(8,128)(2,1)S(1)} collective-permute-done((bf16[32,4096]{1,0:T(8,128)(2,1)S(1)}, bf16[32,4096]{1,0:T(8,128)(2,1)S(1)}, u32[]{:S(2)}, u32[]{:S(2)}) %collective-permute-start.4) | collective-permute-done | bytes 262176 | tf_op jit(solution)/shard_map/ppermute | solution.py:128
  56.5 1.9 %collective-permute-start.5 = (bf16[32,4096]{1,0:T(8,128)(2,1)S(1)}, bf16[32,4096]{1,0:T(8,128)(2,1)S(1)}, u32[]{:S(2)}, u32[]{:S(2)}) collective-permute-start(bf16[32,4096]{1,0:T(8,128)(2,1)S(1)} %collective-permute-done.4.refs_2_.refs_5_), channel_id=1, source_target_pairs={{0,2},{1,31},{2,4},{3,1},{4,6},{5,3},{6,8},{7,5},{8,10},{9,7},{10,... | collective-permute-start | bytes 786440 | tf_op jit(solution)/shard_map/ppermute | solution.py:128
  58.4 0.9 collective-permute-done.13.refs_3_.refs_14_
  59.3 1.9 %collective-permute-start.14 = (bf16[32,4096]{1,0:T(8,128)(2,1)S(1)}, bf16[32,4096]{1,0:T(8,128)(2,1)S(1)}, u32[]{:S(2)}, u32[]{:S(2)}) collective-permute-start(bf16[32,4096]{1,0:T(8,128)(2,1)S(1)} %collective-permute-done.13.refs_3_.refs_14_), channel_id=1, source_target_pairs={{0,2},{1,31},{2,4},{3,1},{4,6},{5,3},{6,8},{7,5},{8,10},{9,7},{10,... | collective-permute-start | bytes 786440 | tf_op jit(solution)/shard_map/ppermute | solution.py:130
  61.3 0.1 stack.3
  61.4 0.0 copy-start
  61.4 0.0 copy-start.1
  61.4 2.1 %collective-permute-start.16 = (bf16[192,4096]{1,0:T(8,128)(2,1)S(1)}, bf16[192,4096]{1,0:T(8,128)(2,1)S(1)}, u32[]{:S(2)}, u32[]{:S(2)}) collective-permute-start(bf16[192,4096]{1,0:T(8,128)(2,1)S(1)} %stack.3), channel_id=1, source_target_pairs={{0,1},{1,0},{2,3},{3,2},{4,5},{5,4},{6,7},{7,6},{8,9},{9,8},{10,11... | collective-permute-start | bytes 4718600 | tf_op jit(solution)/shard_map/ppermute | solution.py:138
  63.5 2.5 %collective-permute-done.5.refs_4_.refs_6_ = bf16[32,4096]{1,0:T(8,128)(2,1)S(1)} collective-permute-done((bf16[32,4096]{1,0:T(8,128)(2,1)S(1)}, bf16[32,4096]{1,0:T(8,128)(2,1)S(1)}, u32[]{:S(2)}, u32[]{:S(2)}) %collective-permute-start.5) | collective-permute-done | bytes 262176 | tf_op jit(solution)/shard_map/ppermute | solution.py:128
  66.0 1.9 %collective-permute-start.6 = (bf16[32,4096]{1,0:T(8,128)(2,1)S(1)}, bf16[32,4096]{1,0:T(8,128)(2,1)S(1)}, u32[]{:S(2)}, u32[]{:S(2)}) collective-permute-start(bf16[32,4096]{1,0:T(8,128)(2,1)S(1)} %collective-permute-done.5.refs_4_.refs_6_), channel_id=1, source_target_pairs={{0,2},{1,31},{2,4},{3,1},{4,6},{5,3},{6,8},{7,5},{8,10},{9,7},{10,... | collective-permute-start | bytes 786440 | tf_op jit(solution)/shard_map/ppermute | solution.py:128
  67.9 0.9 collective-permute-done.14.refs_5_.refs_15_
  68.8 0.1 stack.4
  68.9 2.0 %collective-permute-start.17 = (bf16[192,4096]{1,0:T(8,128)(2,1)S(1)}, bf16[192,4096]{1,0:T(8,128)(2,1)S(1)}, u32[]{:S(2)}, u32[]{:S(2)}) collective-permute-start(bf16[192,4096]{1,0:T(8,128)(2,1)S(1)} %stack.4), channel_id=1, source_target_pairs={{0,1},{1,0},{2,3},{3,2},{4,5},{5,4},{6,7},{7,6},{8,9},{9,8},{10,11... | collective-permute-start | bytes 4718600 | tf_op jit(solution)/shard_map/ppermute | solution.py:138
  70.9 4.6 %collective-permute-done.6.refs_0_.refs_7_ = bf16[32,4096]{1,0:T(8,128)(2,1)S(1)} collective-permute-done((bf16[32,4096]{1,0:T(8,128)(2,1)S(1)}, bf16[32,4096]{1,0:T(8,128)(2,1)S(1)}, u32[]{:S(2)}, u32[]{:S(2)}) %collective-permute-start.6) | collective-permute-done | bytes 262176 | tf_op jit(solution)/shard_map/ppermute | solution.py:128
  75.5 1.9 %collective-permute-start.7 = (bf16[32,4096]{1,0:T(8,128)(2,1)S(1)}, bf16[32,4096]{1,0:T(8,128)(2,1)S(1)}, u32[]{:S(2)}, u32[]{:S(2)}) collective-permute-start(bf16[32,4096]{1,0:T(8,128)(2,1)S(1)} %collective-permute-done.6.refs_0_.refs_7_), channel_id=1, source_target_pairs={{0,2},{1,31},{2,4},{3,1},{4,6},{5,3},{6,8},{7,5},{8,10},{9,7},{10,... | collective-permute-start | bytes 786440 | tf_op jit(solution)/shard_map/ppermute | solution.py:128
  77.4 1.9 %collective-permute-start.15 = (bf16[32,4096]{1,0:T(8,128)(2,1)S(1)}, bf16[32,4096]{1,0:T(8,128)(2,1)S(1)}, u32[]{:S(2)}, u32[]{:S(2)}) collective-permute-start(bf16[32,4096]{1,0:T(8,128)(2,1)S(1)} %collective-permute-done.14.refs_5_.refs_15_), channel_id=1, source_target_pairs={{0,2},{1,31},{2,4},{3,1},{4,6},{5,3},{6,8},{7,5},{8,10},{9,7},{10,... | collective-permute-start | bytes 786440 | tf_op jit(solution)/shard_map/ppermute | solution.py:130
  79.3 3.1 %collective-permute-start.19 = (bf16[128,4096]{1,0:T(8,128)(2,1)S(1)}, bf16[128,4096]{1,0:T(8,128)(2,1)S(1)}, u32[]{:S(2)}, u32[]{:S(2)}) collective-permute-start(bf16[128,4096]{1,0:T(8,128)(2,1)S(1)} %bitcast.6), channel_id=1, source_target_pairs={{0,32},{32,0},{1,33},{33,1},{2,34},{34,2},{3,35},{35,3},{4,36},{36... | collective-permute-start | bytes 3145736 | tf_op jit(solution)/shard_map/ppermute | solution.py:125
  82.5 2.5 %collective-permute-done.7.refs_2_.refs_8_ = bf16[32,4096]{1,0:T(8,128)(2,1)S(1)} collective-permute-done((bf16[32,4096]{1,0:T(8,128)(2,1)S(1)}, bf16[32,4096]{1,0:T(8,128)(2,1)S(1)}, u32[]{:S(2)}, u32[]{:S(2)}) %collective-permute-start.7) | collective-permute-done | bytes 262176 | tf_op jit(solution)/shard_map/ppermute | solution.py:128
  84.9 3.1 %collective-permute-start.20 = (bf16[128,4096]{1,0:T(8,128)(2,1)S(1)}, bf16[128,4096]{1,0:T(8,128)(2,1)S(1)}, u32[]{:S(2)}, u32[]{:S(2)}) collective-permute-start(bf16[128,4096]{1,0:T(8,128)(2,1)S(1)} %bitcast.8), channel_id=1, source_target_pairs={{0,32},{32,0},{1,33},{33,1},{2,34},{34,2},{3,35},{35,3},{4,36},{36... | collective-permute-start | bytes 3145736 | tf_op jit(solution)/shard_map/ppermute | solution.py:126
  88.1 0.0 collective-permute-done.15.refs_1_.refs_16_
  88.1 0.1 stack.5
  88.2 1.9 %collective-permute-start.18 = (bf16[96,4096]{1,0:T(8,128)(2,1)S(1)}, bf16[96,4096]{1,0:T(8,128)(2,1)S(1)}, u32[]{:S(2)}, u32[]{:S(2)}) collective-permute-start(bf16[96,4096]{1,0:T(8,128)(2,1)S(1)} %stack.5), channel_id=1, source_target_pairs={{0,1},{1,0},{2,3},{3,2},{4,5},{5,4},{6,7},{7,6},{8,9},{9,8},{10,11... | collective-permute-start | bytes 2359304 | tf_op jit(solution)/shard_map/ppermute | solution.py:138
  90.1 18.7 %collective-permute-done.19.refs_21_ = bf16[128,4096]{1,0:T(8,128)(2,1)S(1)} collective-permute-done((bf16[128,4096]{1,0:T(8,128)(2,1)S(1)}, bf16[128,4096]{1,0:T(8,128)(2,1)S(1)}, u32[]{:S(2)}, u32[]{:S(2)}) %collective-permute-start.19) | collective-permute-done | bytes 1048608 | tf_op jit(solution)/shard_map/ppermute | solution.py:125
  108.7 21.3 %collective-permute-done.20.refs_23_ = bf16[128,4096]{1,0:T(8,128)(2,1)S(1)} collective-permute-done((bf16[128,4096]{1,0:T(8,128)(2,1)S(1)}, bf16[128,4096]{1,0:T(8,128)(2,1)S(1)}, u32[]{:S(2)}, u32[]{:S(2)}) %collective-permute-start.20) | collective-permute-done | bytes 1048608 | tf_op jit(solution)/shard_map/ppermute | solution.py:126
  130.0 0.0 collective-permute-done.16.refs_17_
  130.0 19.8 %terms.1 = f32[512,256]{1,0:T(8,128)S(1)} custom-call(bf16[32,4096]{1,0:T(8,128)(2,1)S(1)} %pad_maximum_fusion.refs_0_, bf16[32,4096]{1,0:T(8,128)(2,1)S(1)} %collective-permute-done.refs_0_.refs_1_, bf16[32,4096]{1,0:T(8,128)(2,1)S(1)} %collective-permute-done.1.refs_2_, bf16[32,4096]{1,0:T(8,128)(2,1)S(1)} %collective-permute-done.2.refs_4_.refs_3_, ...), custom_call_target="tpu_custom_call" | custom-call | flops 2147483648 | tf_op jit(solution)/shard_map/terms/pallas_call | solution.py:98
  149.9 13.6 %all_to_all.5 = f32[8,64,256]{2,1,0:T(8,128)S(1)} all-to-all(f32[8,64,256]{2,1,0:T(8,128)S(1)} %bitcast.5), channel_id=1, replica_groups=mesh['layer'=8,'trow'=2,'tcol'=32] {'layer'}, dimensions={0} | all-to-all | bytes 1048576 | tf_op jit(solution)/shard_map/all_to_all | solution.py:142
  163.4 0.7 reduce_sum.9
  (5 shorter events, 0.0 us)
Async XLA Ops:
  1.0 5.8 %collective-permute-start.8 = (bf16[32,4096]{1,0:T(8,128)(2,1)S(1)}, bf16[32,4096]{1,0:T(8,128)(2,1)S(1)}, u32[]{:S(2)}, u32[]{:S(2)}) collective-permute-start(bf16[32,4096]{1,0:T(8,128)(2,1)S(1)} %pad_maximum_fusion.refs_0_), channel_id=1, source_target_pairs={{0,1},{1,0},{2,3},{3,2},{4,5},{5,4},{6,7},{7,6},{8,9},{9,8},{10,11... | collective-permute-start | bytes 786440 | tf_op jit(solution)/shard_map/ppermute | solution.py:124
  2.9 15.7 %collective-permute-start = (bf16[32,4096]{1,0:T(8,128)(2,1)S(1)}, bf16[32,4096]{1,0:T(8,128)(2,1)S(1)}, u32[]{:S(2)}, u32[]{:S(2)}) collective-permute-start(bf16[32,4096]{1,0:T(8,128)(2,1)S(1)} %pad_maximum_fusion.refs_0_), channel_id=1, source_target_pairs={{0,2},{1,31},{2,4},{3,1},{4,6},{5,3},{6,8},{7,5},{8,10},{9,7},{10,... | collective-permute-start | bytes 786440 | tf_op jit(solution)/shard_map/ppermute | solution.py:128
  6.8 14.7 %collective-permute-start.9 = (bf16[32,4096]{1,0:T(8,128)(2,1)S(1)}, bf16[32,4096]{1,0:T(8,128)(2,1)S(1)}, u32[]{:S(2)}, u32[]{:S(2)}) collective-permute-start(bf16[32,4096]{1,0:T(8,128)(2,1)S(1)} %collective-permute-done.8.refs_9_), channel_id=1, source_target_pairs={{0,2},{1,31},{2,4},{3,1},{4,6},{5,3},{6,8},{7,5},{8,10},{9,7},{10,... | collective-permute-start | bytes 786440 | tf_op jit(solution)/shard_map/ppermute | solution.py:130
  18.7 9.5 %collective-permute-start.1 = (bf16[32,4096]{1,0:T(8,128)(2,1)S(1)}, bf16[32,4096]{1,0:T(8,128)(2,1)S(1)}, u32[]{:S(2)}, u32[]{:S(2)}) collective-permute-start(bf16[32,4096]{1,0:T(8,128)(2,1)S(1)} %collective-permute-done.refs_0_.refs_1_), channel_id=1, source_target_pairs={{0,2},{1,31},{2,4},{3,1},{4,6},{5,3},{6,8},{7,5},{8,10},{9,7},{10,... | collective-permute-start | bytes 786440 | tf_op jit(solution)/shard_map/ppermute | solution.py:128
  21.5 9.5 %collective-permute-start.10 = (bf16[32,4096]{1,0:T(8,128)(2,1)S(1)}, bf16[32,4096]{1,0:T(8,128)(2,1)S(1)}, u32[]{:S(2)}, u32[]{:S(2)}) collective-permute-start(bf16[32,4096]{1,0:T(8,128)(2,1)S(1)} %collective-permute-done.9.refs_1_.refs_10_), channel_id=1, source_target_pairs={{0,2},{1,31},{2,4},{3,1},{4,6},{5,3},{6,8},{7,5},{8,10},{9,7},{10,... | collective-permute-start | bytes 786440 | tf_op jit(solution)/shard_map/ppermute | solution.py:130
  28.1 9.5 %collective-permute-start.2 = (bf16[32,4096]{1,0:T(8,128)(2,1)S(1)}, bf16[32,4096]{1,0:T(8,128)(2,1)S(1)}, u32[]{:S(2)}, u32[]{:S(2)}) collective-permute-start(bf16[32,4096]{1,0:T(8,128)(2,1)S(1)} %collective-permute-done.1.refs_2_), channel_id=1, source_target_pairs={{0,2},{1,31},{2,4},{3,1},{4,6},{5,3},{6,8},{7,5},{8,10},{9,7},{10,... | collective-permute-start | bytes 786440 | tf_op jit(solution)/shard_map/ppermute | solution.py:128
  30.9 9.5 %collective-permute-start.11 = (bf16[32,4096]{1,0:T(8,128)(2,1)S(1)}, bf16[32,4096]{1,0:T(8,128)(2,1)S(1)}, u32[]{:S(2)}, u32[]{:S(2)}) collective-permute-start(bf16[32,4096]{1,0:T(8,128)(2,1)S(1)} %collective-permute-done.10.refs_3_.refs_11_), channel_id=1, source_target_pairs={{0,2},{1,31},{2,4},{3,1},{4,6},{5,3},{6,8},{7,5},{8,10},{9,7},{10,... | collective-permute-start | bytes 786440 | tf_op jit(solution)/shard_map/ppermute | solution.py:130
  37.6 9.5 %collective-permute-start.3 = (bf16[32,4096]{1,0:T(8,128)(2,1)S(1)}, bf16[32,4096]{1,0:T(8,128)(2,1)S(1)}, u32[]{:S(2)}, u32[]{:S(2)}) collective-permute-start(bf16[32,4096]{1,0:T(8,128)(2,1)S(1)} %collective-permute-done.2.refs_4_.refs_3_), channel_id=1, source_target_pairs={{0,2},{1,31},{2,4},{3,1},{4,6},{5,3},{6,8},{7,5},{8,10},{9,7},{10,... | collective-permute-start | bytes 786440 | tf_op jit(solution)/shard_map/ppermute | solution.py:128
  40.4 9.5 %collective-permute-start.12 = (bf16[32,4096]{1,0:T(8,128)(2,1)S(1)}, bf16[32,4096]{1,0:T(8,128)(2,1)S(1)}, u32[]{:S(2)}, u32[]{:S(2)}) collective-permute-start(bf16[32,4096]{1,0:T(8,128)(2,1)S(1)} %collective-permute-done.11.refs_5_.refs_12_), channel_id=1, source_target_pairs={{0,2},{1,31},{2,4},{3,1},{4,6},{5,3},{6,8},{7,5},{8,10},{9,7},{10,... | collective-permute-start | bytes 786440 | tf_op jit(solution)/shard_map/ppermute | solution.py:130
  47.1 9.5 %collective-permute-start.4 = (bf16[32,4096]{1,0:T(8,128)(2,1)S(1)}, bf16[32,4096]{1,0:T(8,128)(2,1)S(1)}, u32[]{:S(2)}, u32[]{:S(2)}) collective-permute-start(bf16[32,4096]{1,0:T(8,128)(2,1)S(1)} %collective-permute-done.3.refs_0_.refs_4_), channel_id=1, source_target_pairs={{0,2},{1,31},{2,4},{3,1},{4,6},{5,3},{6,8},{7,5},{8,10},{9,7},{10,... | collective-permute-start | bytes 786440 | tf_op jit(solution)/shard_map/ppermute | solution.py:128
  49.9 9.5 %collective-permute-start.13 = (bf16[32,4096]{1,0:T(8,128)(2,1)S(1)}, bf16[32,4096]{1,0:T(8,128)(2,1)S(1)}, u32[]{:S(2)}, u32[]{:S(2)}) collective-permute-start(bf16[32,4096]{1,0:T(8,128)(2,1)S(1)} %collective-permute-done.12.refs_1_.refs_13_), channel_id=1, source_target_pairs={{0,2},{1,31},{2,4},{3,1},{4,6},{5,3},{6,8},{7,5},{8,10},{9,7},{10,... | collective-permute-start | bytes 786440 | tf_op jit(solution)/shard_map/ppermute | solution.py:130
  56.5 9.5 %collective-permute-start.5 = (bf16[32,4096]{1,0:T(8,128)(2,1)S(1)}, bf16[32,4096]{1,0:T(8,128)(2,1)S(1)}, u32[]{:S(2)}, u32[]{:S(2)}) collective-permute-start(bf16[32,4096]{1,0:T(8,128)(2,1)S(1)} %collective-permute-done.4.refs_2_.refs_5_), channel_id=1, source_target_pairs={{0,2},{1,31},{2,4},{3,1},{4,6},{5,3},{6,8},{7,5},{8,10},{9,7},{10,... | collective-permute-start | bytes 786440 | tf_op jit(solution)/shard_map/ppermute | solution.py:128
  59.3 9.5 %collective-permute-start.14 = (bf16[32,4096]{1,0:T(8,128)(2,1)S(1)}, bf16[32,4096]{1,0:T(8,128)(2,1)S(1)}, u32[]{:S(2)}, u32[]{:S(2)}) collective-permute-start(bf16[32,4096]{1,0:T(8,128)(2,1)S(1)} %collective-permute-done.13.refs_3_.refs_14_), channel_id=1, source_target_pairs={{0,2},{1,31},{2,4},{3,1},{4,6},{5,3},{6,8},{7,5},{8,10},{9,7},{10,... | collective-permute-start | bytes 786440 | tf_op jit(solution)/shard_map/ppermute | solution.py:130
  61.4 17.9 %copy-start = (bf16[1,128,4096]{2,1,0:T(8,128)(2,1)S(1)}, bf16[1,128,4096]{2,1,0:T(8,128)(2,1)}, u32[]{:S(2)}) copy-start(bf16[1,128,4096]{2,1,0:T(8,128)(2,1)} %param.6) | copy-start | bytes 3145732
  61.4 23.5 %copy-start.1 = (bf16[1,128,4096]{2,1,0:T(8,128)(2,1)S(1)}, bf16[1,128,4096]{2,1,0:T(8,128)(2,1)}, u32[]{:S(2)}) copy-start(bf16[1,128,4096]{2,1,0:T(8,128)(2,1)} %param.7) | copy-start | bytes 3145732
  61.4 68.6 %collective-permute-start.16 = (bf16[192,4096]{1,0:T(8,128)(2,1)S(1)}, bf16[192,4096]{1,0:T(8,128)(2,1)S(1)}, u32[]{:S(2)}, u32[]{:S(2)}) collective-permute-start(bf16[192,4096]{1,0:T(8,128)(2,1)S(1)} %stack.3), channel_id=1, source_target_pairs={{0,1},{1,0},{2,3},{3,2},{4,5},{5,4},{6,7},{7,6},{8,9},{9,8},{10,11... | collective-permute-start | bytes 4718600 | tf_op jit(solution)/shard_map/ppermute | solution.py:138
  66.0 9.5 %collective-permute-start.6 = (bf16[32,4096]{1,0:T(8,128)(2,1)S(1)}, bf16[32,4096]{1,0:T(8,128)(2,1)S(1)}, u32[]{:S(2)}, u32[]{:S(2)}) collective-permute-start(bf16[32,4096]{1,0:T(8,128)(2,1)S(1)} %collective-permute-done.5.refs_4_.refs_6_), channel_id=1, source_target_pairs={{0,2},{1,31},{2,4},{3,1},{4,6},{5,3},{6,8},{7,5},{8,10},{9,7},{10,... | collective-permute-start | bytes 786440 | tf_op jit(solution)/shard_map/ppermute | solution.py:128
  68.9 61.1 %collective-permute-start.17 = (bf16[192,4096]{1,0:T(8,128)(2,1)S(1)}, bf16[192,4096]{1,0:T(8,128)(2,1)S(1)}, u32[]{:S(2)}, u32[]{:S(2)}) collective-permute-start(bf16[192,4096]{1,0:T(8,128)(2,1)S(1)} %stack.4), channel_id=1, source_target_pairs={{0,1},{1,0},{2,3},{3,2},{4,5},{5,4},{6,7},{7,6},{8,9},{9,8},{10,11... | collective-permute-start | bytes 4718600 | tf_op jit(solution)/shard_map/ppermute | solution.py:138
  75.5 9.5 %collective-permute-start.7 = (bf16[32,4096]{1,0:T(8,128)(2,1)S(1)}, bf16[32,4096]{1,0:T(8,128)(2,1)S(1)}, u32[]{:S(2)}, u32[]{:S(2)}) collective-permute-start(bf16[32,4096]{1,0:T(8,128)(2,1)S(1)} %collective-permute-done.6.refs_0_.refs_7_), channel_id=1, source_target_pairs={{0,2},{1,31},{2,4},{3,1},{4,6},{5,3},{6,8},{7,5},{8,10},{9,7},{10,... | collective-permute-start | bytes 786440 | tf_op jit(solution)/shard_map/ppermute | solution.py:128
  77.4 10.7 %collective-permute-start.15 = (bf16[32,4096]{1,0:T(8,128)(2,1)S(1)}, bf16[32,4096]{1,0:T(8,128)(2,1)S(1)}, u32[]{:S(2)}, u32[]{:S(2)}) collective-permute-start(bf16[32,4096]{1,0:T(8,128)(2,1)S(1)} %collective-permute-done.14.refs_5_.refs_15_), channel_id=1, source_target_pairs={{0,2},{1,31},{2,4},{3,1},{4,6},{5,3},{6,8},{7,5},{8,10},{9,7},{10,... | collective-permute-start | bytes 786440 | tf_op jit(solution)/shard_map/ppermute | solution.py:130
  79.3 29.4 %collective-permute-start.19 = (bf16[128,4096]{1,0:T(8,128)(2,1)S(1)}, bf16[128,4096]{1,0:T(8,128)(2,1)S(1)}, u32[]{:S(2)}, u32[]{:S(2)}) collective-permute-start(bf16[128,4096]{1,0:T(8,128)(2,1)S(1)} %bitcast.6), channel_id=1, source_target_pairs={{0,32},{32,0},{1,33},{33,1},{2,34},{34,2},{3,35},{35,3},{4,36},{36... | collective-permute-start | bytes 3145736 | tf_op jit(solution)/shard_map/ppermute | solution.py:125
  84.9 45.1 %collective-permute-start.20 = (bf16[128,4096]{1,0:T(8,128)(2,1)S(1)}, bf16[128,4096]{1,0:T(8,128)(2,1)S(1)}, u32[]{:S(2)}, u32[]{:S(2)}) collective-permute-start(bf16[128,4096]{1,0:T(8,128)(2,1)S(1)} %bitcast.8), channel_id=1, source_target_pairs={{0,32},{32,0},{1,33},{33,1},{2,34},{34,2},{3,35},{35,3},{4,36},{36... | collective-permute-start | bytes 3145736 | tf_op jit(solution)/shard_map/ppermute | solution.py:126
  88.2 41.9 %collective-permute-start.18 = (bf16[96,4096]{1,0:T(8,128)(2,1)S(1)}, bf16[96,4096]{1,0:T(8,128)(2,1)S(1)}, u32[]{:S(2)}, u32[]{:S(2)}) collective-permute-start(bf16[96,4096]{1,0:T(8,128)(2,1)S(1)} %stack.5), channel_id=1, source_target_pairs={{0,1},{1,0},{2,3},{3,2},{4,5},{5,4},{6,7},{7,6},{8,9},{9,8},{10,11... | collective-permute-start | bytes 2359304 | tf_op jit(solution)/shard_map/ppermute | solution.py:138

commit v2 on v0

v2 whole, which is shorter than its diff:
```python
import functools

import jax
import jax.numpy as jnp
from jax import lax
from jax.experimental import pallas as pl
from jax.experimental.pallas import tpu as pltpu
from jax.sharding import PartitionSpec as P


MIB = 1 << 20
ANY = pl.BlockSpec(memory_space=pl.ANY)
VMEM = pl.BlockSpec(memory_space=pltpu.VMEM)
LEAD = 3

GROUPS = (
    ((0, 0), (0, 1), (1, 1), (0, 2), (1, 2), (0, 3), (1, 3)),
    ((0, 4), (1, 4), (0, 5), (1, 5), (0, 6), (1, 6)),
    ((0, 7), (1, 7), (0, 8)),
)


def stack_kernel(*refs):
    *parts, out, sem = refs
    height = parts[0].shape[0]
    for i, part in enumerate(parts):
        pltpu.make_async_copy(part, out.at[i * height : (i + 1) * height], sem).start()
    pltpu.make_async_copy(out, out, sem).wait()


def stack(parts):
    height, depth = parts[0].shape
    return pl.pallas_call(
        stack_kernel,
        out_shape=jax.ShapeDtypeStruct((len(parts) * height, depth), parts[0].dtype),
        in_specs=[ANY] * len(parts),
        out_specs=ANY,
        scratch_shapes=[pltpu.SemaphoreType.DMA],
        compiler_params=pltpu.CompilerParams(vmem_limit_bytes=MIB),
        cost_estimate=pl.CostEstimate(flops=200_000_000, bytes_accessed=0, transcendentals=0),
        name="stack",
    )(*parts)


def order_kernel(half, *refs):
    n_mine, n_next = half + 1, half - 1
    mine, next_ = refs[:n_mine], refs[n_mine : n_mine + n_next]
    given = refs[n_mine + n_next : n_mine + n_next + len(GROUPS)]
    act, back, sems = refs[n_mine + n_next + len(GROUPS) :]
    tcol = lax.axis_index("tcol")
    z, core = lax.shift_right_logical(tcol, 1), lax.rem(tcol, 2)
    planes = 2 * half
    height = mine[0].shape[0] // 2
    sign = 1 - 2 * core

    def put(ref, first, plane, on):
        at = pl.multiple_of((lax.rem(plane + planes, planes) * 2 + on) * height, height)
        pltpu.make_async_copy(ref.at[first : first + height], act.at[pl.ds(at, height)], sems.at[0]).start()
        pltpu.make_async_copy(ref.at[first + height : first + 2 * height], back.at[pl.ds(at, height)], sems.at[1]).start()

    for step in range(n_mine):
        put(mine[step], 0, z - sign * step, core)
    for step in range(1, half):
        put(next_[step - 1], 0, z - sign * step, 1 - core)
    for ref, group in zip(given, GROUPS):
        for i, (stream, step) in enumerate(group):
            put(ref, 2 * height * i, z + sign * step, 1 - core if stream == 0 else core)
    pltpu.make_async_copy(act, act, sems.at[0]).wait()
    pltpu.make_async_copy(back, back, sems.at[1]).wait()


def in_order(mine, next_, given):
    half = len(mine) - 1
    height, depth = mine[0].shape
    rows = jax.ShapeDtypeStruct((2 * half * height, depth), mine[0].dtype)
    return pl.pallas_call(
        functools.partial(order_kernel, half),
        out_shape=(rows, rows),
        in_specs=[ANY] * (len(mine) + len(next_) + len(given)),
        out_specs=(ANY, ANY),
        scratch_shapes=[pltpu.SemaphoreType.DMA((2,))],
        compiler_params=pltpu.CompilerParams(vmem_limit_bytes=MIB),
        cost_estimate=pl.CostEstimate(flops=1_000_000_000, bytes_accessed=0, transcendentals=0),
        name="order",
    )(*mine, *next_, *given)


def sum_kernel(got, out):
    trow = lax.axis_index("trow")
    width = out.shape[1] // 2
    for half, at in ((0, trow), (1, 1 - trow)):
        to = pl.ds(pl.multiple_of(at * width, width), width)
        out[:, to] = jnp.sum(got[:, :, half * width : (half + 1) * width], axis=0)


def layer_sum(got):
    return pl.pallas_call(
        sum_kernel,
        out_shape=jax.ShapeDtypeStruct(got.shape[1:], got.dtype),
        in_specs=[VMEM],
        out_specs=VMEM,
        compiler_params=pltpu.CompilerParams(vmem_limit_bytes=4 * MIB),
        name="layer_sum",
    )(got)


def local(act_rows, back_rows, act_cols, back_cols):
    layers, tcols = lax.axis_size("layer"), lax.axis_size("tcol")
    planes = tcols // 2
    half = planes // 2
    depth = act_rows.shape[2]

    def along(steps):
        return [(2 * p + c, 2 * ((p + (steps, -steps)[c]) % planes) + c) for p in range(planes) for c in range(2)]

    def aslant(steps):
        return [(2 * p + c, 2 * ((p + (-steps, steps)[c]) % planes) + 1 - c) for p in range(planes) for c in range(2)]

    own = jnp.concatenate((act_rows[0], back_rows[0]), axis=0)
    mine, next_ = {0: own}, {}
    for steps in (LEAD, 1):
        mine[steps] = lax.ppermute(own, "tcol", along(steps))
        next_[steps] = lax.ppermute(own, "tcol", aslant(steps))
    for steps in range(2, half + 1):
        if steps == LEAD:
            continue
        mine[steps] = lax.ppermute(mine[steps - 1], "tcol", along(1))
        if steps < half:
            next_[steps] = lax.ppermute(next_[steps - 1], "tcol", along(1))
    across = [(0, 1), (1, 0)]
    other_act = lax.ppermute(act_cols[0], "trow", across)
    other_back = lax.ppermute(back_cols[0], "trow", across)
    cores = [(t, t ^ 1) for t in range(tcols)]
    given = []
    for group in GROUPS:
        parts = [(mine, next_)[stream][steps] for stream, steps in group]
        given.append(lax.ppermute(stack(parts), "tcol", cores))

    act, back = in_order([mine[s] for s in range(half + 1)], [next_[s] for s in range(1, half)], given)
    cols_act = jnp.concatenate((act_cols[0], other_act), axis=0)
    cols_back = jnp.concatenate((back_cols[0], other_back), axis=0)
    gram_act = jnp.einsum("rd,cd->rc", act, cols_act, preferred_element_type=jnp.float32)
    gram_back = jnp.einsum("rd,cd->rc", back, cols_back, preferred_element_type=jnp.float32)
    terms = gram_act * gram_back / depth
    got = lax.all_to_all(terms.reshape(layers, -1, terms.shape[-1]), "layer", 0, 0, tiled=True)
    return layer_sum(got)


def solution(mesh):
    in_specs = (
        P("layer", ("trow", "tcol"), None),
        P("layer", ("trow", "tcol"), None),
        P("layer", ("tcol", "trow"), None),
        P("layer", ("tcol", "trow"), None),
    )
    out_specs = P(("trow", "layer"), "tcol")
    return jax.shard_map(local, mesh=mesh, in_specs=in_specs, out_specs=out_specs, check_vma=False)
```

time: 194 us -> 149 us (0.77)
  waiting for transfers between devices: 153 us -> 50.2 us
  starting transfers between devices: 0.04 us -> 66.5 us
  Pallas kernels: 0 us -> 13.8 us
  between operations: 13.4 us -> 0.34 us
  matrix products: 7.32 us -> 2.57 us
  other arithmetic: 4.52 us -> 1.07 us
    all_gather x2 -> x0, waiting for transfers between devices: 153 us -> none  [in_one_piece(): lax.all_gather(both, axis, axis=dim, tiled=True)]
    ppermute x0 -> x20, starting transfers between devices: none -> 66.5 us  [the longest x2 18.4 us: local(): next_[steps] = lax.ppermute(own, 'tcol', aslant(steps))]
    ppermute x0 -> x20, waiting for transfers between devices: none -> 50.2 us  [the longest x1 20.2 us: local(): other_act = lax.ppermute(act_cols[0], 'trow', across)]
    pallas_call x0 -> x5, Pallas kernels: none -> 13.8 us  [the longest x1 12.8 us: in_order(): pl.pallas_call(functools.partial(order_kernel, half), out_shape=(rows, ro...]
    dot_general x2, matrix products: 7.32 us -> 2.57 us  [the longest x1 1.28 us: local(): jnp.einsum('rd,cd->rc', act, cols_act, preferred_element_type=jnp.float32)]
    concatenate x2 -> x1, other arithmetic: 3.85 us -> 1.07 us  [local(): own = jnp.concatenate((act_rows[0], back_rows[0]), axis=0)]
  transfers between devices with their start and end apart: 2 -> 20, of which waited for: 2 -> 6; matrix products, arithmetic and copies ran while one was open for 0% -> 1% of each run, Pallas kernels for 0% -> 9%
where the time goes in v2:
time: 149 us; the launch traced here: 148 us
  starting transfers between devices  66.5 us (45%)
  waiting for transfers between devices  50.2 us (34%)
  Pallas kernels  13.8 us (9%)
  blocking collectives  13.8 us (9%)
  matrix products  2.57 us (2%)
    ppermute x1, waiting for transfers between devices, local(): other_act = lax.ppermute(act_cols[0], 'trow', across)  20.2 us
    ppermute x2, starting transfers between devices, local(): next_[steps] = lax.ppermute(own, 'tcol', aslant(steps))  18.4 us
    ppermute x6, starting transfers between devices, local(): mine[steps] = lax.ppermute(mine[steps - 1], 'tcol', along(1))  18 us
    ppermute x2, waiting for transfers between devices, local(): next_[steps] = lax.ppermute(own, 'tcol', aslant(steps))  15.4 us
    all_to_all x1, blocking collectives, local(): lax.all_to_all(terms.reshape(layers, -1, terms.shape[-1]), 'layer', 0, 0,...  13.8 us
    ppermute x5, starting transfers between devices, local(): next_[steps] = lax.ppermute(next_[steps - 1], 'tcol', along(1))  13.6 us
    pallas_call x1, Pallas kernels, in_order(): pl.pallas_call(functools.partial(order_kernel, half), out_shape=(rows, ro...  12.8 us
    ppermute x6, waiting for transfers between devices, local(): mine[steps] = lax.ppermute(mine[steps - 1], 'tcol', along(1))  10.4 us
  transfers between devices with their start and end apart: 20, of which 6 were waited for; matrix products, arithmetic and copies ran while one was open for 1% of the time, Pallas kernels for 9%

profile of v2, /device:TPU:24, one launch (start us, length us, event | category | flops | bytes accessed | tf_op | source)
XLA Modules:
  0.0 148.2 jit_solution(4204394608084044130)
XLA Ops:
  0.0 1.1 pad_maximum_fusion.refs_0_
  1.1 0.0 copy-start.1
  1.1 11.9 %collective-permute-start.10 = (bf16[32,4096]{1,0:T(8,128)(2,1)S(1)}, bf16[32,4096]{1,0:T(8,128)(2,1)S(1)}, u32[]{:S(2)}, u32[]{:S(2)}) collective-permute-start(bf16[32,4096]{1,0:T(8,128)(2,1)S(1)} %pad_maximum_fusion.refs_0_), channel_id=1, source_target_pairs={{0,27},{1,6},{2,29},{3,8},{4,31},{5,10},{6,1},{7,12},{8,3},{9,14},... | collective-permute-start | bytes 786440 | tf_op jit(solution)/shard_map/ppermute | solution.py:123
  13.0 1.9 %collective-permute-start.2 = (bf16[32,4096]{1,0:T(8,128)(2,1)S(1)}, bf16[32,4096]{1,0:T(8,128)(2,1)S(1)}, u32[]{:S(2)}, u32[]{:S(2)}) collective-permute-start(bf16[32,4096]{1,0:T(8,128)(2,1)S(1)} %pad_maximum_fusion.refs_0_), channel_id=1, source_target_pairs={{0,6},{1,27},{2,8},{3,29},{4,10},{5,31},{6,12},{7,1},{8,14},{9,3},... | collective-permute-start | bytes 786440 | tf_op jit(solution)/shard_map/ppermute | solution.py:122
  14.9 15.4 %collective-permute-done.10.refs_6_.refs_11_ = bf16[32,4096]{1,0:T(8,128)(2,1)S(1)} collective-permute-done((bf16[32,4096]{1,0:T(8,128)(2,1)S(1)}, bf16[32,4096]{1,0:T(8,128)(2,1)S(1)}, u32[]{:S(2)}, u32[]{:S(2)}) %collective-permute-start.10) | collective-permute-done | bytes 262176 | tf_op jit(solution)/shard_map/ppermute | solution.py:123
  30.3 1.9 %collective-permute-start.11 = (bf16[32,4096]{1,0:T(8,128)(2,1)S(1)}, bf16[32,4096]{1,0:T(8,128)(2,1)S(1)}, u32[]{:S(2)}, u32[]{:S(2)}) collective-permute-start(bf16[32,4096]{1,0:T(8,128)(2,1)S(1)} %collective-permute-done.10.refs_6_.refs_11_), channel_id=1, source_target_pairs={{0,2},{1,31},{2,4},{3,1},{4,6},{5,3},{6,8},{7,5},{8,10},{9,7},{10,... | collective-permute-start | bytes 786440 | tf_op jit(solution)/shard_map/ppermute | solution.py:129
  32.2 0.0 collective-permute-done.2.refs_5_.refs_3_
  32.2 2.1 %collective-permute-start.3 = (bf16[32,4096]{1,0:T(8,128)(2,1)S(1)}, bf16[32,4096]{1,0:T(8,128)(2,1)S(1)}, u32[]{:S(2)}, u32[]{:S(2)}) collective-permute-start(bf16[32,4096]{1,0:T(8,128)(2,1)S(1)} %collective-permute-done.2.refs_5_.refs_3_), channel_id=1, source_target_pairs={{0,2},{1,31},{2,4},{3,1},{4,6},{5,3},{6,8},{7,5},{8,10},{9,7},{10,... | collective-permute-start | bytes 786440 | tf_op jit(solution)/shard_map/ppermute | solution.py:127
  34.4 2.6 %collective-permute-start = (bf16[32,4096]{1,0:T(8,128)(2,1)S(1)}, bf16[32,4096]{1,0:T(8,128)(2,1)S(1)}, u32[]{:S(2)}, u32[]{:S(2)}) collective-permute-start(bf16[32,4096]{1,0:T(8,128)(2,1)S(1)} %pad_maximum_fusion.refs_0_), channel_id=1, source_target_pairs={{0,2},{1,31},{2,4},{3,1},{4,6},{5,3},{6,8},{7,5},{8,10},{9,7},{10,... | collective-permute-start | bytes 786440 | tf_op jit(solution)/shard_map/ppermute | solution.py:122
  37.0 6.5 %collective-permute-start.8 = (bf16[32,4096]{1,0:T(8,128)(2,1)S(1)}, bf16[32,4096]{1,0:T(8,128)(2,1)S(1)}, u32[]{:S(2)}, u32[]{:S(2)}) collective-permute-start(bf16[32,4096]{1,0:T(8,128)(2,1)S(1)} %pad_maximum_fusion.refs_0_), channel_id=1, source_target_pairs={{0,31},{1,2},{2,1},{3,4},{4,3},{5,6},{6,5},{7,8},{8,7},{9,10},{10,... | collective-permute-start | bytes 786440 | tf_op jit(solution)/shard_map/ppermute | solution.py:123
  43.5 0.0 collective-permute-done.11.refs_1_.refs_12_
  43.5 3.6 %collective-permute-start.12 = (bf16[32,4096]{1,0:T(8,128)(2,1)S(1)}, bf16[32,4096]{1,0:T(8,128)(2,1)S(1)}, u32[]{:S(2)}, u32[]{:S(2)}) collective-permute-start(bf16[32,4096]{1,0:T(8,128)(2,1)S(1)} %collective-permute-done.11.refs_1_.refs_12_), channel_id=1, source_target_pairs={{0,2},{1,31},{2,4},{3,1},{4,6},{5,3},{6,8},{7,5},{8,10},{9,7},{10,... | collective-permute-start | bytes 786440 | tf_op jit(solution)/shard_map/ppermute | solution.py:129
  47.1 0.0 collective-permute-done.3.refs_0_.refs_4_
  47.1 1.9 %collective-permute-start.4 = (bf16[32,4096]{1,0:T(8,128)(2,1)S(1)}, bf16[32,4096]{1,0:T(8,128)(2,1)S(1)}, u32[]{:S(2)}, u32[]{:S(2)}) collective-permute-start(bf16[32,4096]{1,0:T(8,128)(2,1)S(1)} %collective-permute-done.3.refs_0_.refs_4_), channel_id=1, source_target_pairs={{0,2},{1,31},{2,4},{3,1},{4,6},{5,3},{6,8},{7,5},{8,10},{9,7},{10,... | collective-permute-start | bytes 786440 | tf_op jit(solution)/shard_map/ppermute | solution.py:127
  49.1 0.0 collective-permute-done.refs_1_
  49.1 2.5 %collective-permute-start.1 = (bf16[32,4096]{1,0:T(8,128)(2,1)S(1)}, bf16[32,4096]{1,0:T(8,128)(2,1)S(1)}, u32[]{:S(2)}, u32[]{:S(2)}) collective-permute-start(bf16[32,4096]{1,0:T(8,128)(2,1)S(1)} %collective-permute-done.refs_1_), channel_id=1, source_target_pairs={{0,2},{1,31},{2,4},{3,1},{4,6},{5,3},{6,8},{7,5},{8,10},{9,7},{10,... | collective-permute-start | bytes 786440 | tf_op jit(solution)/shard_map/ppermute | solution.py:127
  51.6 0.0 collective-permute-done.8.refs_2_.refs_9_
  51.6 1.9 %collective-permute-start.9 = (bf16[32,4096]{1,0:T(8,128)(2,1)S(1)}, bf16[32,4096]{1,0:T(8,128)(2,1)S(1)}, u32[]{:S(2)}, u32[]{:S(2)}) collective-permute-start(bf16[32,4096]{1,0:T(8,128)(2,1)S(1)} %collective-permute-done.8.refs_2_.refs_9_), channel_id=1, source_target_pairs={{0,2},{1,31},{2,4},{3,1},{4,6},{5,3},{6,8},{7,5},{8,10},{9,7},{10,... | collective-permute-start | bytes 786440 | tf_op jit(solution)/shard_map/ppermute | solution.py:129
  53.5 0.0 collective-permute-done.12.refs_3_.refs_13_
  53.5 3.3 %collective-permute-start.13 = (bf16[32,4096]{1,0:T(8,128)(2,1)S(1)}, bf16[32,4096]{1,0:T(8,128)(2,1)S(1)}, u32[]{:S(2)}, u32[]{:S(2)}) collective-permute-start(bf16[32,4096]{1,0:T(8,128)(2,1)S(1)} %collective-permute-done.12.refs_3_.refs_13_), channel_id=1, source_target_pairs={{0,2},{1,31},{2,4},{3,1},{4,6},{5,3},{6,8},{7,5},{8,10},{9,7},{10,... | collective-permute-start | bytes 786440 | tf_op jit(solution)/shard_map/ppermute | solution.py:129
  56.8 0.0 collective-permute-done.4.refs_2_.refs_5_
  56.8 6.1 %collective-permute-start.5 = (bf16[32,4096]{1,0:T(8,128)(2,1)S(1)}, bf16[32,4096]{1,0:T(8,128)(2,1)S(1)}, u32[]{:S(2)}, u32[]{:S(2)}) collective-permute-start(bf16[32,4096]{1,0:T(8,128)(2,1)S(1)} %collective-permute-done.4.refs_2_.refs_5_), channel_id=1, source_target_pairs={{0,2},{1,31},{2,4},{3,1},{4,6},{5,3},{6,8},{7,5},{8,10},{9,7},{10,... | collective-permute-start | bytes 786440 | tf_op jit(solution)/shard_map/ppermute | solution.py:127
  62.9 0.0 collective-permute-done.1.refs_3_.refs_2_
  62.9 0.0 collective-permute-done.9.refs_4_.refs_10_
  62.9 0.1 stack.3
  63.1 1.9 %collective-permute-start.15 = (bf16[224,4096]{1,0:T(8,128)(2,1)S(1)}, bf16[224,4096]{1,0:T(8,128)(2,1)S(1)}, u32[]{:S(2)}, u32[]{:S(2)}) collective-permute-start(bf16[224,4096]{1,0:T(8,128)(2,1)S(1)} %stack.3), channel_id=1, source_target_pairs={{0,1},{1,0},{2,3},{3,2},{4,5},{5,4},{6,7},{7,6},{8,9},{9,8},{10,11... | collective-permute-start | bytes 5505032 | tf_op jit(solution)/shard_map/ppermute | solution.py:137
  65.0 0.0 collective-permute-done.13.refs_5_.refs_14_
  65.1 2.8 %collective-permute-done.5.refs_4_.refs_6_ = bf16[32,4096]{1,0:T(8,128)(2,1)S(1)} collective-permute-done((bf16[32,4096]{1,0:T(8,128)(2,1)S(1)}, bf16[32,4096]{1,0:T(8,128)(2,1)S(1)}, u32[]{:S(2)}, u32[]{:S(2)}) %collective-permute-start.5) | collective-permute-done | bytes 262176 | tf_op jit(solution)/shard_map/ppermute | solution.py:127
  67.9 0.1 stack.4
  68.0 1.9 %collective-permute-start.16 = (bf16[192,4096]{1,0:T(8,128)(2,1)S(1)}, bf16[192,4096]{1,0:T(8,128)(2,1)S(1)}, u32[]{:S(2)}, u32[]{:S(2)}) collective-permute-start(bf16[192,4096]{1,0:T(8,128)(2,1)S(1)} %stack.4), channel_id=1, source_target_pairs={{0,1},{1,0},{2,3},{3,2},{4,5},{5,4},{6,7},{7,6},{8,9},{9,8},{10,11... | collective-permute-start | bytes 4718600 | tf_op jit(solution)/shard_map/ppermute | solution.py:137
  69.9 3.3 %collective-permute-start.6 = (bf16[32,4096]{1,0:T(8,128)(2,1)S(1)}, bf16[32,4096]{1,0:T(8,128)(2,1)S(1)}, u32[]{:S(2)}, u32[]{:S(2)}) collective-permute-start(bf16[32,4096]{1,0:T(8,128)(2,1)S(1)} %collective-permute-done.5.refs_4_.refs_6_), channel_id=1, source_target_pairs={{0,2},{1,31},{2,4},{3,1},{4,6},{5,3},{6,8},{7,5},{8,10},{9,7},{10,... | collective-permute-start | bytes 786440 | tf_op jit(solution)/shard_map/ppermute | solution.py:127
  73.2 2.8 %collective-permute-start.14 = (bf16[32,4096]{1,0:T(8,128)(2,1)S(1)}, bf16[32,4096]{1,0:T(8,128)(2,1)S(1)}, u32[]{:S(2)}, u32[]{:S(2)}) collective-permute-start(bf16[32,4096]{1,0:T(8,128)(2,1)S(1)} %collective-permute-done.13.refs_5_.refs_14_), channel_id=1, source_target_pairs={{0,2},{1,31},{2,4},{3,1},{4,6},{5,3},{6,8},{7,5},{8,10},{9,7},{10,... | collective-permute-start | bytes 786440 | tf_op jit(solution)/shard_map/ppermute | solution.py:129
  76.0 3.3 %collective-permute-done.6.refs_0_.refs_7_ = bf16[32,4096]{1,0:T(8,128)(2,1)S(1)} collective-permute-done((bf16[32,4096]{1,0:T(8,128)(2,1)S(1)}, bf16[32,4096]{1,0:T(8,128)(2,1)S(1)}, u32[]{:S(2)}, u32[]{:S(2)}) %collective-permute-start.6) | collective-permute-done | bytes 262176 | tf_op jit(solution)/shard_map/ppermute | solution.py:127
  79.4 2.1 %collective-permute-start.7 = (bf16[32,4096]{1,0:T(8,128)(2,1)S(1)}, bf16[32,4096]{1,0:T(8,128)(2,1)S(1)}, u32[]{:S(2)}, u32[]{:S(2)}) collective-permute-start(bf16[32,4096]{1,0:T(8,128)(2,1)S(1)} %collective-permute-done.6.refs_0_.refs_7_), channel_id=1, source_target_pairs={{0,2},{1,31},{2,4},{3,1},{4,6},{5,3},{6,8},{7,5},{8,10},{9,7},{10,... | collective-permute-start | bytes 786440 | tf_op jit(solution)/shard_map/ppermute | solution.py:127
  81.5 3.1 %collective-permute-start.19 = (bf16[128,4096]{1,0:T(8,128)(2,1)S(1)}, bf16[128,4096]{1,0:T(8,128)(2,1)S(1)}, u32[]{:S(2)}, u32[]{:S(2)}) collective-permute-start(bf16[128,4096]{1,0:T(8,128)(2,1)S(1)} %bitcast.10), channel_id=1, source_target_pairs={{0,32},{32,0},{1,33},{33,1},{2,34},{34,2},{3,35},{35,3},{4,36},{36... | collective-permute-start | bytes 3145736 | tf_op jit(solution)/shard_map/ppermute | solution.py:132
  84.7 0.0 collective-permute-done.14.refs_1_.refs_15_
  84.7 4.2 %collective-permute-done.7.refs_2_.refs_8_ = bf16[32,4096]{1,0:T(8,128)(2,1)S(1)} collective-permute-done((bf16[32,4096]{1,0:T(8,128)(2,1)S(1)}, bf16[32,4096]{1,0:T(8,128)(2,1)S(1)}, u32[]{:S(2)}, u32[]{:S(2)}) %collective-permute-start.7) | collective-permute-done | bytes 262176 | tf_op jit(solution)/shard_map/ppermute | solution.py:127
  88.9 0.1 stack.5
  88.9 1.9 %collective-permute-start.17 = (bf16[96,4096]{1,0:T(8,128)(2,1)S(1)}, bf16[96,4096]{1,0:T(8,128)(2,1)S(1)}, u32[]{:S(2)}, u32[]{:S(2)}) collective-permute-start(bf16[96,4096]{1,0:T(8,128)(2,1)S(1)} %stack.5), channel_id=1, source_target_pairs={{0,1},{1,0},{2,3},{3,2},{4,5},{5,4},{6,7},{7,6},{8,9},{9,8},{10,11... | collective-permute-start | bytes 2359304 | tf_op jit(solution)/shard_map/ppermute | solution.py:137
  90.9 3.1 %collective-permute-start.18 = (bf16[128,4096]{1,0:T(8,128)(2,1)S(1)}, bf16[128,4096]{1,0:T(8,128)(2,1)S(1)}, u32[]{:S(2)}, u32[]{:S(2)}) collective-permute-start(bf16[128,4096]{1,0:T(8,128)(2,1)S(1)} %bitcast.12), channel_id=1, source_target_pairs={{0,32},{32,0},{1,33},{33,1},{2,34},{34,2},{3,35},{35,3},{4,36},{36... | collective-permute-start | bytes 3145736 | tf_op jit(solution)/shard_map/ppermute | solution.py:131
  94.0 0.0 collective-permute-done.15.refs_16_
  94.1 12.8 %order.1 = (bf16[512,4096]{1,0:T(8,128)(2,1)S(1)}, bf16[512,4096]{1,0:T(8,128)(2,1)S(1)}) custom-call(bf16[32,4096]{1,0:T(8,128)(2,1)S(1)} %pad_maximum_fusion.refs_0_, bf16[32,4096]{1,0:T(8,128)(2,1)S(1)} %collective-permute-done.refs_1_, bf16[32,4096]{1,0:T(8,128)(2,1)S(1)} %collective-permute-done.1.refs_3_.refs_2_, ...), custom_call_target="tpu_custom_call" | custom-call | flops 1000000000 | tf_op jit(solution)/shard_map/order/pallas_call | solution.py:76
  106.8 4.1 %collective-permute-done.19 = bf16[128,4096]{1,0:T(8,128)(2,1)S(1)} collective-permute-done((bf16[128,4096]{1,0:T(8,128)(2,1)S(1)}, bf16[128,4096]{1,0:T(8,128)(2,1)S(1)}, u32[]{:S(2)}, u32[]{:S(2)}) %collective-permute-start.19) | collective-permute-done | bytes 1048608 | tf_op jit(solution)/shard_map/ppermute | solution.py:132
  110.9 1.3 fusion.4
  112.2 20.2 %collective-permute-done.18 = bf16[128,4096]{1,0:T(8,128)(2,1)S(1)} collective-permute-done((bf16[128,4096]{1,0:T(8,128)(2,1)S(1)}, bf16[128,4096]{1,0:T(8,128)(2,1)S(1)}, u32[]{:S(2)}, u32[]{:S(2)}) %collective-permute-start.18) | collective-permute-done | bytes 1048608 | tf_op jit(solution)/shard_map/ppermute | solution.py:131
  132.5 1.3 multiply_multiply_fusion
  133.7 13.8 %all_to_all.5.got = f32[8,64,256]{2,1,0:T(8,128)S(1)} all-to-all(f32[8,64,256]{2,1,0:T(8,128)S(1)} %bitcast.7), channel_id=1, replica_groups=mesh['layer'=8,'trow'=2,'tcol'=32] {'layer'}, dimensions={0} | all-to-all | bytes 1048576 | tf_op jit(solution)/shard_map/all_to_all | solution.py:145
  147.5 0.7 layer_sum.1
  (5 shorter events, 0.0 us)
Async XLA Ops:
  0.0 81.5 %copy-start = (bf16[1,128,4096]{2,1,0:T(8,128)(2,1)S(1)}, bf16[1,128,4096]{2,1,0:T(8,128)(2,1)}, u32[]{:S(2)}) copy-start(bf16[1,128,4096]{2,1,0:T(8,128)(2,1)} %param.7) | copy-start | bytes 3145732
  1.1 89.8 %copy-start.1 = (bf16[1,128,4096]{2,1,0:T(8,128)(2,1)S(1)}, bf16[1,128,4096]{2,1,0:T(8,128)(2,1)}, u32[]{:S(2)}) copy-start(bf16[1,128,4096]{2,1,0:T(8,128)(2,1)} %param.6) | copy-start | bytes 3145732
  1.1 29.2 %collective-permute-start.10 = (bf16[32,4096]{1,0:T(8,128)(2,1)S(1)}, bf16[32,4096]{1,0:T(8,128)(2,1)S(1)}, u32[]{:S(2)}, u32[]{:S(2)}) collective-permute-start(bf16[32,4096]{1,0:T(8,128)(2,1)S(1)} %pad_maximum_fusion.refs_0_), channel_id=1, source_target_pairs={{0,27},{1,6},{2,29},{3,8},{4,31},{5,10},{6,1},{7,12},{8,3},{9,14},... | collective-permute-start | bytes 786440 | tf_op jit(solution)/shard_map/ppermute | solution.py:123
  13.0 19.3 %collective-permute-start.2 = (bf16[32,4096]{1,0:T(8,128)(2,1)S(1)}, bf16[32,4096]{1,0:T(8,128)(2,1)S(1)}, u32[]{:S(2)}, u32[]{:S(2)}) collective-permute-start(bf16[32,4096]{1,0:T(8,128)(2,1)S(1)} %pad_maximum_fusion.refs_0_), channel_id=1, source_target_pairs={{0,6},{1,27},{2,8},{3,29},{4,10},{5,31},{6,12},{7,1},{8,14},{9,3},... | collective-permute-start | bytes 786440 | tf_op jit(solution)/shard_map/ppermute | solution.py:122
  30.3 13.2 %collective-permute-start.11 = (bf16[32,4096]{1,0:T(8,128)(2,1)S(1)}, bf16[32,4096]{1,0:T(8,128)(2,1)S(1)}, u32[]{:S(2)}, u32[]{:S(2)}) collective-permute-start(bf16[32,4096]{1,0:T(8,128)(2,1)S(1)} %collective-permute-done.10.refs_6_.refs_11_), channel_id=1, source_target_pairs={{0,2},{1,31},{2,4},{3,1},{4,6},{5,3},{6,8},{7,5},{8,10},{9,7},{10,... | collective-permute-start | bytes 786440 | tf_op jit(solution)/shard_map/ppermute | solution.py:129
  32.2 14.9 %collective-permute-start.3 = (bf16[32,4096]{1,0:T(8,128)(2,1)S(1)}, bf16[32,4096]{1,0:T(8,128)(2,1)S(1)}, u32[]{:S(2)}, u32[]{:S(2)}) collective-permute-start(bf16[32,4096]{1,0:T(8,128)(2,1)S(1)} %collective-permute-done.2.refs_5_.refs_3_), channel_id=1, source_target_pairs={{0,2},{1,31},{2,4},{3,1},{4,6},{5,3},{6,8},{7,5},{8,10},{9,7},{10,... | collective-permute-start | bytes 786440 | tf_op jit(solution)/shard_map/ppermute | solution.py:127
  34.4 14.7 %collective-permute-start = (bf16[32,4096]{1,0:T(8,128)(2,1)S(1)}, bf16[32,4096]{1,0:T(8,128)(2,1)S(1)}, u32[]{:S(2)}, u32[]{:S(2)}) collective-permute-start(bf16[32,4096]{1,0:T(8,128)(2,1)S(1)} %pad_maximum_fusion.refs_0_), channel_id=1, source_target_pairs={{0,2},{1,31},{2,4},{3,1},{4,6},{5,3},{6,8},{7,5},{8,10},{9,7},{10,... | collective-permute-start | bytes 786440 | tf_op jit(solution)/shard_map/ppermute | solution.py:122
  37.0 14.6 %collective-permute-start.8 = (bf16[32,4096]{1,0:T(8,128)(2,1)S(1)}, bf16[32,4096]{1,0:T(8,128)(2,1)S(1)}, u32[]{:S(2)}, u32[]{:S(2)}) collective-permute-start(bf16[32,4096]{1,0:T(8,128)(2,1)S(1)} %pad_maximum_fusion.refs_0_), channel_id=1, source_target_pairs={{0,31},{1,2},{2,1},{3,4},{4,3},{5,6},{6,5},{7,8},{8,7},{9,10},{10,... | collective-permute-start | bytes 786440 | tf_op jit(solution)/shard_map/ppermute | solution.py:123
  43.5 10.0 %collective-permute-start.12 = (bf16[32,4096]{1,0:T(8,128)(2,1)S(1)}, bf16[32,4096]{1,0:T(8,128)(2,1)S(1)}, u32[]{:S(2)}, u32[]{:S(2)}) collective-permute-start(bf16[32,4096]{1,0:T(8,128)(2,1)S(1)} %collective-permute-done.11.refs_1_.refs_12_), channel_id=1, source_target_pairs={{0,2},{1,31},{2,4},{3,1},{4,6},{5,3},{6,8},{7,5},{8,10},{9,7},{10,... | collective-permute-start | bytes 786440 | tf_op jit(solution)/shard_map/ppermute | solution.py:129
  47.1 9.7 %collective-permute-start.4 = (bf16[32,4096]{1,0:T(8,128)(2,1)S(1)}, bf16[32,4096]{1,0:T(8,128)(2,1)S(1)}, u32[]{:S(2)}, u32[]{:S(2)}) collective-permute-start(bf16[32,4096]{1,0:T(8,128)(2,1)S(1)} %collective-permute-done.3.refs_0_.refs_4_), channel_id=1, source_target_pairs={{0,2},{1,31},{2,4},{3,1},{4,6},{5,3},{6,8},{7,5},{8,10},{9,7},{10,... | collective-permute-start | bytes 786440 | tf_op jit(solution)/shard_map/ppermute | solution.py:127
  49.1 13.8 %collective-permute-start.1 = (bf16[32,4096]{1,0:T(8,128)(2,1)S(1)}, bf16[32,4096]{1,0:T(8,128)(2,1)S(1)}, u32[]{:S(2)}, u32[]{:S(2)}) collective-permute-start(bf16[32,4096]{1,0:T(8,128)(2,1)S(1)} %collective-permute-done.refs_1_), channel_id=1, source_target_pairs={{0,2},{1,31},{2,4},{3,1},{4,6},{5,3},{6,8},{7,5},{8,10},{9,7},{10,... | collective-permute-start | bytes 786440 | tf_op jit(solution)/shard_map/ppermute | solution.py:127
  51.6 11.4 %collective-permute-start.9 = (bf16[32,4096]{1,0:T(8,128)(2,1)S(1)}, bf16[32,4096]{1,0:T(8,128)(2,1)S(1)}, u32[]{:S(2)}, u32[]{:S(2)}) collective-permute-start(bf16[32,4096]{1,0:T(8,128)(2,1)S(1)} %collective-permute-done.8.refs_2_.refs_9_), channel_id=1, source_target_pairs={{0,2},{1,31},{2,4},{3,1},{4,6},{5,3},{6,8},{7,5},{8,10},{9,7},{10,... | collective-permute-start | bytes 786440 | tf_op jit(solution)/shard_map/ppermute | solution.py:129
  53.5 11.6 %collective-permute-start.13 = (bf16[32,4096]{1,0:T(8,128)(2,1)S(1)}, bf16[32,4096]{1,0:T(8,128)(2,1)S(1)}, u32[]{:S(2)}, u32[]{:S(2)}) collective-permute-start(bf16[32,4096]{1,0:T(8,128)(2,1)S(1)} %collective-permute-done.12.refs_3_.refs_13_), channel_id=1, source_target_pairs={{0,2},{1,31},{2,4},{3,1},{4,6},{5,3},{6,8},{7,5},{8,10},{9,7},{10,... | collective-permute-start | bytes 786440 | tf_op jit(solution)/shard_map/ppermute | solution.py:129
  56.8 11.0 %collective-permute-start.5 = (bf16[32,4096]{1,0:T(8,128)(2,1)S(1)}, bf16[32,4096]{1,0:T(8,128)(2,1)S(1)}, u32[]{:S(2)}, u32[]{:S(2)}) collective-permute-start(bf16[32,4096]{1,0:T(8,128)(2,1)S(1)} %collective-permute-done.4.refs_2_.refs_5_), channel_id=1, source_target_pairs={{0,2},{1,31},{2,4},{3,1},{4,6},{5,3},{6,8},{7,5},{8,10},{9,7},{10,... | collective-permute-start | bytes 786440 | tf_op jit(solution)/shard_map/ppermute | solution.py:127
  63.1 30.9 %collective-permute-start.15 = (bf16[224,4096]{1,0:T(8,128)(2,1)S(1)}, bf16[224,4096]{1,0:T(8,128)(2,1)S(1)}, u32[]{:S(2)}, u32[]{:S(2)}) collective-permute-start(bf16[224,4096]{1,0:T(8,128)(2,1)S(1)} %stack.3), channel_id=1, source_target_pairs={{0,1},{1,0},{2,3},{3,2},{4,5},{5,4},{6,7},{7,6},{8,9},{9,8},{10,11... | collective-permute-start | bytes 5505032 | tf_op jit(solution)/shard_map/ppermute | solution.py:137
  68.0 26.1 %collective-permute-start.16 = (bf16[192,4096]{1,0:T(8,128)(2,1)S(1)}, bf16[192,4096]{1,0:T(8,128)(2,1)S(1)}, u32[]{:S(2)}, u32[]{:S(2)}) collective-permute-start(bf16[192,4096]{1,0:T(8,128)(2,1)S(1)} %stack.4), channel_id=1, source_target_pairs={{0,1},{1,0},{2,3},{3,2},{4,5},{5,4},{6,7},{7,6},{8,9},{9,8},{10,11... | collective-permute-start | bytes 4718600 | tf_op jit(solution)/shard_map/ppermute | solution.py:137
  69.9 9.5 %collective-permute-start.6 = (bf16[32,4096]{1,0:T(8,128)(2,1)S(1)}, bf16[32,4096]{1,0:T(8,128)(2,1)S(1)}, u32[]{:S(2)}, u32[]{:S(2)}) collective-permute-start(bf16[32,4096]{1,0:T(8,128)(2,1)S(1)} %collective-permute-done.5.refs_4_.refs_6_), channel_id=1, source_target_pairs={{0,2},{1,31},{2,4},{3,1},{4,6},{5,3},{6,8},{7,5},{8,10},{9,7},{10,... | collective-permute-start | bytes 786440 | tf_op jit(solution)/shard_map/ppermute | solution.py:127
  73.2 11.4 %collective-permute-start.14 = (bf16[32,4096]{1,0:T(8,128)(2,1)S(1)}, bf16[32,4096]{1,0:T(8,128)(2,1)S(1)}, u32[]{:S(2)}, u32[]{:S(2)}) collective-permute-start(bf16[32,4096]{1,0:T(8,128)(2,1)S(1)} %collective-permute-done.13.refs_5_.refs_14_), channel_id=1, source_target_pairs={{0,2},{1,31},{2,4},{3,1},{4,6},{5,3},{6,8},{7,5},{8,10},{9,7},{10,... | collective-permute-start | bytes 786440 | tf_op jit(solution)/shard_map/ppermute | solution.py:129
  79.4 9.5 %collective-permute-start.7 = (bf16[32,4096]{1,0:T(8,128)(2,1)S(1)}, bf16[32,4096]{1,0:T(8,128)(2,1)S(1)}, u32[]{:S(2)}, u32[]{:S(2)}) collective-permute-start(bf16[32,4096]{1,0:T(8,128)(2,1)S(1)} %collective-permute-done.6.refs_0_.refs_7_), channel_id=1, source_target_pairs={{0,2},{1,31},{2,4},{3,1},{4,6},{5,3},{6,8},{7,5},{8,10},{9,7},{10,... | collective-permute-start | bytes 786440 | tf_op jit(solution)/shard_map/ppermute | solution.py:127
  81.5 29.4 %collective-permute-start.19 = (bf16[128,4096]{1,0:T(8,128)(2,1)S(1)}, bf16[128,4096]{1,0:T(8,128)(2,1)S(1)}, u32[]{:S(2)}, u32[]{:S(2)}) collective-permute-start(bf16[128,4096]{1,0:T(8,128)(2,1)S(1)} %bitcast.10), channel_id=1, source_target_pairs={{0,32},{32,0},{1,33},{33,1},{2,34},{34,2},{3,35},{35,3},{4,36},{36... | collective-permute-start | bytes 3145736 | tf_op jit(solution)/shard_map/ppermute | solution.py:132
  88.9 5.1 %collective-permute-start.17 = (bf16[96,4096]{1,0:T(8,128)(2,1)S(1)}, bf16[96,4096]{1,0:T(8,128)(2,1)S(1)}, u32[]{:S(2)}, u32[]{:S(2)}) collective-permute-start(bf16[96,4096]{1,0:T(8,128)(2,1)S(1)} %stack.5), channel_id=1, source_target_pairs={{0,1},{1,0},{2,3},{3,2},{4,5},{5,4},{6,7},{7,6},{8,9},{9,8},{10,11... | collective-permute-start | bytes 2359304 | tf_op jit(solution)/shard_map/ppermute | solution.py:137
  90.9 41.6 %collective-permute-start.18 = (bf16[128,4096]{1,0:T(8,128)(2,1)S(1)}, bf16[128,4096]{1,0:T(8,128)(2,1)S(1)}, u32[]{:S(2)}, u32[]{:S(2)}) collective-permute-start(bf16[128,4096]{1,0:T(8,128)(2,1)S(1)} %bitcast.12), channel_id=1, source_target_pairs={{0,32},{32,0},{1,33},{33,1},{2,34},{34,2},{3,35},{35,3},{4,36},{36... | collective-permute-start | bytes 3145736 | tf_op jit(solution)/shard_map/ppermute | solution.py:131

commit v3 on v2

v3 whole, which is shorter than its diff:
```python
import functools

import jax
import jax.numpy as jnp
from jax import lax
from jax.experimental import pallas as pl
from jax.experimental.pallas import tpu as pltpu
from jax.sharding import PartitionSpec as P


MIB = 1 << 20
VMEM = pl.BlockSpec(memory_space=pltpu.VMEM)
GROUPS = (
    ((0, 0), (0, 1), (1, 1), (0, 2), (1, 2), (0, 3), (1, 3)),
    ((0, 4), (1, 4), (0, 5), (1, 5), (0, 6), (1, 6)),
    ((0, 7), (1, 7), (0, 8), (1, 8)),
)


def stack_kernel(*refs):
    *parts, out = refs
    height = parts[0].shape[0] // 2
    for i, part in enumerate(parts):
        out[0, i * height : (i + 1) * height, :] = part[:height, :]
        out[1, i * height : (i + 1) * height, :] = part[height:, :]


def stack(parts):
    height, depth = parts[0].shape
    return pl.pallas_call(
        stack_kernel,
        out_shape=jax.ShapeDtypeStruct((2, len(parts) * height // 2, depth), parts[0].dtype),
        in_specs=[VMEM] * len(parts),
        out_specs=VMEM,
        compiler_params=pltpu.CompilerParams(vmem_limit_bytes=8 * MIB),
        cost_estimate=pl.CostEstimate(flops=200_000_000, bytes_accessed=0, transcendentals=0),
        name="stack",
    )(*parts)


def order_kernel(height, terms, out):
    tcol = lax.axis_index("tcol")
    z, core = lax.shift_right_logical(tcol, 1), lax.rem(tcol, 2)
    planes = out.shape[0] // (2 * height)
    sign = 1 - 2 * core
    shards = [shard for group in GROUPS for shard in group]

    def put(source, plane, on):
        at = pl.multiple_of((lax.rem(plane + planes, planes) * 2 + on) * height, height)
        out[pl.ds(at, height), :] = terms[pl.ds(source, height), :]

    for i, (stream, step) in enumerate(shards):
        mine_at, given_at = i * height, (len(shards) + i) * height
        if step == planes // 2:
            put(pl.multiple_of(jnp.where(core == 1, mine_at, given_at), height), z + step, 1 - stream)
        else:
            put(mine_at, z - sign * step, core if stream == 0 else 1 - core)
            put(given_at, z + sign * step, 1 - core if stream == 0 else core)


def in_order(terms, height, planes):
    return pl.pallas_call(
        functools.partial(order_kernel, height),
        out_shape=jax.ShapeDtypeStruct((2 * planes * height, terms.shape[1]), terms.dtype),
        in_specs=[VMEM],
        out_specs=VMEM,
        compiler_params=pltpu.CompilerParams(vmem_limit_bytes=4 * MIB),
        name="order",
    )(terms)


def sum_kernel(got, out):
    trow = lax.axis_index("trow")
    width = out.shape[1] // 2
    for half, at in ((0, trow), (1, 1 - trow)):
        to = pl.ds(pl.multiple_of(at * width, width), width)
        out[:, to] = jnp.sum(got[:, :, half * width : (half + 1) * width], axis=0)


def layer_sum(got):
    return pl.pallas_call(
        sum_kernel,
        out_shape=jax.ShapeDtypeStruct(got.shape[1:], got.dtype),
        in_specs=[VMEM],
        out_specs=VMEM,
        compiler_params=pltpu.CompilerParams(vmem_limit_bytes=4 * MIB),
        name="layer_sum",
    )(got)


def local(act_rows, back_rows, act_cols, back_cols):
    layers, tcols = lax.axis_size("layer"), lax.axis_size("tcol")
    planes = tcols // 2
    half = planes // 2
    depth = act_rows.shape[2]

    along = [(2 * p + c, 2 * ((p + (1, -1)[c]) % planes) + c) for p in range(planes) for c in range(2)]
    aslant = [(2 * p + c, 2 * ((p + (-1, 1)[c]) % planes) + 1 - c) for p in range(planes) for c in range(2)]
    cores = [(t, t ^ 1) for t in range(tcols)]

    own = jnp.concatenate((act_rows[0], back_rows[0]), axis=0)
    held = {(0, 0): own, (0, 1): lax.ppermute(own, "tcol", along), (1, 1): lax.ppermute(own, "tcol", aslant)}
    for step in range(2, half + 1):
        pairs = along if step < half else [(a, b) for a, b in along if a % 2 == 1]
        held[0, step] = lax.ppermute(held[0, step - 1], "tcol", pairs)
        held[1, step] = lax.ppermute(held[1, step - 1], "tcol", pairs)
    across = [(0, 1), (1, 0)]
    other_act = lax.ppermute(act_cols[0], "trow", across)
    other_back = lax.ppermute(back_cols[0], "trow", across)
    mine = [stack([held[shard] for shard in group]) for group in GROUPS]
    given = [lax.ppermute(rows, "tcol", cores) for rows in mine]

    act = jnp.concatenate([rows[0] for rows in mine + given], axis=0)
    back = jnp.concatenate([rows[1] for rows in mine + given], axis=0)
    cols_act = jnp.concatenate((act_cols[0], other_act), axis=0)
    cols_back = jnp.concatenate((back_cols[0], other_back), axis=0)
    gram_act = jnp.einsum("rd,cd->rc", act, cols_act, preferred_element_type=jnp.float32)
    gram_back = jnp.einsum("rd,cd->rc", back, cols_back, preferred_element_type=jnp.float32)
    terms = in_order(gram_act * gram_back / depth, act_rows.shape[1], planes)
    got = lax.all_to_all(terms.reshape(layers, -1, terms.shape[-1]), "layer", 0, 0, tiled=True)
    return layer_sum(got)


def solution(mesh):
    in_specs = (
        P("layer", ("trow", "tcol"), None),
        P("layer", ("trow", "tcol"), None),
        P("layer", ("tcol", "trow"), None),
        P("layer", ("tcol", "trow"), None),
    )
    out_specs = P(("trow", "layer"), "tcol")
    return jax.shard_map(local, mesh=mesh, in_specs=in_specs, out_specs=out_specs, check_vma=False)
```

time: 149 us -> 124 us (0.83)
  Pallas kernels: 13.8 us -> 1.07 us
  starting transfers between devices: 66.5 us -> 55.3 us
  waiting for transfers between devices: 50.2 us -> 48.7 us
    pallas_call x4, Pallas kernels: 13.1 us -> 0.41 us  [the longest x3 0.3 us: stack(): pl.pallas_call(stack_kernel, out_shape=jax.ShapeDtypeStruct((2, len(parts...]
    ppermute x18 -> x19, starting transfers between devices: 60.2 us -> 48 us  [the longest x7 12.8 us: local(): held[1, step] = lax.ppermute(held[1, step - 1], 'tcol', pairs)]
    ppermute x18 -> x19, waiting for transfers between devices: 25.8 us -> 33.3 us  [the longest x7 22.5 us: local(): held[0, step] = lax.ppermute(held[0, step - 1], 'tcol', pairs)]
    ppermute x1, waiting for transfers between devices: 20.2 us -> 15.4 us  [local(): other_act = lax.ppermute(act_cols[0], 'trow', across)]
    ppermute x1, waiting for transfers between devices: 4.09 us -> 0.01 us  [local(): other_back = lax.ppermute(back_cols[0], 'trow', across)]
  transfers between devices with their start and end apart: 20 -> 21, of which waited for: 6 -> 13; matrix products, arithmetic and copies ran while one was open for 1% -> 2% of each run, Pallas kernels for 9% -> 0%
where the time goes in v3:
time: 124 us; the launch traced here: 123 us
  starting transfers between devices  55.3 us (45%)
  waiting for transfers between devices  48.7 us (39%)
  blocking collectives  13.1 us (11%)
  matrix products  2.71 us (2%)
    ppermute x7, waiting for transfers between devices, local(): held[0, step] = lax.ppermute(held[0, step - 1], 'tcol', pairs)  22.5 us
    ppermute x1, waiting for transfers between devices, local(): other_act = lax.ppermute(act_cols[0], 'trow', across)  15.4 us
    all_to_all x1, blocking collectives, local(): lax.all_to_all(terms.reshape(layers, -1, terms.shape[-1]), 'layer', 0, 0,...  13.1 us
    ppermute x7, starting transfers between devices, local(): held[1, step] = lax.ppermute(held[1, step - 1], 'tcol', pairs)  12.8 us
    ppermute x7, starting transfers between devices, local(): held[0, step] = lax.ppermute(held[0, step - 1], 'tcol', pairs)  12.1 us
    ppermute x1, starting transfers between devices, local(): lax.ppermute(own, 'tcol', aslant)  9.65 us
    ppermute x3, starting transfers between devices, local(): given = [lax.ppermute(rows, 'tcol', cores) for rows in mine]  9.57 us
    ppermute x7, waiting for transfers between devices, local(): held[1, step] = lax.ppermute(held[1, step - 1], 'tcol', pairs)  5.71 us
  transfers between devices with their start and end apart: 21, of which 13 were waited for; matrix products, arithmetic and copies ran while one was open for 2% of the time, Pallas kernels for 0%

profile of v3, /device:TPU:24, one launch (start us, length us, event | category | flops | bytes accessed | tf_op | source)
XLA Modules:
  0.0 123.1 jit_solution(11048594629554205304)
XLA Ops:
  0.0 1.0 pad_maximum_fusion.refs_0_
  1.0 3.8 %collective-permute-start = (bf16[32,4096]{1,0:T(8,128)(2,1)S(1)}, bf16[32,4096]{1,0:T(8,128)(2,1)S(1)}, u32[]{:S(2)}, u32[]{:S(2)}) collective-permute-start(bf16[32,4096]{1,0:T(8,128)(2,1)S(1)} %pad_maximum_fusion.refs_0_), channel_id=1, source_target_pairs={{0,2},{1,31},{2,4},{3,1},{4,6},{5,3},{6,8},{7,5},{8,10},{9,7},{10,... | collective-permute-start | bytes 786440 | tf_op jit(solution)/shard_map/ppermute | solution.py:102
  4.8 9.7 %collective-permute-start.1 = (bf16[32,4096]{1,0:T(8,128)(2,1)S(1)}, bf16[32,4096]{1,0:T(8,128)(2,1)S(1)}, u32[]{:S(2)}, u32[]{:S(2)}) collective-permute-start(bf16[32,4096]{1,0:T(8,128)(2,1)S(1)} %pad_maximum_fusion.refs_0_), channel_id=1, source_target_pairs={{0,31},{1,2},{2,1},{3,4},{4,3},{5,6},{6,5},{7,8},{8,7},{9,10},{10,... | collective-permute-start | bytes 786440 | tf_op jit(solution)/shard_map/ppermute | solution.py:102
  14.5 3.3 %collective-permute-done.refs_1_ = bf16[32,4096]{1,0:T(8,128)(2,1)S(1)} collective-permute-done((bf16[32,4096]{1,0:T(8,128)(2,1)S(1)}, bf16[32,4096]{1,0:T(8,128)(2,1)S(1)}, u32[]{:S(2)}, u32[]{:S(2)}) %collective-permute-start) | collective-permute-done | bytes 262176 | tf_op jit(solution)/shard_map/ppermute | solution.py:102
  17.8 1.9 %collective-permute-start.2 = (bf16[32,4096]{1,0:T(8,128)(2,1)S(1)}, bf16[32,4096]{1,0:T(8,128)(2,1)S(1)}, u32[]{:S(2)}, u32[]{:S(2)}) collective-permute-start(bf16[32,4096]{1,0:T(8,128)(2,1)S(1)} %collective-permute-done.refs_1_), channel_id=1, source_target_pairs={{0,2},{1,31},{2,4},{3,1},{4,6},{5,3},{6,8},{7,5},{8,10},{9,7},{10,... | collective-permute-start | bytes 786440 | tf_op jit(solution)/shard_map/ppermute | solution.py:105
  19.7 1.9 %collective-permute-start.3 = (bf16[32,4096]{1,0:T(8,128)(2,1)S(1)}, bf16[32,4096]{1,0:T(8,128)(2,1)S(1)}, u32[]{:S(2)}, u32[]{:S(2)}) collective-permute-start(bf16[32,4096]{1,0:T(8,128)(2,1)S(1)} %collective-permute-done.1.refs_2_), channel_id=1, source_target_pairs={{0,2},{1,31},{2,4},{3,1},{4,6},{5,3},{6,8},{7,5},{8,10},{9,7},{10,... | collective-permute-start | bytes 786440 | tf_op jit(solution)/shard_map/ppermute | solution.py:106
  21.6 5.6 %collective-permute-done.2.refs_3_ = bf16[32,4096]{1,0:T(8,128)(2,1)S(1)} collective-permute-done((bf16[32,4096]{1,0:T(8,128)(2,1)S(1)}, bf16[32,4096]{1,0:T(8,128)(2,1)S(1)}, u32[]{:S(2)}, u32[]{:S(2)}) %collective-permute-start.2) | collective-permute-done | bytes 262176 | tf_op jit(solution)/shard_map/ppermute | solution.py:105
  27.2 1.9 %collective-permute-start.4 = (bf16[32,4096]{1,0:T(8,128)(2,1)S(1)}, bf16[32,4096]{1,0:T(8,128)(2,1)S(1)}, u32[]{:S(2)}, u32[]{:S(2)}) collective-permute-start(bf16[32,4096]{1,0:T(8,128)(2,1)S(1)} %collective-permute-done.2.refs_3_), channel_id=1, source_target_pairs={{0,2},{1,31},{2,4},{3,1},{4,6},{5,3},{6,8},{7,5},{8,10},{9,7},{10,... | collective-permute-start | bytes 786440 | tf_op jit(solution)/shard_map/ppermute | solution.py:105
  29.1 0.9 collective-permute-done.3.refs_4_
  30.0 1.9 %collective-permute-start.5 = (bf16[32,4096]{1,0:T(8,128)(2,1)S(1)}, bf16[32,4096]{1,0:T(8,128)(2,1)S(1)}, u32[]{:S(2)}, u32[]{:S(2)}) collective-permute-start(bf16[32,4096]{1,0:T(8,128)(2,1)S(1)} %collective-permute-done.3.refs_4_), channel_id=1, source_target_pairs={{0,2},{1,31},{2,4},{3,1},{4,6},{5,3},{6,8},{7,5},{8,10},{9,7},{10,... | collective-permute-start | bytes 786440 | tf_op jit(solution)/shard_map/ppermute | solution.py:106
  31.9 4.7 %collective-permute-done.4.refs_5_ = bf16[32,4096]{1,0:T(8,128)(2,1)S(1)} collective-permute-done((bf16[32,4096]{1,0:T(8,128)(2,1)S(1)}, bf16[32,4096]{1,0:T(8,128)(2,1)S(1)}, u32[]{:S(2)}, u32[]{:S(2)}) %collective-permute-start.4) | collective-permute-done | bytes 262176 | tf_op jit(solution)/shard_map/ppermute | solution.py:105
  36.7 1.9 %collective-permute-start.6 = (bf16[32,4096]{1,0:T(8,128)(2,1)S(1)}, bf16[32,4096]{1,0:T(8,128)(2,1)S(1)}, u32[]{:S(2)}, u32[]{:S(2)}) collective-permute-start(bf16[32,4096]{1,0:T(8,128)(2,1)S(1)} %collective-permute-done.4.refs_5_), channel_id=1, source_target_pairs={{0,2},{1,31},{2,4},{3,1},{4,6},{5,3},{6,8},{7,5},{8,10},{9,7},{10,... | collective-permute-start | bytes 786440 | tf_op jit(solution)/shard_map/ppermute | solution.py:105
  38.6 0.9 collective-permute-done.5.refs_6_
  39.5 1.9 %collective-permute-start.7 = (bf16[32,4096]{1,0:T(8,128)(2,1)S(1)}, bf16[32,4096]{1,0:T(8,128)(2,1)S(1)}, u32[]{:S(2)}, u32[]{:S(2)}) collective-permute-start(bf16[32,4096]{1,0:T(8,128)(2,1)S(1)} %collective-permute-done.5.refs_6_), channel_id=1, source_target_pairs={{0,2},{1,31},{2,4},{3,1},{4,6},{5,3},{6,8},{7,5},{8,10},{9,7},{10,... | collective-permute-start | bytes 786440 | tf_op jit(solution)/shard_map/ppermute | solution.py:106
  41.4 4.7 %collective-permute-done.6.refs_0_ = bf16[32,4096]{1,0:T(8,128)(2,1)S(1)} collective-permute-done((bf16[32,4096]{1,0:T(8,128)(2,1)S(1)}, bf16[32,4096]{1,0:T(8,128)(2,1)S(1)}, u32[]{:S(2)}, u32[]{:S(2)}) %collective-permute-start.6) | collective-permute-done | bytes 262176 | tf_op jit(solution)/shard_map/ppermute | solution.py:105
  46.2 1.9 %collective-permute-start.8 = (bf16[32,4096]{1,0:T(8,128)(2,1)S(1)}, bf16[32,4096]{1,0:T(8,128)(2,1)S(1)}, u32[]{:S(2)}, u32[]{:S(2)}) collective-permute-start(bf16[32,4096]{1,0:T(8,128)(2,1)S(1)} %collective-permute-done.6.refs_0_), channel_id=1, source_target_pairs={{0,2},{1,31},{2,4},{3,1},{4,6},{5,3},{6,8},{7,5},{8,10},{9,7},{10,... | collective-permute-start | bytes 786440 | tf_op jit(solution)/shard_map/ppermute | solution.py:105
  48.1 0.9 collective-permute-done.7.refs_1_
  49.0 1.9 %collective-permute-start.9 = (bf16[32,4096]{1,0:T(8,128)(2,1)S(1)}, bf16[32,4096]{1,0:T(8,128)(2,1)S(1)}, u32[]{:S(2)}, u32[]{:S(2)}) collective-permute-start(bf16[32,4096]{1,0:T(8,128)(2,1)S(1)} %collective-permute-done.7.refs_1_), channel_id=1, source_target_pairs={{0,2},{1,31},{2,4},{3,1},{4,6},{5,3},{6,8},{7,5},{8,10},{9,7},{10,... | collective-permute-start | bytes 786440 | tf_op jit(solution)/shard_map/ppermute | solution.py:106
  50.9 4.7 %collective-permute-done.8.refs_2_ = bf16[32,4096]{1,0:T(8,128)(2,1)S(1)} collective-permute-done((bf16[32,4096]{1,0:T(8,128)(2,1)S(1)}, bf16[32,4096]{1,0:T(8,128)(2,1)S(1)}, u32[]{:S(2)}, u32[]{:S(2)}) %collective-permute-start.8) | collective-permute-done | bytes 262176 | tf_op jit(solution)/shard_map/ppermute | solution.py:105
  55.6 1.9 %collective-permute-start.10 = (bf16[32,4096]{1,0:T(8,128)(2,1)S(1)}, bf16[32,4096]{1,0:T(8,128)(2,1)S(1)}, u32[]{:S(2)}, u32[]{:S(2)}) collective-permute-start(bf16[32,4096]{1,0:T(8,128)(2,1)S(1)} %collective-permute-done.8.refs_2_), channel_id=1, source_target_pairs={{0,2},{1,31},{2,4},{3,1},{4,6},{5,3},{6,8},{7,5},{8,10},{9,7},{10,... | collective-permute-start | bytes 786440 | tf_op jit(solution)/shard_map/ppermute | solution.py:105
  57.5 0.9 collective-permute-done.9.refs_3_
  58.4 1.9 %collective-permute-start.11 = (bf16[32,4096]{1,0:T(8,128)(2,1)S(1)}, bf16[32,4096]{1,0:T(8,128)(2,1)S(1)}, u32[]{:S(2)}, u32[]{:S(2)}) collective-permute-start(bf16[32,4096]{1,0:T(8,128)(2,1)S(1)} %collective-permute-done.9.refs_3_), channel_id=1, source_target_pairs={{0,2},{1,31},{2,4},{3,1},{4,6},{5,3},{6,8},{7,5},{8,10},{9,7},{10,... | collective-permute-start | bytes 786440 | tf_op jit(solution)/shard_map/ppermute | solution.py:106
  60.3 3.1 %collective-permute-start.20 = (bf16[128,4096]{1,0:T(8,128)(2,1)}, bf16[128,4096]{1,0:T(8,128)(2,1)S(1)}, u32[]{:S(2)}, u32[]{:S(2)}) collective-permute-start(bf16[128,4096]{1,0:T(8,128)(2,1)} %bitcast.58), channel_id=1, source_target_pairs={{0,32},{32,0},{1,33},{33,1},{2,34},{34,2},{3,35},{35,3},{4,36},{36... | collective-permute-start | bytes 3145736 | tf_op jit(solution)/shard_map/ppermute | solution.py:109
  63.5 4.2 %collective-permute-start.19 = (bf16[128,4096]{1,0:T(8,128)(2,1)}, bf16[128,4096]{1,0:T(8,128)(2,1)S(1)}, u32[]{:S(2)}, u32[]{:S(2)}) collective-permute-start(bf16[128,4096]{1,0:T(8,128)(2,1)} %bitcast.60), channel_id=1, source_target_pairs={{0,32},{32,0},{1,33},{33,1},{2,34},{34,2},{3,35},{35,3},{4,36},{36... | collective-permute-start | bytes 3145736 | tf_op jit(solution)/shard_map/ppermute | solution.py:108
  67.7 0.1 stack.3
  67.8 1.9 %collective-permute-start.12 = (bf16[32,4096]{1,0:T(8,128)(2,1)S(1)}, bf16[32,4096]{1,0:T(8,128)(2,1)S(1)}, u32[]{:S(2)}, u32[]{:S(2)}) collective-permute-start(bf16[32,4096]{1,0:T(8,128)(2,1)S(1)} %collective-permute-done.10.refs_4_), channel_id=1, source_target_pairs={{0,2},{1,31},{2,4},{3,1},{4,6},{5,3},{6,8},{7,5},{8,10},{9,7},{10,... | collective-permute-start | bytes 786440 | tf_op jit(solution)/shard_map/ppermute | solution.py:105
  69.8 2.6 %collective-permute-start.13 = (bf16[32,4096]{1,0:T(8,128)(2,1)S(1)}, bf16[32,4096]{1,0:T(8,128)(2,1)S(1)}, u32[]{:S(2)}, u32[]{:S(2)}) collective-permute-start(bf16[32,4096]{1,0:T(8,128)(2,1)S(1)} %collective-permute-done.11.refs_5_), channel_id=1, source_target_pairs={{0,2},{1,31},{2,4},{3,1},{4,6},{5,3},{6,8},{7,5},{8,10},{9,7},{10,... | collective-permute-start | bytes 786440 | tf_op jit(solution)/shard_map/ppermute | solution.py:106
  72.4 0.2 fusion.17
  72.6 1.9 %collective-permute-start.16 = (bf16[2,112,4096]{2,1,0:T(8,128)(2,1)S(1)}, bf16[2,112,4096]{2,1,0:T(8,128)(2,1)S(1)}, u32[]{:S(2)}, u32[]{:S(2)}) collective-permute-start(bf16[2,112,4096]{2,1,0:T(8,128)(2,1)S(1)} %stack.3), channel_id=1, source_target_pairs={{0,1},{1,0},{2,3},{3,2},{4,5},{5,4},{6,7},{7,6},{8,9},{9,8},{10,11... | collective-permute-start | bytes 5505032 | tf_op jit(solution)/shard_map/ppermute | solution.py:111
  74.5 0.1 stack.4
  74.6 2.7 %collective-permute-done.12.refs_0_ = bf16[32,4096]{1,0:T(8,128)(2,1)S(1)} collective-permute-done((bf16[32,4096]{1,0:T(8,128)(2,1)S(1)}, bf16[32,4096]{1,0:T(8,128)(2,1)S(1)}, u32[]{:S(2)}, u32[]{:S(2)}) %collective-permute-start.12) | collective-permute-done | bytes 262176 | tf_op jit(solution)/shard_map/ppermute | solution.py:105
  77.3 0.7 collective-permute-start.14
  78.0 2.1 %collective-permute-done.13.refs_1_ = bf16[32,4096]{1,0:T(8,128)(2,1)S(1)} collective-permute-done((bf16[32,4096]{1,0:T(8,128)(2,1)S(1)}, bf16[32,4096]{1,0:T(8,128)(2,1)S(1)}, u32[]{:S(2)}, u32[]{:S(2)}) %collective-permute-start.13) | collective-permute-done | bytes 262176 | tf_op jit(solution)/shard_map/ppermute | solution.py:106
  80.1 0.7 collective-permute-start.15
  80.8 0.1 fusion.21
  81.0 4.1 %collective-permute-start.17 = (bf16[2,96,4096]{2,1,0:T(8,128)(2,1)S(1)}, bf16[2,96,4096]{2,1,0:T(8,128)(2,1)S(1)}, u32[]{:S(2)}, u32[]{:S(2)}) collective-permute-start(bf16[2,96,4096]{2,1,0:T(8,128)(2,1)S(1)} %stack.4), channel_id=1, source_target_pairs={{0,1},{1,0},{2,3},{3,2},{4,5},{5,4},{6,7},{7,6},{8,9},{9,8},{10,11... | collective-permute-start | bytes 4718600 | tf_op jit(solution)/shard_map/ppermute | solution.py:111
  85.2 3.6 %collective-permute-start.18 = (bf16[2,64,4096]{2,1,0:T(8,128)(2,1)S(1)}, bf16[2,64,4096]{2,1,0:T(8,128)(2,1)S(1)}, u32[]{:S(2)}, u32[]{:S(2)}) collective-permute-start(bf16[2,64,4096]{2,1,0:T(8,128)(2,1)S(1)} %stack.5), channel_id=1, source_target_pairs={{0,1},{1,0},{2,3},{3,2},{4,5},{5,4},{6,7},{7,6},{8,9},{9,8},{10,11... | collective-permute-start | bytes 3145736 | tf_op jit(solution)/shard_map/ppermute | solution.py:111
  88.7 0.1 fusion.25
  88.9 0.2 fusion.16
  89.1 0.1 fusion.20
  89.2 1.8 %collective-permute-done.18 = bf16[2,64,4096]{2,1,0:T(8,128)(2,1)S(1)} collective-permute-done((bf16[2,64,4096]{2,1,0:T(8,128)(2,1)S(1)}, bf16[2,64,4096]{2,1,0:T(8,128)(2,1)S(1)}, u32[]{:S(2)}, u32[]{:S(2)}) %collective-permute-start.18) | collective-permute-done | bytes 1048608 | tf_op jit(solution)/shard_map/ppermute | solution.py:111
  91.0 0.1 fusion.24
  91.1 1.3 %fusion.4 = f32[544,256]{1,0:T(8,128)S(1)} fusion(bf16[544,4096]{1,0:T(8,128)(2,1)S(1)} %get-tuple-element.14, bf16[128,4096]{1,0:T(8,128)(2,1)S(1)} %collective-permute-done.20, bf16[128,4096]{1,0:T(8,128)(2,1)S(1)} %bitcast.59), kind=kOutput, calls=%fused_computation.4 | convolution fusion | flops 1145044992 | bytes 7110656 | tf_op jit(solution)/shard_map/rd,cd->rc/dot_general | solution.py:118
  92.5 15.4 %collective-permute-done.19 = bf16[128,4096]{1,0:T(8,128)(2,1)S(1)} collective-permute-done((bf16[128,4096]{1,0:T(8,128)(2,1)}, bf16[128,4096]{1,0:T(8,128)(2,1)S(1)}, u32[]{:S(2)}, u32[]{:S(2)}) %collective-permute-start.19) | collective-permute-done | bytes 1048608 | tf_op jit(solution)/shard_map/ppermute | solution.py:108
  107.9 1.4 %fusion.11.terms = f32[544,256]{1,0:T(8,128)S(1)} fusion(f32[544,256]{1,0:T(8,128)S(1)} %fusion.4, bf16[544,4096]{1,0:T(8,128)(2,1)S(1)} %get-tuple-element.13, bf16[128,4096]{1,0:T(8,128)(2,1)S(1)} %collective-permute-done.19, bf16[128,4096]{1,0:T(8,128)(2,1)S(1)} %bitcast.61), kind=kOutput, calls=%fused_computation.9 | convolution fusion | flops 1145323520 | bytes 7667712 | tf_op jit(solution)/shard_map/rd,cd->rc/dot_general | solution.py:117
  109.3 0.1 order.1
  109.4 13.1 %all_to_all.5.got = f32[8,64,256]{2,1,0:T(8,128)S(1)} all-to-all(f32[8,64,256]{2,1,0:T(8,128)S(1)} %bitcast.55), channel_id=1, replica_groups=mesh['layer'=8,'trow'=2,'tcol'=32] {'layer'}, dimensions={0} | all-to-all | bytes 1048576 | tf_op jit(solution)/shard_map/all_to_all | solution.py:120
  122.5 0.7 layer_sum.1
  (13 shorter events, 0.1 us)
Async XLA Ops:
  1.0 16.8 %collective-permute-start = (bf16[32,4096]{1,0:T(8,128)(2,1)S(1)}, bf16[32,4096]{1,0:T(8,128)(2,1)S(1)}, u32[]{:S(2)}, u32[]{:S(2)}) collective-permute-start(bf16[32,4096]{1,0:T(8,128)(2,1)S(1)} %pad_maximum_fusion.refs_0_), channel_id=1, source_target_pairs={{0,2},{1,31},{2,4},{3,1},{4,6},{5,3},{6,8},{7,5},{8,10},{9,7},{10,... | collective-permute-start | bytes 786440 | tf_op jit(solution)/shard_map/ppermute | solution.py:102
  4.8 14.9 %collective-permute-start.1 = (bf16[32,4096]{1,0:T(8,128)(2,1)S(1)}, bf16[32,4096]{1,0:T(8,128)(2,1)S(1)}, u32[]{:S(2)}, u32[]{:S(2)}) collective-permute-start(bf16[32,4096]{1,0:T(8,128)(2,1)S(1)} %pad_maximum_fusion.refs_0_), channel_id=1, source_target_pairs={{0,31},{1,2},{2,1},{3,4},{4,3},{5,6},{6,5},{7,8},{8,7},{9,10},{10,... | collective-permute-start | bytes 786440 | tf_op jit(solution)/shard_map/ppermute | solution.py:102
  17.8 9.5 %collective-permute-start.2 = (bf16[32,4096]{1,0:T(8,128)(2,1)S(1)}, bf16[32,4096]{1,0:T(8,128)(2,1)S(1)}, u32[]{:S(2)}, u32[]{:S(2)}) collective-permute-start(bf16[32,4096]{1,0:T(8,128)(2,1)S(1)} %collective-permute-done.refs_1_), channel_id=1, source_target_pairs={{0,2},{1,31},{2,4},{3,1},{4,6},{5,3},{6,8},{7,5},{8,10},{9,7},{10,... | collective-permute-start | bytes 786440 | tf_op jit(solution)/shard_map/ppermute | solution.py:105
  19.7 10.3 %collective-permute-start.3 = (bf16[32,4096]{1,0:T(8,128)(2,1)S(1)}, bf16[32,4096]{1,0:T(8,128)(2,1)S(1)}, u32[]{:S(2)}, u32[]{:S(2)}) collective-permute-start(bf16[32,4096]{1,0:T(8,128)(2,1)S(1)} %collective-permute-done.1.refs_2_), channel_id=1, source_target_pairs={{0,2},{1,31},{2,4},{3,1},{4,6},{5,3},{6,8},{7,5},{8,10},{9,7},{10,... | collective-permute-start | bytes 786440 | tf_op jit(solution)/shard_map/ppermute | solution.py:106
  27.2 9.5 %collective-permute-start.4 = (bf16[32,4096]{1,0:T(8,128)(2,1)S(1)}, bf16[32,4096]{1,0:T(8,128)(2,1)S(1)}, u32[]{:S(2)}, u32[]{:S(2)}) collective-permute-start(bf16[32,4096]{1,0:T(8,128)(2,1)S(1)} %collective-permute-done.2.refs_3_), channel_id=1, source_target_pairs={{0,2},{1,31},{2,4},{3,1},{4,6},{5,3},{6,8},{7,5},{8,10},{9,7},{10,... | collective-permute-start | bytes 786440 | tf_op jit(solution)/shard_map/ppermute | solution.py:105
  30.0 9.5 %collective-permute-start.5 = (bf16[32,4096]{1,0:T(8,128)(2,1)S(1)}, bf16[32,4096]{1,0:T(8,128)(2,1)S(1)}, u32[]{:S(2)}, u32[]{:S(2)}) collective-permute-start(bf16[32,4096]{1,0:T(8,128)(2,1)S(1)} %collective-permute-done.3.refs_4_), channel_id=1, source_target_pairs={{0,2},{1,31},{2,4},{3,1},{4,6},{5,3},{6,8},{7,5},{8,10},{9,7},{10,... | collective-permute-start | bytes 786440 | tf_op jit(solution)/shard_map/ppermute | solution.py:106
  36.7 9.5 %collective-permute-start.6 = (bf16[32,4096]{1,0:T(8,128)(2,1)S(1)}, bf16[32,4096]{1,0:T(8,128)(2,1)S(1)}, u32[]{:S(2)}, u32[]{:S(2)}) collective-permute-start(bf16[32,4096]{1,0:T(8,128)(2,1)S(1)} %collective-permute-done.4.refs_5_), channel_id=1, source_target_pairs={{0,2},{1,31},{2,4},{3,1},{4,6},{5,3},{6,8},{7,5},{8,10},{9,7},{10,... | collective-permute-start | bytes 786440 | tf_op jit(solution)/shard_map/ppermute | solution.py:105
  39.5 9.5 %collective-permute-start.7 = (bf16[32,4096]{1,0:T(8,128)(2,1)S(1)}, bf16[32,4096]{1,0:T(8,128)(2,1)S(1)}, u32[]{:S(2)}, u32[]{:S(2)}) collective-permute-start(bf16[32,4096]{1,0:T(8,128)(2,1)S(1)} %collective-permute-done.5.refs_6_), channel_id=1, source_target_pairs={{0,2},{1,31},{2,4},{3,1},{4,6},{5,3},{6,8},{7,5},{8,10},{9,7},{10,... | collective-permute-start | bytes 786440 | tf_op jit(solution)/shard_map/ppermute | solution.py:106
  46.2 9.5 %collective-permute-start.8 = (bf16[32,4096]{1,0:T(8,128)(2,1)S(1)}, bf16[32,4096]{1,0:T(8,128)(2,1)S(1)}, u32[]{:S(2)}, u32[]{:S(2)}) collective-permute-start(bf16[32,4096]{1,0:T(8,128)(2,1)S(1)} %collective-permute-done.6.refs_0_), channel_id=1, source_target_pairs={{0,2},{1,31},{2,4},{3,1},{4,6},{5,3},{6,8},{7,5},{8,10},{9,7},{10,... | collective-permute-start | bytes 786440 | tf_op jit(solution)/shard_map/ppermute | solution.py:105
  49.0 9.5 %collective-permute-start.9 = (bf16[32,4096]{1,0:T(8,128)(2,1)S(1)}, bf16[32,4096]{1,0:T(8,128)(2,1)S(1)}, u32[]{:S(2)}, u32[]{:S(2)}) collective-permute-start(bf16[32,4096]{1,0:T(8,128)(2,1)S(1)} %collective-permute-done.7.refs_1_), channel_id=1, source_target_pairs={{0,2},{1,31},{2,4},{3,1},{4,6},{5,3},{6,8},{7,5},{8,10},{9,7},{10,... | collective-permute-start | bytes 786440 | tf_op jit(solution)/shard_map/ppermute | solution.py:106
  55.6 12.2 %collective-permute-start.10 = (bf16[32,4096]{1,0:T(8,128)(2,1)S(1)}, bf16[32,4096]{1,0:T(8,128)(2,1)S(1)}, u32[]{:S(2)}, u32[]{:S(2)}) collective-permute-start(bf16[32,4096]{1,0:T(8,128)(2,1)S(1)} %collective-permute-done.8.refs_2_), channel_id=1, source_target_pairs={{0,2},{1,31},{2,4},{3,1},{4,6},{5,3},{6,8},{7,5},{8,10},{9,7},{10,... | collective-permute-start | bytes 786440 | tf_op jit(solution)/shard_map/ppermute | solution.py:105
  58.4 11.4 %collective-permute-start.11 = (bf16[32,4096]{1,0:T(8,128)(2,1)S(1)}, bf16[32,4096]{1,0:T(8,128)(2,1)S(1)}, u32[]{:S(2)}, u32[]{:S(2)}) collective-permute-start(bf16[32,4096]{1,0:T(8,128)(2,1)S(1)} %collective-permute-done.9.refs_3_), channel_id=1, source_target_pairs={{0,2},{1,31},{2,4},{3,1},{4,6},{5,3},{6,8},{7,5},{8,10},{9,7},{10,... | collective-permute-start | bytes 786440 | tf_op jit(solution)/shard_map/ppermute | solution.py:106
  60.3 30.8 %collective-permute-start.20 = (bf16[128,4096]{1,0:T(8,128)(2,1)}, bf16[128,4096]{1,0:T(8,128)(2,1)S(1)}, u32[]{:S(2)}, u32[]{:S(2)}) collective-permute-start(bf16[128,4096]{1,0:T(8,128)(2,1)} %bitcast.58), channel_id=1, source_target_pairs={{0,32},{32,0},{1,33},{33,1},{2,34},{34,2},{3,35},{35,3},{4,36},{36... | collective-permute-start | bytes 3145736 | tf_op jit(solution)/shard_map/ppermute | solution.py:109
  63.5 44.4 %collective-permute-start.19 = (bf16[128,4096]{1,0:T(8,128)(2,1)}, bf16[128,4096]{1,0:T(8,128)(2,1)S(1)}, u32[]{:S(2)}, u32[]{:S(2)}) collective-permute-start(bf16[128,4096]{1,0:T(8,128)(2,1)} %bitcast.60), channel_id=1, source_target_pairs={{0,32},{32,0},{1,33},{33,1},{2,34},{34,2},{3,35},{35,3},{4,36},{36... | collective-permute-start | bytes 3145736 | tf_op jit(solution)/shard_map/ppermute | solution.py:108
  67.8 9.5 %collective-permute-start.12 = (bf16[32,4096]{1,0:T(8,128)(2,1)S(1)}, bf16[32,4096]{1,0:T(8,128)(2,1)S(1)}, u32[]{:S(2)}, u32[]{:S(2)}) collective-permute-start(bf16[32,4096]{1,0:T(8,128)(2,1)S(1)} %collective-permute-done.10.refs_4_), channel_id=1, source_target_pairs={{0,2},{1,31},{2,4},{3,1},{4,6},{5,3},{6,8},{7,5},{8,10},{9,7},{10,... | collective-permute-start | bytes 786440 | tf_op jit(solution)/shard_map/ppermute | solution.py:105
  69.8 10.3 %collective-permute-start.13 = (bf16[32,4096]{1,0:T(8,128)(2,1)S(1)}, bf16[32,4096]{1,0:T(8,128)(2,1)S(1)}, u32[]{:S(2)}, u32[]{:S(2)}) collective-permute-start(bf16[32,4096]{1,0:T(8,128)(2,1)S(1)} %collective-permute-done.11.refs_5_), channel_id=1, source_target_pairs={{0,2},{1,31},{2,4},{3,1},{4,6},{5,3},{6,8},{7,5},{8,10},{9,7},{10,... | collective-permute-start | bytes 786440 | tf_op jit(solution)/shard_map/ppermute | solution.py:106
  72.6 16.3 %collective-permute-start.16 = (bf16[2,112,4096]{2,1,0:T(8,128)(2,1)S(1)}, bf16[2,112,4096]{2,1,0:T(8,128)(2,1)S(1)}, u32[]{:S(2)}, u32[]{:S(2)}) collective-permute-start(bf16[2,112,4096]{2,1,0:T(8,128)(2,1)S(1)} %stack.3), channel_id=1, source_target_pairs={{0,1},{1,0},{2,3},{3,2},{4,5},{5,4},{6,7},{7,6},{8,9},{9,8},{10,11... | collective-permute-start | bytes 5505032 | tf_op jit(solution)/shard_map/ppermute | solution.py:111
  77.3 3.6 %collective-permute-start.14 = (bf16[32,4096]{1,0:T(8,128)(2,1)S(1)}, bf16[32,4096]{1,0:T(8,128)(2,1)S(1)}, u32[]{:S(2)}, u32[]{:S(2)}) collective-permute-start(bf16[32,4096]{1,0:T(8,128)(2,1)S(1)} %collective-permute-done.12.refs_0_), channel_id=1, source_target_pairs={{1,31},{3,1},{5,3},{7,5},{9,7},{11,9},{13,11},{15,13},{17,15},{19,... | collective-permute-start | bytes 786440 | tf_op jit(solution)/shard_map/ppermute | solution.py:105
  80.1 4.9 %collective-permute-start.15 = (bf16[32,4096]{1,0:T(8,128)(2,1)S(1)}, bf16[32,4096]{1,0:T(8,128)(2,1)S(1)}, u32[]{:S(2)}, u32[]{:S(2)}) collective-permute-start(bf16[32,4096]{1,0:T(8,128)(2,1)S(1)} %collective-permute-done.13.refs_1_), channel_id=1, source_target_pairs={{1,31},{3,1},{5,3},{7,5},{9,7},{11,9},{13,11},{15,13},{17,15},{19,... | collective-permute-start | bytes 786440 | tf_op jit(solution)/shard_map/ppermute | solution.py:106
  81.0 8.1 %collective-permute-start.17 = (bf16[2,96,4096]{2,1,0:T(8,128)(2,1)S(1)}, bf16[2,96,4096]{2,1,0:T(8,128)(2,1)S(1)}, u32[]{:S(2)}, u32[]{:S(2)}) collective-permute-start(bf16[2,96,4096]{2,1,0:T(8,128)(2,1)S(1)} %stack.4), channel_id=1, source_target_pairs={{0,1},{1,0},{2,3},{3,2},{4,5},{5,4},{6,7},{7,6},{8,9},{9,8},{10,11... | collective-permute-start | bytes 4718600 | tf_op jit(solution)/shard_map/ppermute | solution.py:111
  85.2 5.8 %collective-permute-start.18 = (bf16[2,64,4096]{2,1,0:T(8,128)(2,1)S(1)}, bf16[2,64,4096]{2,1,0:T(8,128)(2,1)S(1)}, u32[]{:S(2)}, u32[]{:S(2)}) collective-permute-start(bf16[2,64,4096]{2,1,0:T(8,128)(2,1)S(1)} %stack.5), channel_id=1, source_target_pairs={{0,1},{1,0},{2,3},{3,2},{4,5},{5,4},{6,7},{7,6},{8,9},{9,8},{10,11... | collective-permute-start | bytes 3145736 | tf_op jit(solution)/shard_map/ppermute | solution.py:111
  88.8 2.3 %copy-start = (bf16[1,128,4096]{2,1,0:T(8,128)(2,1)S(1)}, bf16[1,128,4096]{2,1,0:T(8,128)(2,1)}, u32[]{:S(2)}) copy-start(bf16[1,128,4096]{2,1,0:T(8,128)(2,1)} %param.7) | copy-start | bytes 3145732
  91.1 16.8 %copy-start.1 = (bf16[1,128,4096]{2,1,0:T(8,128)(2,1)S(1)}, bf16[1,128,4096]{2,1,0:T(8,128)(2,1)}, u32[]{:S(2)}) copy-start(bf16[1,128,4096]{2,1,0:T(8,128)(2,1)} %param.6) | copy-start | bytes 3145732

commit v4 on v3

--- a/solution.py
+++ b/solution.py
@@ -13,7 +13,8 @@
 GROUPS = (
     ((0, 0), (0, 1), (1, 1), (0, 2), (1, 2), (0, 3), (1, 3)),
     ((0, 4), (1, 4), (0, 5), (1, 5), (0, 6), (1, 6)),
-    ((0, 7), (1, 7), (0, 8), (1, 8)),
+    ((0, 7), (1, 7)),
+    ((0, 8),),
 )
 
 
@@ -42,20 +43,17 @@
     tcol = lax.axis_index("tcol")
     z, core = lax.shift_right_logical(tcol, 1), lax.rem(tcol, 2)
     planes = out.shape[0] // (2 * height)
-    sign = 1 - 2 * core
+    sign = 1 - 2 * lax.rem(z + core, 2)
     shards = [shard for group in GROUPS for shard in group]
 
     def put(source, plane, on):
         at = pl.multiple_of((lax.rem(plane + planes, planes) * 2 + on) * height, height)
-        out[pl.ds(at, height), :] = terms[pl.ds(source, height), :]
+        out[pl.ds(at, height), :] = terms[source : source + height, :]
 
     for i, (stream, step) in enumerate(shards):
-        mine_at, given_at = i * height, (len(shards) + i) * height
-        if step == planes // 2:
-            put(pl.multiple_of(jnp.where(core == 1, mine_at, given_at), height), z + step, 1 - stream)
-        else:
-            put(mine_at, z - sign * step, core if stream == 0 else 1 - core)
-            put(given_at, z + sign * step, 1 - core if stream == 0 else core)
+        on = core if (stream + step) % 2 == 0 else 1 - core
+        put(i * height, z - sign * step, on)
+        put((len(shards) + i) * height, z + sign * step, 1 - on)
 
 
 def in_order(terms, height, planes):
@@ -94,21 +92,28 @@
     half = planes // 2
     depth = act_rows.shape[2]
 
-    along = [(2 * p + c, 2 * ((p + (1, -1)[c]) % planes) + c) for p in range(planes) for c in range(2)]
-    aslant = [(2 * p + c, 2 * ((p + (-1, 1)[c]) % planes) + 1 - c) for p in range(planes) for c in range(2)]
+    along, aslant = [], []
+    for p in range(planes):
+        for c in range(2):
+            step = 1 - 2 * ((p + c) % 2)
+            along.append((2 * p + c, 2 * ((p + step) % planes) + 1 - c))
+            aslant.append((2 * p + c, 2 * ((p - step) % planes) + c))
     cores = [(t, t ^ 1) for t in range(tcols)]
 
+    def moved(value, axis, pairs):
+        return lax.ppermute(value, axis, pairs)
+
     own = jnp.concatenate((act_rows[0], back_rows[0]), axis=0)
-    held = {(0, 0): own, (0, 1): lax.ppermute(own, "tcol", along), (1, 1): lax.ppermute(own, "tcol", aslant)}
+    held = {(0, 0): own, (0, 1): moved(own, "tcol", along), (1, 1): moved(own, "tcol", aslant)}
     for step in range(2, half + 1):
-        pairs = along if step < half else [(a, b) for a, b in along if a % 2 == 1]
-        held[0, step] = lax.ppermute(held[0, step - 1], "tcol", pairs)
-        held[1, step] = lax.ppermute(held[1, step - 1], "tcol", pairs)
+        held[0, step] = moved(held[0, step - 1], "tcol", along)
+        if step < half:
+            held[1, step] = moved(held[1, step - 1], "tcol", along)
     across = [(0, 1), (1, 0)]
-    other_act = lax.ppermute(act_cols[0], "trow", across)
-    other_back = lax.ppermute(back_cols[0], "trow", across)
+    other_act = moved(act_cols[0], "trow", across)
+    other_back = moved(back_cols[0], "trow", across)
     mine = [stack([held[shard] for shard in group]) for group in GROUPS]
-    given = [lax.ppermute(rows, "tcol", cores) for rows in mine]
+    given = [moved(rows, "tcol", cores) for rows in mine]
 
     act = jnp.concatenate([rows[0] for rows in mine + given], axis=0)
     back = jnp.concatenate([rows[1] for rows in mine + given], axis=0)

time: 124 us -> 117 us (0.944)
  the two profiles are of different devices: /device:TPU:24 before, /device:TPU:1 now
where the time goes in v4:
time: 117 us
  starting transfers between devices  78.5 us (67%)
  waiting for transfers between devices  18.3 us (16%)
  blocking collectives  13.9 us (12%)
  matrix products  2.58 us (2%)
    ppermute x21, starting transfers between devices, moved(): return lax.ppermute(value, axis, pairs)  78.5 us
    ppermute x21, waiting for transfers between devices, moved(): return lax.ppermute(value, axis, pairs)  18.3 us
    all_to_all x1, blocking collectives, local(): lax.all_to_all(terms.reshape(layers, -1, terms.shape[-1]), 'layer', 0, 0,...  13.9 us
  transfers between devices with their start and end apart: 21, of which 10 were waited for; matrix products, arithmetic and copies ran while one was open for 2% of the time, Pallas kernels for 0%

profile of v4, /device:TPU:1, one launch (start us, length us, event | category | flops | bytes accessed | tf_op | source)
XLA Modules:
  0.0 116.6 jit_solution(11835939167367111933)
XLA Ops:
  0.0 1.0 pad_maximum_fusion.refs_0_
  1.0 12.5 %collective-permute-start = (bf16[32,4096]{1,0:T(8,128)(2,1)S(1)}, bf16[32,4096]{1,0:T(8,128)(2,1)S(1)}, u32[]{:S(2)}, u32[]{:S(2)}) collective-permute-start(bf16[32,4096]{1,0:T(8,128)(2,1)S(1)} %pad_maximum_fusion.refs_0_), channel_id=1, source_target_pairs={{0,3},{1,30},{2,1},{3,4},{4,7},{5,2},{6,5},{7,8},{8,11},{9,6},{10,... | collective-permute-start | bytes 786440 | tf_op jit(solution)/shard_map/ppermute | solution.py:104
  13.5 1.9 %collective-permute-start.1 = (bf16[32,4096]{1,0:T(8,128)(2,1)S(1)}, bf16[32,4096]{1,0:T(8,128)(2,1)S(1)}, u32[]{:S(2)}, u32[]{:S(2)}) collective-permute-start(bf16[32,4096]{1,0:T(8,128)(2,1)S(1)} %pad_maximum_fusion.refs_0_), channel_id=1, source_target_pairs={{0,30},{1,3},{2,4},{3,1},{4,2},{5,7},{6,8},{7,5},{8,6},{9,11},{10,... | collective-permute-start | bytes 786440 | tf_op jit(solution)/shard_map/ppermute | solution.py:104
  15.4 1.4 %collective-permute-done.refs_1_ = bf16[32,4096]{1,0:T(8,128)(2,1)S(1)} collective-permute-done((bf16[32,4096]{1,0:T(8,128)(2,1)S(1)}, bf16[32,4096]{1,0:T(8,128)(2,1)S(1)}, u32[]{:S(2)}, u32[]{:S(2)}) %collective-permute-start) | collective-permute-done | bytes 262176 | tf_op jit(solution)/shard_map/ppermute | solution.py:104
  16.8 5.6 %collective-permute-start.2 = (bf16[32,4096]{1,0:T(8,128)(2,1)S(1)}, bf16[32,4096]{1,0:T(8,128)(2,1)S(1)}, u32[]{:S(2)}, u32[]{:S(2)}) collective-permute-start(bf16[32,4096]{1,0:T(8,128)(2,1)S(1)} %collective-permute-done.refs_1_), channel_id=1, source_target_pairs={{0,3},{1,30},{2,1},{3,4},{4,7},{5,2},{6,5},{7,8},{8,11},{9,6},{10,... | collective-permute-start | bytes 786440 | tf_op jit(solution)/shard_map/ppermute | solution.py:104
  22.4 2.9 %collective-permute-start.3 = (bf16[32,4096]{1,0:T(8,128)(2,1)S(1)}, bf16[32,4096]{1,0:T(8,128)(2,1)S(1)}, u32[]{:S(2)}, u32[]{:S(2)}) collective-permute-start(bf16[32,4096]{1,0:T(8,128)(2,1)S(1)} %collective-permute-done.1.refs_2_), channel_id=1, source_target_pairs={{0,3},{1,30},{2,1},{3,4},{4,7},{5,2},{6,5},{7,8},{8,11},{9,6},{10,... | collective-permute-start | bytes 786440 | tf_op jit(solution)/shard_map/ppermute | solution.py:104
  25.3 0.4 collective-permute-done.2.refs_3_
  25.7 5.6 %collective-permute-start.4 = (bf16[32,4096]{1,0:T(8,128)(2,1)S(1)}, bf16[32,4096]{1,0:T(8,128)(2,1)S(1)}, u32[]{:S(2)}, u32[]{:S(2)}) collective-permute-start(bf16[32,4096]{1,0:T(8,128)(2,1)S(1)} %collective-permute-done.2.refs_3_), channel_id=1, source_target_pairs={{0,3},{1,30},{2,1},{3,4},{4,7},{5,2},{6,5},{7,8},{8,11},{9,6},{10,... | collective-permute-start | bytes 786440 | tf_op jit(solution)/shard_map/ppermute | solution.py:104
  31.3 0.0 collective-permute-done.3.refs_4_
  31.3 2.9 %collective-permute-start.5 = (bf16[32,4096]{1,0:T(8,128)(2,1)S(1)}, bf16[32,4096]{1,0:T(8,128)(2,1)S(1)}, u32[]{:S(2)}, u32[]{:S(2)}) collective-permute-start(bf16[32,4096]{1,0:T(8,128)(2,1)S(1)} %collective-permute-done.3.refs_4_), channel_id=1, source_target_pairs={{0,3},{1,30},{2,1},{3,4},{4,7},{5,2},{6,5},{7,8},{8,11},{9,6},{10,... | collective-permute-start | bytes 786440 | tf_op jit(solution)/shard_map/ppermute | solution.py:104
  34.2 0.4 collective-permute-done.4.refs_5_
  34.6 5.6 %collective-permute-start.6 = (bf16[32,4096]{1,0:T(8,128)(2,1)S(1)}, bf16[32,4096]{1,0:T(8,128)(2,1)S(1)}, u32[]{:S(2)}, u32[]{:S(2)}) collective-permute-start(bf16[32,4096]{1,0:T(8,128)(2,1)S(1)} %collective-permute-done.4.refs_5_), channel_id=1, source_target_pairs={{0,3},{1,30},{2,1},{3,4},{4,7},{5,2},{6,5},{7,8},{8,11},{9,6},{10,... | collective-permute-start | bytes 786440 | tf_op jit(solution)/shard_map/ppermute | solution.py:104
  40.2 0.0 collective-permute-done.5.refs_6_
  40.2 2.9 %collective-permute-start.7 = (bf16[32,4096]{1,0:T(8,128)(2,1)S(1)}, bf16[32,4096]{1,0:T(8,128)(2,1)S(1)}, u32[]{:S(2)}, u32[]{:S(2)}) collective-permute-start(bf16[32,4096]{1,0:T(8,128)(2,1)S(1)} %collective-permute-done.5.refs_6_), channel_id=1, source_target_pairs={{0,3},{1,30},{2,1},{3,4},{4,7},{5,2},{6,5},{7,8},{8,11},{9,6},{10,... | collective-permute-start | bytes 786440 | tf_op jit(solution)/shard_map/ppermute | solution.py:104
  43.1 0.4 collective-permute-done.6.refs_0_
  43.5 5.6 %collective-permute-start.8 = (bf16[32,4096]{1,0:T(8,128)(2,1)S(1)}, bf16[32,4096]{1,0:T(8,128)(2,1)S(1)}, u32[]{:S(2)}, u32[]{:S(2)}) collective-permute-start(bf16[32,4096]{1,0:T(8,128)(2,1)S(1)} %collective-permute-done.6.refs_0_), channel_id=1, source_target_pairs={{0,3},{1,30},{2,1},{3,4},{4,7},{5,2},{6,5},{7,8},{8,11},{9,6},{10,... | collective-permute-start | bytes 786440 | tf_op jit(solution)/shard_map/ppermute | solution.py:104
  49.1 2.9 %collective-permute-start.9 = (bf16[32,4096]{1,0:T(8,128)(2,1)S(1)}, bf16[32,4096]{1,0:T(8,128)(2,1)S(1)}, u32[]{:S(2)}, u32[]{:S(2)}) collective-permute-start(bf16[32,4096]{1,0:T(8,128)(2,1)S(1)} %collective-permute-done.7.refs_1_), channel_id=1, source_target_pairs={{0,3},{1,30},{2,1},{3,4},{4,7},{5,2},{6,5},{7,8},{8,11},{9,6},{10,... | collective-permute-start | bytes 786440 | tf_op jit(solution)/shard_map/ppermute | solution.py:104
  52.0 4.8 %collective-permute-start.20 = (bf16[128,4096]{1,0:T(8,128)(2,1)}, bf16[128,4096]{1,0:T(8,128)(2,1)S(1)}, u32[]{:S(2)}, u32[]{:S(2)}) collective-permute-start(bf16[128,4096]{1,0:T(8,128)(2,1)} %bitcast.74), channel_id=1, source_target_pairs={{0,32},{32,0},{1,33},{33,1},{2,34},{34,2},{3,35},{35,3},{4,36},{36... | collective-permute-start | bytes 3145736 | tf_op jit(solution)/shard_map/ppermute | solution.py:104
  56.8 2.0 %collective-permute-start.19 = (bf16[128,4096]{1,0:T(8,128)(2,1)}, bf16[128,4096]{1,0:T(8,128)(2,1)S(1)}, u32[]{:S(2)}, u32[]{:S(2)}) collective-permute-start(bf16[128,4096]{1,0:T(8,128)(2,1)} %bitcast.76), channel_id=1, source_target_pairs={{0,32},{32,0},{1,33},{33,1},{2,34},{34,2},{3,35},{35,3},{4,36},{36... | collective-permute-start | bytes 3145736 | tf_op jit(solution)/shard_map/ppermute | solution.py:104
  58.8 0.1 stack.4
  58.9 0.0 collective-permute-done.8.refs_2_
  58.9 2.5 %collective-permute-start.10 = (bf16[32,4096]{1,0:T(8,128)(2,1)S(1)}, bf16[32,4096]{1,0:T(8,128)(2,1)S(1)}, u32[]{:S(2)}, u32[]{:S(2)}) collective-permute-start(bf16[32,4096]{1,0:T(8,128)(2,1)S(1)} %collective-permute-done.8.refs_2_), channel_id=1, source_target_pairs={{0,3},{1,30},{2,1},{3,4},{4,7},{5,2},{6,5},{7,8},{8,11},{9,6},{10,... | collective-permute-start | bytes 786440 | tf_op jit(solution)/shard_map/ppermute | solution.py:104
  61.4 1.9 %collective-permute-start.11 = (bf16[32,4096]{1,0:T(8,128)(2,1)S(1)}, bf16[32,4096]{1,0:T(8,128)(2,1)S(1)}, u32[]{:S(2)}, u32[]{:S(2)}) collective-permute-start(bf16[32,4096]{1,0:T(8,128)(2,1)S(1)} %collective-permute-done.9.refs_3_), channel_id=1, source_target_pairs={{0,3},{1,30},{2,1},{3,4},{4,7},{5,2},{6,5},{7,8},{8,11},{9,6},{10,... | collective-permute-start | bytes 786440 | tf_op jit(solution)/shard_map/ppermute | solution.py:104
  63.4 0.2 fusion.17
  63.6 1.9 %collective-permute-start.15 = (bf16[2,112,4096]{2,1,0:T(8,128)(2,1)S(1)}, bf16[2,112,4096]{2,1,0:T(8,128)(2,1)S(1)}, u32[]{:S(2)}, u32[]{:S(2)}) collective-permute-start(bf16[2,112,4096]{2,1,0:T(8,128)(2,1)S(1)} %stack.4), channel_id=1, source_target_pairs={{0,1},{1,0},{2,3},{3,2},{4,5},{5,4},{6,7},{7,6},{8,9},{9,8},{10,11... | collective-permute-start | bytes 5505032 | tf_op jit(solution)/shard_map/ppermute | solution.py:104
  65.5 1.4 %collective-permute-done.10.refs_4_ = bf16[32,4096]{1,0:T(8,128)(2,1)S(1)} collective-permute-done((bf16[32,4096]{1,0:T(8,128)(2,1)S(1)}, bf16[32,4096]{1,0:T(8,128)(2,1)S(1)}, u32[]{:S(2)}, u32[]{:S(2)}) %collective-permute-start.10) | collective-permute-done | bytes 262176 | tf_op jit(solution)/shard_map/ppermute | solution.py:104
  66.9 4.1 %collective-permute-start.12 = (bf16[32,4096]{1,0:T(8,128)(2,1)S(1)}, bf16[32,4096]{1,0:T(8,128)(2,1)S(1)}, u32[]{:S(2)}, u32[]{:S(2)}) collective-permute-start(bf16[32,4096]{1,0:T(8,128)(2,1)S(1)} %collective-permute-done.10.refs_4_), channel_id=1, source_target_pairs={{0,3},{1,30},{2,1},{3,4},{4,7},{5,2},{6,5},{7,8},{8,11},{9,6},{10,... | collective-permute-start | bytes 786440 | tf_op jit(solution)/shard_map/ppermute | solution.py:104
  71.1 0.1 stack.5
  71.2 2.4 %collective-permute-start.13 = (bf16[32,4096]{1,0:T(8,128)(2,1)S(1)}, bf16[32,4096]{1,0:T(8,128)(2,1)S(1)}, u32[]{:S(2)}, u32[]{:S(2)}) collective-permute-start(bf16[32,4096]{1,0:T(8,128)(2,1)S(1)} %collective-permute-done.11.refs_5_), channel_id=1, source_target_pairs={{0,3},{1,30},{2,1},{3,4},{4,7},{5,2},{6,5},{7,8},{8,11},{9,6},{10,... | collective-permute-start | bytes 786440 | tf_op jit(solution)/shard_map/ppermute | solution.py:104
  73.6 0.1 fusion.21
  73.7 1.2 %collective-permute-done.12.refs_0_ = bf16[32,4096]{1,0:T(8,128)(2,1)S(1)} collective-permute-done((bf16[32,4096]{1,0:T(8,128)(2,1)S(1)}, bf16[32,4096]{1,0:T(8,128)(2,1)S(1)}, u32[]{:S(2)}, u32[]{:S(2)}) %collective-permute-start.12) | collective-permute-done | bytes 262176 | tf_op jit(solution)/shard_map/ppermute | solution.py:104
  74.9 2.6 %collective-permute-start.16 = (bf16[2,96,4096]{2,1,0:T(8,128)(2,1)S(1)}, bf16[2,96,4096]{2,1,0:T(8,128)(2,1)S(1)}, u32[]{:S(2)}, u32[]{:S(2)}) collective-permute-start(bf16[2,96,4096]{2,1,0:T(8,128)(2,1)S(1)} %stack.5), channel_id=1, source_target_pairs={{0,1},{1,0},{2,3},{3,2},{4,5},{5,4},{6,7},{7,6},{8,9},{9,8},{10,11... | collective-permute-start | bytes 4718600 | tf_op jit(solution)/shard_map/ppermute | solution.py:104
  77.5 1.7 %collective-permute-done.13.refs_1_ = bf16[32,4096]{1,0:T(8,128)(2,1)S(1)} collective-permute-done((bf16[32,4096]{1,0:T(8,128)(2,1)S(1)}, bf16[32,4096]{1,0:T(8,128)(2,1)S(1)}, u32[]{:S(2)}, u32[]{:S(2)}) %collective-permute-start.13) | collective-permute-done | bytes 262176 | tf_op jit(solution)/shard_map/ppermute | solution.py:104
  79.2 3.6 %collective-permute-start.14 = (bf16[32,4096]{1,0:T(8,128)(2,1)S(1)}, bf16[32,4096]{1,0:T(8,128)(2,1)S(1)}, u32[]{:S(2)}, u32[]{:S(2)}) collective-permute-start(bf16[32,4096]{1,0:T(8,128)(2,1)S(1)} %collective-permute-done.12.refs_0_), channel_id=1, source_target_pairs={{0,3},{1,30},{2,1},{3,4},{4,7},{5,2},{6,5},{7,8},{8,11},{9,6},{10,... | collective-permute-start | bytes 786440 | tf_op jit(solution)/shard_map/ppermute | solution.py:104
  82.9 4.3 %collective-permute-done.14.refs_0_ = bf16[32,4096]{1,0:T(8,128)(2,1)S(1)} collective-permute-done((bf16[32,4096]{1,0:T(8,128)(2,1)S(1)}, bf16[32,4096]{1,0:T(8,128)(2,1)S(1)}, u32[]{:S(2)}, u32[]{:S(2)}) %collective-permute-start.14) | collective-permute-done | bytes 262176 | tf_op jit(solution)/shard_map/ppermute | solution.py:104
  87.2 2.3 %collective-permute-start.17 = (bf16[2,32,4096]{2,1,0:T(8,128)(2,1)S(1)}, bf16[2,32,4096]{2,1,0:T(8,128)(2,1)S(1)}, u32[]{:S(2)}, u32[]{:S(2)}) collective-permute-start(bf16[2,32,4096]{2,1,0:T(8,128)(2,1)S(1)} %stack.6), channel_id=1, source_target_pairs={{0,1},{1,0},{2,3},{3,2},{4,5},{5,4},{6,7},{7,6},{8,9},{9,8},{10,11... | collective-permute-start | bytes 1572872 | tf_op jit(solution)/shard_map/ppermute | solution.py:104
  89.5 2.0 %collective-permute-start.18 = (bf16[2,16,4096]{2,1,0:T(8,128)(2,1)S(1)}, bf16[2,16,4096]{2,1,0:T(8,128)(2,1)S(1)}, u32[]{:S(2)}, u32[]{:S(2)}) collective-permute-start(bf16[2,16,4096]{2,1,0:T(8,128)(2,1)S(1)} %stack.7), channel_id=1, source_target_pairs={{0,1},{1,0},{2,3},{3,2},{4,5},{5,4},{6,7},{7,6},{8,9},{9,8},{10,11... | collective-permute-start | bytes 786440 | tf_op jit(solution)/shard_map/ppermute | solution.py:104
  91.5 0.0 copy-start
  91.6 0.2 fusion.16
  91.8 0.1 fusion.20
  92.0 1.0 collective-permute-done.18
  93.0 0.0 copy-start.1
  93.0 1.3 %fusion.4 = f32[512,256]{1,0:T(8,128)S(1)} fusion(bf16[512,4096]{1,0:T(8,128)(2,1)S(1)} %get-tuple-element.18, bf16[128,4096]{1,0:T(8,128)(2,1)S(1)} %collective-permute-done.20, bf16[128,4096]{1,0:T(8,128)(2,1)S(1)} %bitcast.75), kind=kOutput, calls=%fused_computation.4 | convolution fusion | flops 1077936128 | bytes 6815744 | tf_op jit(solution)/shard_map/rd,cd->rc/dot_general | solution.py:123
  94.3 6.3 %collective-permute-done.19 = bf16[128,4096]{1,0:T(8,128)(2,1)S(1)} collective-permute-done((bf16[128,4096]{1,0:T(8,128)(2,1)}, bf16[128,4096]{1,0:T(8,128)(2,1)S(1)}, u32[]{:S(2)}, u32[]{:S(2)}) %collective-permute-start.19) | collective-permute-done | bytes 1048608 | tf_op jit(solution)/shard_map/ppermute | solution.py:104
  100.6 1.3 %fusion.11.terms = f32[512,256]{1,0:T(8,128)S(1)} fusion(f32[512,256]{1,0:T(8,128)S(1)} %fusion.4, bf16[512,4096]{1,0:T(8,128)(2,1)S(1)} %get-tuple-element.17, bf16[128,4096]{1,0:T(8,128)(2,1)S(1)} %collective-permute-done.19, bf16[128,4096]{1,0:T(8,128)(2,1)S(1)} %bitcast.77), kind=kOutput, calls=%fused_computation.9 | convolution fusion | flops 1078198272 | bytes 7340032 | tf_op jit(solution)/shard_map/rd,cd->rc/dot_general | solution.py:122
  101.9 0.1 order.1
  102.0 13.9 %all_to_all.5.got = f32[8,64,256]{2,1,0:T(8,128)S(1)} all-to-all(f32[8,64,256]{2,1,0:T(8,128)S(1)} %bitcast.71), channel_id=1, replica_groups=mesh['layer'=8,'trow'=2,'tcol'=32] {'layer'}, dimensions={0} | all-to-all | bytes 1048576 | tf_op jit(solution)/shard_map/all_to_all | solution.py:125
  115.9 0.7 layer_sum.1
  (16 shorter events, 0.2 us)
Async XLA Ops:
  1.0 15.8 %collective-permute-start = (bf16[32,4096]{1,0:T(8,128)(2,1)S(1)}, bf16[32,4096]{1,0:T(8,128)(2,1)S(1)}, u32[]{:S(2)}, u32[]{:S(2)}) collective-permute-start(bf16[32,4096]{1,0:T(8,128)(2,1)S(1)} %pad_maximum_fusion.refs_0_), channel_id=1, source_target_pairs={{0,3},{1,30},{2,1},{3,4},{4,7},{5,2},{6,5},{7,8},{8,11},{9,6},{10,... | collective-permute-start | bytes 786440 | tf_op jit(solution)/shard_map/ppermute | solution.py:104
  13.5 8.9 %collective-permute-start.1 = (bf16[32,4096]{1,0:T(8,128)(2,1)S(1)}, bf16[32,4096]{1,0:T(8,128)(2,1)S(1)}, u32[]{:S(2)}, u32[]{:S(2)}) collective-permute-start(bf16[32,4096]{1,0:T(8,128)(2,1)S(1)} %pad_maximum_fusion.refs_0_), channel_id=1, source_target_pairs={{0,30},{1,3},{2,4},{3,1},{4,2},{5,7},{6,8},{7,5},{8,6},{9,11},{10,... | collective-permute-start | bytes 786440 | tf_op jit(solution)/shard_map/ppermute | solution.py:104
  16.8 8.9 %collective-permute-start.2 = (bf16[32,4096]{1,0:T(8,128)(2,1)S(1)}, bf16[32,4096]{1,0:T(8,128)(2,1)S(1)}, u32[]{:S(2)}, u32[]{:S(2)}) collective-permute-start(bf16[32,4096]{1,0:T(8,128)(2,1)S(1)} %collective-permute-done.refs_1_), channel_id=1, source_target_pairs={{0,3},{1,30},{2,1},{3,4},{4,7},{5,2},{6,5},{7,8},{8,11},{9,6},{10,... | collective-permute-start | bytes 786440 | tf_op jit(solution)/shard_map/ppermute | solution.py:104
  22.4 8.9 %collective-permute-start.3 = (bf16[32,4096]{1,0:T(8,128)(2,1)S(1)}, bf16[32,4096]{1,0:T(8,128)(2,1)S(1)}, u32[]{:S(2)}, u32[]{:S(2)}) collective-permute-start(bf16[32,4096]{1,0:T(8,128)(2,1)S(1)} %collective-permute-done.1.refs_2_), channel_id=1, source_target_pairs={{0,3},{1,30},{2,1},{3,4},{4,7},{5,2},{6,5},{7,8},{8,11},{9,6},{10,... | collective-permute-start | bytes 786440 | tf_op jit(solution)/shard_map/ppermute | solution.py:104
  25.7 8.9 %collective-permute-start.4 = (bf16[32,4096]{1,0:T(8,128)(2,1)S(1)}, bf16[32,4096]{1,0:T(8,128)(2,1)S(1)}, u32[]{:S(2)}, u32[]{:S(2)}) collective-permute-start(bf16[32,4096]{1,0:T(8,128)(2,1)S(1)} %collective-permute-done.2.refs_3_), channel_id=1, source_target_pairs={{0,3},{1,30},{2,1},{3,4},{4,7},{5,2},{6,5},{7,8},{8,11},{9,6},{10,... | collective-permute-start | bytes 786440 | tf_op jit(solution)/shard_map/ppermute | solution.py:104
  31.3 8.9 %collective-permute-start.5 = (bf16[32,4096]{1,0:T(8,128)(2,1)S(1)}, bf16[32,4096]{1,0:T(8,128)(2,1)S(1)}, u32[]{:S(2)}, u32[]{:S(2)}) collective-permute-start(bf16[32,4096]{1,0:T(8,128)(2,1)S(1)} %collective-permute-done.3.refs_4_), channel_id=1, source_target_pairs={{0,3},{1,30},{2,1},{3,4},{4,7},{5,2},{6,5},{7,8},{8,11},{9,6},{10,... | collective-permute-start | bytes 786440 | tf_op jit(solution)/shard_map/ppermute | solution.py:104
  34.6 8.9 %collective-permute-start.6 = (bf16[32,4096]{1,0:T(8,128)(2,1)S(1)}, bf16[32,4096]{1,0:T(8,128)(2,1)S(1)}, u32[]{:S(2)}, u32[]{:S(2)}) collective-permute-start(bf16[32,4096]{1,0:T(8,128)(2,1)S(1)} %collective-permute-done.4.refs_5_), channel_id=1, source_target_pairs={{0,3},{1,30},{2,1},{3,4},{4,7},{5,2},{6,5},{7,8},{8,11},{9,6},{10,... | collective-permute-start | bytes 786440 | tf_op jit(solution)/shard_map/ppermute | solution.py:104
  40.2 8.9 %collective-permute-start.7 = (bf16[32,4096]{1,0:T(8,128)(2,1)S(1)}, bf16[32,4096]{1,0:T(8,128)(2,1)S(1)}, u32[]{:S(2)}, u32[]{:S(2)}) collective-permute-start(bf16[32,4096]{1,0:T(8,128)(2,1)S(1)} %collective-permute-done.5.refs_6_), channel_id=1, source_target_pairs={{0,3},{1,30},{2,1},{3,4},{4,7},{5,2},{6,5},{7,8},{8,11},{9,6},{10,... | collective-permute-start | bytes 786440 | tf_op jit(solution)/shard_map/ppermute | solution.py:104
  43.5 15.5 %collective-permute-start.8 = (bf16[32,4096]{1,0:T(8,128)(2,1)S(1)}, bf16[32,4096]{1,0:T(8,128)(2,1)S(1)}, u32[]{:S(2)}, u32[]{:S(2)}) collective-permute-start(bf16[32,4096]{1,0:T(8,128)(2,1)S(1)} %collective-permute-done.6.refs_0_), channel_id=1, source_target_pairs={{0,3},{1,30},{2,1},{3,4},{4,7},{5,2},{6,5},{7,8},{8,11},{9,6},{10,... | collective-permute-start | bytes 786440 | tf_op jit(solution)/shard_map/ppermute | solution.py:104
  49.1 12.4 %collective-permute-start.9 = (bf16[32,4096]{1,0:T(8,128)(2,1)S(1)}, bf16[32,4096]{1,0:T(8,128)(2,1)S(1)}, u32[]{:S(2)}, u32[]{:S(2)}) collective-permute-start(bf16[32,4096]{1,0:T(8,128)(2,1)S(1)} %collective-permute-done.7.refs_1_), channel_id=1, source_target_pairs={{0,3},{1,30},{2,1},{3,4},{4,7},{5,2},{6,5},{7,8},{8,11},{9,6},{10,... | collective-permute-start | bytes 786440 | tf_op jit(solution)/shard_map/ppermute | solution.py:104
  52.0 41.0 %collective-permute-start.20 = (bf16[128,4096]{1,0:T(8,128)(2,1)}, bf16[128,4096]{1,0:T(8,128)(2,1)S(1)}, u32[]{:S(2)}, u32[]{:S(2)}) collective-permute-start(bf16[128,4096]{1,0:T(8,128)(2,1)} %bitcast.74), channel_id=1, source_target_pairs={{0,32},{32,0},{1,33},{33,1},{2,34},{34,2},{3,35},{35,3},{4,36},{36... | collective-permute-start | bytes 3145736 | tf_op jit(solution)/shard_map/ppermute | solution.py:104
  56.8 43.8 %collective-permute-start.19 = (bf16[128,4096]{1,0:T(8,128)(2,1)}, bf16[128,4096]{1,0:T(8,128)(2,1)S(1)}, u32[]{:S(2)}, u32[]{:S(2)}) collective-permute-start(bf16[128,4096]{1,0:T(8,128)(2,1)} %bitcast.76), channel_id=1, source_target_pairs={{0,32},{32,0},{1,33},{33,1},{2,34},{34,2},{3,35},{35,3},{4,36},{36... | collective-permute-start | bytes 3145736 | tf_op jit(solution)/shard_map/ppermute | solution.py:104
  58.9 8.0 %collective-permute-start.10 = (bf16[32,4096]{1,0:T(8,128)(2,1)S(1)}, bf16[32,4096]{1,0:T(8,128)(2,1)S(1)}, u32[]{:S(2)}, u32[]{:S(2)}) collective-permute-start(bf16[32,4096]{1,0:T(8,128)(2,1)S(1)} %collective-permute-done.8.refs_2_), channel_id=1, source_target_pairs={{0,3},{1,30},{2,1},{3,4},{4,7},{5,2},{6,5},{7,8},{8,11},{9,6},{10,... | collective-permute-start | bytes 786440 | tf_op jit(solution)/shard_map/ppermute | solution.py:104
  61.4 9.6 %collective-permute-start.11 = (bf16[32,4096]{1,0:T(8,128)(2,1)S(1)}, bf16[32,4096]{1,0:T(8,128)(2,1)S(1)}, u32[]{:S(2)}, u32[]{:S(2)}) collective-permute-start(bf16[32,4096]{1,0:T(8,128)(2,1)S(1)} %collective-permute-done.9.refs_3_), channel_id=1, source_target_pairs={{0,3},{1,30},{2,1},{3,4},{4,7},{5,2},{6,5},{7,8},{8,11},{9,6},{10,... | collective-permute-start | bytes 786440 | tf_op jit(solution)/shard_map/ppermute | solution.py:104
  63.6 26.0 %collective-permute-start.15 = (bf16[2,112,4096]{2,1,0:T(8,128)(2,1)S(1)}, bf16[2,112,4096]{2,1,0:T(8,128)(2,1)S(1)}, u32[]{:S(2)}, u32[]{:S(2)}) collective-permute-start(bf16[2,112,4096]{2,1,0:T(8,128)(2,1)S(1)} %stack.4), channel_id=1, source_target_pairs={{0,1},{1,0},{2,3},{3,2},{4,5},{5,4},{6,7},{7,6},{8,9},{9,8},{10,11... | collective-permute-start | bytes 5505032 | tf_op jit(solution)/shard_map/ppermute | solution.py:104
  66.9 8.0 %collective-permute-start.12 = (bf16[32,4096]{1,0:T(8,128)(2,1)S(1)}, bf16[32,4096]{1,0:T(8,128)(2,1)S(1)}, u32[]{:S(2)}, u32[]{:S(2)}) collective-permute-start(bf16[32,4096]{1,0:T(8,128)(2,1)S(1)} %collective-permute-done.10.refs_4_), channel_id=1, source_target_pairs={{0,3},{1,30},{2,1},{3,4},{4,7},{5,2},{6,5},{7,8},{8,11},{9,6},{10,... | collective-permute-start | bytes 786440 | tf_op jit(solution)/shard_map/ppermute | solution.py:104
  71.2 8.0 %collective-permute-start.13 = (bf16[32,4096]{1,0:T(8,128)(2,1)S(1)}, bf16[32,4096]{1,0:T(8,128)(2,1)S(1)}, u32[]{:S(2)}, u32[]{:S(2)}) collective-permute-start(bf16[32,4096]{1,0:T(8,128)(2,1)S(1)} %collective-permute-done.11.refs_5_), channel_id=1, source_target_pairs={{0,3},{1,30},{2,1},{3,4},{4,7},{5,2},{6,5},{7,8},{8,11},{9,6},{10,... | collective-permute-start | bytes 786440 | tf_op jit(solution)/shard_map/ppermute | solution.py:104
  74.9 16.8 %collective-permute-start.16 = (bf16[2,96,4096]{2,1,0:T(8,128)(2,1)S(1)}, bf16[2,96,4096]{2,1,0:T(8,128)(2,1)S(1)}, u32[]{:S(2)}, u32[]{:S(2)}) collective-permute-start(bf16[2,96,4096]{2,1,0:T(8,128)(2,1)S(1)} %stack.5), channel_id=1, source_target_pairs={{0,1},{1,0},{2,3},{3,2},{4,5},{5,4},{6,7},{7,6},{8,9},{9,8},{10,11... | collective-permute-start | bytes 4718600 | tf_op jit(solution)/shard_map/ppermute | solution.py:104
  79.2 8.0 %collective-permute-start.14 = (bf16[32,4096]{1,0:T(8,128)(2,1)S(1)}, bf16[32,4096]{1,0:T(8,128)(2,1)S(1)}, u32[]{:S(2)}, u32[]{:S(2)}) collective-permute-start(bf16[32,4096]{1,0:T(8,128)(2,1)S(1)} %collective-permute-done.12.refs_0_), channel_id=1, source_target_pairs={{0,3},{1,30},{2,1},{3,4},{4,7},{5,2},{6,5},{7,8},{8,11},{9,6},{10,... | collective-permute-start | bytes 786440 | tf_op jit(solution)/shard_map/ppermute | solution.py:104
  87.2 4.8 %collective-permute-start.17 = (bf16[2,32,4096]{2,1,0:T(8,128)(2,1)S(1)}, bf16[2,32,4096]{2,1,0:T(8,128)(2,1)S(1)}, u32[]{:S(2)}, u32[]{:S(2)}) collective-permute-start(bf16[2,32,4096]{2,1,0:T(8,128)(2,1)S(1)} %stack.6), channel_id=1, source_target_pairs={{0,1},{1,0},{2,3},{3,2},{4,5},{5,4},{6,7},{7,6},{8,9},{9,8},{10,11... | collective-permute-start | bytes 1572872 | tf_op jit(solution)/shard_map/ppermute | solution.py:104
  89.5 3.4 %collective-permute-start.18 = (bf16[2,16,4096]{2,1,0:T(8,128)(2,1)S(1)}, bf16[2,16,4096]{2,1,0:T(8,128)(2,1)S(1)}, u32[]{:S(2)}, u32[]{:S(2)}) collective-permute-start(bf16[2,16,4096]{2,1,0:T(8,128)(2,1)S(1)} %stack.7), channel_id=1, source_target_pairs={{0,1},{1,0},{2,3},{3,2},{4,5},{5,4},{6,7},{7,6},{8,9},{9,8},{10,11... | collective-permute-start | bytes 786440 | tf_op jit(solution)/shard_map/ppermute | solution.py:104
  91.5 1.5 %copy-start = (bf16[1,128,4096]{2,1,0:T(8,128)(2,1)S(1)}, bf16[1,128,4096]{2,1,0:T(8,128)(2,1)}, u32[]{:S(2)}) copy-start(bf16[1,128,4096]{2,1,0:T(8,128)(2,1)} %param.7) | copy-start | bytes 3145732
  93.0 7.6 %copy-start.1 = (bf16[1,128,4096]{2,1,0:T(8,128)(2,1)S(1)}, bf16[1,128,4096]{2,1,0:T(8,128)(2,1)}, u32[]{:S(2)}) copy-start(bf16[1,128,4096]{2,1,0:T(8,128)(2,1)} %param.6) | copy-start | bytes 3145732

commit v5 on v3

v5 whole, which is shorter than its diff:
```python
import functools

import jax
import jax.numpy as jnp
from jax import lax
from jax.experimental import pallas as pl
from jax.experimental.pallas import tpu as pltpu
from jax.sharding import PartitionSpec as P


MIB = 1 << 20
VMEM = pl.BlockSpec(memory_space=pltpu.VMEM)
GROUPS = (
    ((0, 0), (0, 1), (1, 1), (0, 2), (1, 2), (0, 3), (1, 3)),
    ((0, 4), (1, 4), (0, 5), (1, 5), (0, 6), (1, 6)),
    ((0, 7), (1, 7)),
)


def stack_kernel(*refs):
    *parts, out = refs
    height = parts[0].shape[0] // 2
    for i, part in enumerate(parts):
        out[0, i * height : (i + 1) * height, :] = part[:height, :]
        out[1, i * height : (i + 1) * height, :] = part[height:, :]


def stack(parts):
    height, depth = parts[0].shape
    return pl.pallas_call(
        stack_kernel,
        out_shape=jax.ShapeDtypeStruct((2, len(parts) * height // 2, depth), parts[0].dtype),
        in_specs=[VMEM] * len(parts),
        out_specs=VMEM,
        compiler_params=pltpu.CompilerParams(vmem_limit_bytes=8 * MIB),
        cost_estimate=pl.CostEstimate(flops=200_000_000, bytes_accessed=0, transcendentals=0),
        name="stack",
    )(*parts)


def finish_kernel(height, depth, early, *refs):
    stacks, (own_act, other_act, own_back, other_back, out, act, back) = refs[:-7], refs[-7:]
    tcol = lax.axis_index("tcol")
    z, core = lax.shift_right_logical(tcol, 1), lax.rem(tcol, 2)
    planes = out.shape[0] // (2 * height)
    sign = 1 - 2 * lax.rem(z + core, 2)

    def put(rows, shard, given):
        stream, step = shard
        plane = z + sign * step if given else z - sign * step
        on = core if (stream + step + given) % 2 == 0 else 1 - core
        at = pl.multiple_of((lax.rem(plane + planes, planes) * 2 + on) * height, height)
        out[pl.ds(at, height), :] = rows

    first = [shard for group in GROUPS[:-1] for shard in group]
    for i, shard in enumerate(first + first):
        put(early[i * height : (i + 1) * height, :], shard, int(i >= len(first)))

    late = list(GROUPS[-1]) + [(0, planes // 2)]
    at = 0
    for stack in stacks:
        for i in range(stack.shape[1] // height):
            act[at : at + height, :] = stack[0, i * height : (i + 1) * height, :]
            back[at : at + height, :] = stack[1, i * height : (i + 1) * height, :]
            at += height
    dims = (((1,), (1,)), ((), ()))

    def grams(cols, rows):
        return [lax.dot_general(c[...], rows[...], dims, preferred_element_type=jnp.float32) for c in cols]

    gram_act, gram_back = grams((own_act, other_act), act), grams((own_back, other_back), back)
    terms = jnp.concatenate([(a * b * (1.0 / depth)).T for a, b in zip(gram_act, gram_back)], axis=1)
    for i, shard in enumerate(late + late):
        put(terms[i * height : (i + 1) * height, :], shard, int(i >= len(late)))


def finish(early, stacks, cols, height, planes):
    width, depth = cols[0].shape
    late = sum(s.shape[1] for s in stacks)
    return pl.pallas_call(
        functools.partial(finish_kernel, height, depth),
        out_shape=jax.ShapeDtypeStruct((2 * planes * height, 2 * width), early.dtype),
        in_specs=[VMEM] * (1 + len(stacks) + len(cols)),
        out_specs=VMEM,
        scratch_shapes=[pltpu.VMEM((late, depth), cols[0].dtype)] * 2,
        compiler_params=pltpu.CompilerParams(vmem_limit_bytes=12 * MIB),
        cost_estimate=pl.CostEstimate(flops=8 * late * width * depth, bytes_accessed=0, transcendentals=0),
        name="finish",
    )(early, *stacks, *cols)


def sum_kernel(got, out):
    trow = lax.axis_index("trow")
    width = out.shape[1] // 2
    for half, at in ((0, trow), (1, 1 - trow)):
        to = pl.ds(pl.multiple_of(at * width, width), width)
        out[:, to] = jnp.sum(got[:, :, half * width : (half + 1) * width], axis=0)


def layer_sum(got):
    return pl.pallas_call(
        sum_kernel,
        out_shape=jax.ShapeDtypeStruct(got.shape[1:], got.dtype),
        in_specs=[VMEM],
        out_specs=VMEM,
        compiler_params=pltpu.CompilerParams(vmem_limit_bytes=4 * MIB),
        name="layer_sum",
    )(got)


def local(act_rows, back_rows, act_cols, back_cols):
    layers, tcols = lax.axis_size("layer"), lax.axis_size("tcol")
    planes = tcols // 2
    half = planes // 2
    depth = act_rows.shape[2]

    along, aslant, beside = [], [], []
    for p in range(planes):
        for c in range(2):
            step = 1 - 2 * ((p + c) % 2)
            along.append((2 * p + c, 2 * ((p + step) % planes) + 1 - c))
            aslant.append((2 * p + c, 2 * ((p - step) % planes) + c))
            beside.append((2 * p + c, 2 * ((p + step) % planes) + c))
    cores = [(t, t ^ 1) for t in range(tcols)]

    own = jnp.concatenate((act_rows[0], back_rows[0]), axis=0)
    held = {(0, 0): own, (0, 1): lax.ppermute(own, "tcol", along), (1, 1): lax.ppermute(own, "tcol", aslant)}
    for step in range(2, half + 1):
        held[0, step] = lax.ppermute(held[0, step - 1], "tcol", along)
        if step < half:
            held[1, step] = lax.ppermute(held[1, step - 1], "tcol", along)
    last = [held[0, half], lax.ppermute(held[0, half - 1], "tcol", beside)]
    across = [(0, 1), (1, 0)]
    other_act = lax.ppermute(act_cols[0], "trow", across)
    other_back = lax.ppermute(back_cols[0], "trow", across)
    mine = [stack([held[shard] for shard in group]) for group in GROUPS]
    given = [lax.ppermute(rows, "tcol", cores) for rows in mine]

    early = mine[:-1] + given[:-1]
    rows, cols = jnp.concatenate([s[0] for s in early], axis=0), jnp.concatenate((act_cols[0], other_act), axis=0)
    gram_act = jnp.einsum("rd,cd->rc", rows, cols, preferred_element_type=jnp.float32)
    rows, cols = jnp.concatenate([s[1] for s in early], axis=0), jnp.concatenate((back_cols[0], other_back), axis=0)
    gram_back = jnp.einsum("rd,cd->rc", rows, cols, preferred_element_type=jnp.float32)
    terms = gram_act * gram_back / depth
    height = act_rows.shape[1]
    last = [s.reshape(2, height, depth) for s in last]
    stacks = (mine[-1], last[0], given[-1], last[1])
    terms = finish(terms, stacks, (act_cols[0], other_act, back_cols[0], other_back), height, planes)
    got = lax.all_to_all(terms.reshape(layers, -1, terms.shape[-1]), "layer", 0, 0, tiled=True)
    return layer_sum(got)


def solution(mesh):
    in_specs = (
        P("layer", ("trow", "tcol"), None),
        P("layer", ("trow", "tcol"), None),
        P("layer", ("tcol", "trow"), None),
        P("layer", ("tcol", "trow"), None),
    )
    out_specs = P(("trow", "layer"), "tcol")
    return jax.shard_map(local, mesh=mesh, in_specs=in_specs, out_specs=out_specs, check_vma=False)
```

time: 124 us -> 125 us (level)
  waiting for transfers between devices: 48.7 us -> 42.3 us
  starting transfers between devices: 55.3 us -> 61.3 us
    ppermute x14, starting transfers between devices: 24.9 us -> 31.3 us  [the longest x7 14.4 us: local(): held[0, step] = lax.ppermute(held[0, step - 1], 'tcol', along)]
    ppermute x14, waiting for transfers between devices: 28.2 us -> 25.6 us  [the longest x7 18.8 us: local(): held[0, step] = lax.ppermute(held[0, step - 1], 'tcol', along)]
    ppermute x1, waiting for transfers between devices: 3.27 us -> 1.12 us  [local(): lax.ppermute(own, 'tcol', along)]
    ppermute x3, waiting for transfers between devices: 1.79 us -> 0.01 us  [local(): given = [lax.ppermute(rows, 'tcol', cores) for rows in mine]]
    ppermute x1, waiting for transfers between devices: 0.01 us -> 1.3 us  [local(): lax.ppermute(own, 'tcol', aslant)]
  transfers between devices with their start and end apart: 21 -> 21, of which waited for: 13 -> 12; matrix products, arithmetic and copies ran while one was open for 2% -> 2% of each run, Pallas kernels for 0% -> 0%
where the time goes in v5:
time: 125 us; the launch traced here: 123 us
  starting transfers between devices  61.3 us (49%)
  waiting for transfers between devices  42.3 us (34%)
  blocking collectives  13.4 us (11%)
  Pallas kernels  2.22 us (2%)
  matrix products  2.15 us (2%)
    ppermute x7, waiting for transfers between devices, local(): held[0, step] = lax.ppermute(held[0, step - 1], 'tcol', along)  18.8 us
    ppermute x7, starting transfers between devices, local(): held[0, step] = lax.ppermute(held[0, step - 1], 'tcol', along)  14.4 us
    ppermute x1, waiting for transfers between devices, local(): other_act = lax.ppermute(act_cols[0], 'trow', across)  14.3 us
    all_to_all x1, blocking collectives, local(): lax.all_to_all(terms.reshape(layers, -1, terms.shape[-1]), 'layer', 0, 0,...  13.4 us
    ppermute x6, starting transfers between devices, local(): held[1, step] = lax.ppermute(held[1, step - 1], 'tcol', along)  12.7 us
    ppermute x1, starting transfers between devices, local(): lax.ppermute(own, 'tcol', aslant)  10.5 us
    ppermute x3, starting transfers between devices, local(): given = [lax.ppermute(rows, 'tcol', cores) for rows in mine]  8.93 us
    ppermute x6, waiting for transfers between devices, local(): held[1, step] = lax.ppermute(held[1, step - 1], 'tcol', along)  6.85 us
  transfers between devices with their start and end apart: 21, of which 12 were waited for; matrix products, arithmetic and copies ran while one was open for 2% of the time, Pallas kernels for 0%

profile of v5, /device:TPU:24, one launch (start us, length us, event | category | flops | bytes accessed | tf_op | source)
XLA Modules:
  0.0 123.3 jit_solution(807179560840643932)
XLA Ops:
  0.0 1.0 pad_maximum_fusion.refs_0_
  1.0 3.3 %collective-permute-start = (bf16[32,4096]{1,0:T(8,128)(2,1)S(1)}, bf16[32,4096]{1,0:T(8,128)(2,1)S(1)}, u32[]{:S(2)}, u32[]{:S(2)}) collective-permute-start(bf16[32,4096]{1,0:T(8,128)(2,1)S(1)} %pad_maximum_fusion.refs_0_), channel_id=1, source_target_pairs={{0,3},{1,30},{2,1},{3,4},{4,7},{5,2},{6,5},{7,8},{8,11},{9,6},{10,... | collective-permute-start | bytes 786440 | tf_op jit(solution)/shard_map/ppermute | solution.py:127
  4.3 10.5 %collective-permute-start.1 = (bf16[32,4096]{1,0:T(8,128)(2,1)S(1)}, bf16[32,4096]{1,0:T(8,128)(2,1)S(1)}, u32[]{:S(2)}, u32[]{:S(2)}) collective-permute-start(bf16[32,4096]{1,0:T(8,128)(2,1)S(1)} %pad_maximum_fusion.refs_0_), channel_id=1, source_target_pairs={{0,30},{1,3},{2,4},{3,1},{4,2},{5,7},{6,8},{7,5},{8,6},{9,11},{10,... | collective-permute-start | bytes 786440 | tf_op jit(solution)/shard_map/ppermute | solution.py:127
  14.8 1.1 collective-permute-done.refs_1_
  15.9 1.9 %collective-permute-start.2 = (bf16[32,4096]{1,0:T(8,128)(2,1)S(1)}, bf16[32,4096]{1,0:T(8,128)(2,1)S(1)}, u32[]{:S(2)}, u32[]{:S(2)}) collective-permute-start(bf16[32,4096]{1,0:T(8,128)(2,1)S(1)} %collective-permute-done.refs_1_), channel_id=1, source_target_pairs={{0,3},{1,30},{2,1},{3,4},{4,7},{5,2},{6,5},{7,8},{8,11},{9,6},{10,... | collective-permute-start | bytes 786440 | tf_op jit(solution)/shard_map/ppermute | solution.py:129
  17.8 1.3 %collective-permute-done.1.refs_2_ = bf16[32,4096]{1,0:T(8,128)(2,1)S(1)} collective-permute-done((bf16[32,4096]{1,0:T(8,128)(2,1)S(1)}, bf16[32,4096]{1,0:T(8,128)(2,1)S(1)}, u32[]{:S(2)}, u32[]{:S(2)}) %collective-permute-start.1) | collective-permute-done | bytes 262176 | tf_op jit(solution)/shard_map/ppermute | solution.py:127
  19.1 2.3 %collective-permute-start.3 = (bf16[32,4096]{1,0:T(8,128)(2,1)S(1)}, bf16[32,4096]{1,0:T(8,128)(2,1)S(1)}, u32[]{:S(2)}, u32[]{:S(2)}) collective-permute-start(bf16[32,4096]{1,0:T(8,128)(2,1)S(1)} %collective-permute-done.1.refs_2_), channel_id=1, source_target_pairs={{0,3},{1,30},{2,1},{3,4},{4,7},{5,2},{6,5},{7,8},{8,11},{9,6},{10,... | collective-permute-start | bytes 786440 | tf_op jit(solution)/shard_map/ppermute | solution.py:131
  21.4 3.3 %collective-permute-done.2.refs_3_ = bf16[32,4096]{1,0:T(8,128)(2,1)S(1)} collective-permute-done((bf16[32,4096]{1,0:T(8,128)(2,1)S(1)}, bf16[32,4096]{1,0:T(8,128)(2,1)S(1)}, u32[]{:S(2)}, u32[]{:S(2)}) %collective-permute-start.2) | collective-permute-done | bytes 262176 | tf_op jit(solution)/shard_map/ppermute | solution.py:129
  24.8 1.9 %collective-permute-start.4 = (bf16[32,4096]{1,0:T(8,128)(2,1)S(1)}, bf16[32,4096]{1,0:T(8,128)(2,1)S(1)}, u32[]{:S(2)}, u32[]{:S(2)}) collective-permute-start(bf16[32,4096]{1,0:T(8,128)(2,1)S(1)} %collective-permute-done.2.refs_3_), channel_id=1, source_target_pairs={{0,3},{1,30},{2,1},{3,4},{4,7},{5,2},{6,5},{7,8},{8,11},{9,6},{10,... | collective-permute-start | bytes 786440 | tf_op jit(solution)/shard_map/ppermute | solution.py:129
  26.7 1.3 %collective-permute-done.3.refs_4_ = bf16[32,4096]{1,0:T(8,128)(2,1)S(1)} collective-permute-done((bf16[32,4096]{1,0:T(8,128)(2,1)S(1)}, bf16[32,4096]{1,0:T(8,128)(2,1)S(1)}, u32[]{:S(2)}, u32[]{:S(2)}) %collective-permute-start.3) | collective-permute-done | bytes 262176 | tf_op jit(solution)/shard_map/ppermute | solution.py:131
  28.0 1.9 %collective-permute-start.5 = (bf16[32,4096]{1,0:T(8,128)(2,1)S(1)}, bf16[32,4096]{1,0:T(8,128)(2,1)S(1)}, u32[]{:S(2)}, u32[]{:S(2)}) collective-permute-start(bf16[32,4096]{1,0:T(8,128)(2,1)S(1)} %collective-permute-done.3.refs_4_), channel_id=1, source_target_pairs={{0,3},{1,30},{2,1},{3,4},{4,7},{5,2},{6,5},{7,8},{8,11},{9,6},{10,... | collective-permute-start | bytes 786440 | tf_op jit(solution)/shard_map/ppermute | solution.py:131
  29.9 3.8 %collective-permute-done.4.refs_5_ = bf16[32,4096]{1,0:T(8,128)(2,1)S(1)} collective-permute-done((bf16[32,4096]{1,0:T(8,128)(2,1)S(1)}, bf16[32,4096]{1,0:T(8,128)(2,1)S(1)}, u32[]{:S(2)}, u32[]{:S(2)}) %collective-permute-start.4) | collective-permute-done | bytes 262176 | tf_op jit(solution)/shard_map/ppermute | solution.py:129
  33.7 1.9 %collective-permute-start.6 = (bf16[32,4096]{1,0:T(8,128)(2,1)S(1)}, bf16[32,4096]{1,0:T(8,128)(2,1)S(1)}, u32[]{:S(2)}, u32[]{:S(2)}) collective-permute-start(bf16[32,4096]{1,0:T(8,128)(2,1)S(1)} %collective-permute-done.4.refs_5_), channel_id=1, source_target_pairs={{0,3},{1,30},{2,1},{3,4},{4,7},{5,2},{6,5},{7,8},{8,11},{9,6},{10,... | collective-permute-start | bytes 786440 | tf_op jit(solution)/shard_map/ppermute | solution.py:129
  35.6 1.3 %collective-permute-done.5.refs_6_ = bf16[32,4096]{1,0:T(8,128)(2,1)S(1)} collective-permute-done((bf16[32,4096]{1,0:T(8,128)(2,1)S(1)}, bf16[32,4096]{1,0:T(8,128)(2,1)S(1)}, u32[]{:S(2)}, u32[]{:S(2)}) %collective-permute-start.5) | collective-permute-done | bytes 262176 | tf_op jit(solution)/shard_map/ppermute | solution.py:131
  36.9 1.9 %collective-permute-start.7 = (bf16[32,4096]{1,0:T(8,128)(2,1)S(1)}, bf16[32,4096]{1,0:T(8,128)(2,1)S(1)}, u32[]{:S(2)}, u32[]{:S(2)}) collective-permute-start(bf16[32,4096]{1,0:T(8,128)(2,1)S(1)} %collective-permute-done.5.refs_6_), channel_id=1, source_target_pairs={{0,3},{1,30},{2,1},{3,4},{4,7},{5,2},{6,5},{7,8},{8,11},{9,6},{10,... | collective-permute-start | bytes 786440 | tf_op jit(solution)/shard_map/ppermute | solution.py:131
  38.8 3.8 %collective-permute-done.6.refs_0_ = bf16[32,4096]{1,0:T(8,128)(2,1)S(1)} collective-permute-done((bf16[32,4096]{1,0:T(8,128)(2,1)S(1)}, bf16[32,4096]{1,0:T(8,128)(2,1)S(1)}, u32[]{:S(2)}, u32[]{:S(2)}) %collective-permute-start.6) | collective-permute-done | bytes 262176 | tf_op jit(solution)/shard_map/ppermute | solution.py:129
  42.6 1.9 %collective-permute-start.8 = (bf16[32,4096]{1,0:T(8,128)(2,1)S(1)}, bf16[32,4096]{1,0:T(8,128)(2,1)S(1)}, u32[]{:S(2)}, u32[]{:S(2)}) collective-permute-start(bf16[32,4096]{1,0:T(8,128)(2,1)S(1)} %collective-permute-done.6.refs_0_), channel_id=1, source_target_pairs={{0,3},{1,30},{2,1},{3,4},{4,7},{5,2},{6,5},{7,8},{8,11},{9,6},{10,... | collective-permute-start | bytes 786440 | tf_op jit(solution)/shard_map/ppermute | solution.py:129
  44.5 1.3 %collective-permute-done.7.refs_1_ = bf16[32,4096]{1,0:T(8,128)(2,1)S(1)} collective-permute-done((bf16[32,4096]{1,0:T(8,128)(2,1)S(1)}, bf16[32,4096]{1,0:T(8,128)(2,1)S(1)}, u32[]{:S(2)}, u32[]{:S(2)}) %collective-permute-start.7) | collective-permute-done | bytes 262176 | tf_op jit(solution)/shard_map/ppermute | solution.py:131
  45.8 1.9 %collective-permute-start.9 = (bf16[32,4096]{1,0:T(8,128)(2,1)S(1)}, bf16[32,4096]{1,0:T(8,128)(2,1)S(1)}, u32[]{:S(2)}, u32[]{:S(2)}) collective-permute-start(bf16[32,4096]{1,0:T(8,128)(2,1)S(1)} %collective-permute-done.7.refs_1_), channel_id=1, source_target_pairs={{0,3},{1,30},{2,1},{3,4},{4,7},{5,2},{6,5},{7,8},{8,11},{9,6},{10,... | collective-permute-start | bytes 786440 | tf_op jit(solution)/shard_map/ppermute | solution.py:131
  47.7 3.1 %collective-permute-start.15 = (bf16[128,4096]{1,0:T(8,128)(2,1)}, bf16[128,4096]{1,0:T(8,128)(2,1)S(1)}, u32[]{:S(2)}, u32[]{:S(2)}) collective-permute-start(bf16[128,4096]{1,0:T(8,128)(2,1)} %bitcast.24), channel_id=1, source_target_pairs={{0,32},{32,0},{1,33},{33,1},{2,34},{34,2},{3,35},{35,3},{4,36},{36... | collective-permute-start | bytes 3145736 | tf_op jit(solution)/shard_map/ppermute | solution.py:135
  50.8 0.1 stack.3
  51.0 5.0 %collective-permute-start.12 = (bf16[2,112,4096]{2,1,0:T(8,128)(2,1)S(1)}, bf16[2,112,4096]{2,1,0:T(8,128)(2,1)S(1)}, u32[]{:S(2)}, u32[]{:S(2)}) collective-permute-start(bf16[2,112,4096]{2,1,0:T(8,128)(2,1)S(1)} %stack.3), channel_id=1, source_target_pairs={{0,1},{1,0},{2,3},{3,2},{4,5},{5,4},{6,7},{7,6},{8,9},{9,8},{10,11... | collective-permute-start | bytes 5505032 | tf_op jit(solution)/shard_map/ppermute | solution.py:137
  55.9 0.0 collective-permute-done.8.refs_2_
  55.9 2.9 %collective-permute-start.10 = (bf16[32,4096]{1,0:T(8,128)(2,1)S(1)}, bf16[32,4096]{1,0:T(8,128)(2,1)S(1)}, u32[]{:S(2)}, u32[]{:S(2)}) collective-permute-start(bf16[32,4096]{1,0:T(8,128)(2,1)S(1)} %collective-permute-done.8.refs_2_), channel_id=1, source_target_pairs={{0,3},{1,30},{2,1},{3,4},{4,7},{5,2},{6,5},{7,8},{8,11},{9,6},{10,... | collective-permute-start | bytes 786440 | tf_op jit(solution)/shard_map/ppermute | solution.py:129
  58.9 1.9 %collective-permute-start.11 = (bf16[32,4096]{1,0:T(8,128)(2,1)S(1)}, bf16[32,4096]{1,0:T(8,128)(2,1)S(1)}, u32[]{:S(2)}, u32[]{:S(2)}) collective-permute-start(bf16[32,4096]{1,0:T(8,128)(2,1)S(1)} %collective-permute-done.9.refs_3_), channel_id=1, source_target_pairs={{0,3},{1,30},{2,1},{3,4},{4,7},{5,2},{6,5},{7,8},{8,11},{9,6},{10,... | collective-permute-start | bytes 786440 | tf_op jit(solution)/shard_map/ppermute | solution.py:131
  60.8 0.2 slice_bitcast_fusion.3
  61.0 3.8 %collective-permute-done.10.refs_4_ = bf16[32,4096]{1,0:T(8,128)(2,1)S(1)} collective-permute-done((bf16[32,4096]{1,0:T(8,128)(2,1)S(1)}, bf16[32,4096]{1,0:T(8,128)(2,1)S(1)}, u32[]{:S(2)}, u32[]{:S(2)}) %collective-permute-start.10) | collective-permute-done | bytes 262176 | tf_op jit(solution)/shard_map/ppermute | solution.py:129
  64.8 2.9 %collective-permute-done.11.refs_5_ = bf16[32,4096]{1,0:T(8,128)(2,1)S(1)} collective-permute-done((bf16[32,4096]{1,0:T(8,128)(2,1)S(1)}, bf16[32,4096]{1,0:T(8,128)(2,1)S(1)}, u32[]{:S(2)}, u32[]{:S(2)}) %collective-permute-start.11) | collective-permute-done | bytes 262176 | tf_op jit(solution)/shard_map/ppermute | solution.py:131
  67.8 0.1 stack.4
  67.9 0.0 copy-start.1
  67.9 2.1 %collective-permute-start.13 = (bf16[2,96,4096]{2,1,0:T(8,128)(2,1)S(1)}, bf16[2,96,4096]{2,1,0:T(8,128)(2,1)S(1)}, u32[]{:S(2)}, u32[]{:S(2)}) collective-permute-start(bf16[2,96,4096]{2,1,0:T(8,128)(2,1)S(1)} %stack.4), channel_id=1, source_target_pairs={{0,1},{1,0},{2,3},{3,2},{4,5},{5,4},{6,7},{7,6},{8,9},{9,8},{10,11... | collective-permute-start | bytes 4718600 | tf_op jit(solution)/shard_map/ppermute | solution.py:137
  70.0 1.9 %collective-permute-start.16 = (bf16[32,4096]{1,0:T(8,128)(2,1)S(1)}, bf16[32,4096]{1,0:T(8,128)(2,1)S(1)}, u32[]{:S(2)}, u32[]{:S(2)}) collective-permute-start(bf16[32,4096]{1,0:T(8,128)(2,1)S(1)} %collective-permute-done.10.refs_4_), channel_id=1, source_target_pairs={{0,3},{1,30},{2,1},{3,4},{4,7},{5,2},{6,5},{7,8},{8,11},{9,6},{10,... | collective-permute-start | bytes 786440 | tf_op jit(solution)/shard_map/ppermute | solution.py:129
  71.9 2.7 %collective-permute-start.17 = (bf16[32,4096]{1,0:T(8,128)(2,1)S(1)}, bf16[32,4096]{1,0:T(8,128)(2,1)S(1)}, u32[]{:S(2)}, u32[]{:S(2)}) collective-permute-start(bf16[32,4096]{1,0:T(8,128)(2,1)S(1)} %collective-permute-done.11.refs_5_), channel_id=1, source_target_pairs={{0,3},{1,30},{2,1},{3,4},{4,7},{5,2},{6,5},{7,8},{8,11},{9,6},{10,... | collective-permute-start | bytes 786440 | tf_op jit(solution)/shard_map/ppermute | solution.py:131
  74.6 0.1 slice_bitcast_fusion.7
  74.8 4.1 %collective-permute-done.16.refs_0_ = bf16[32,4096]{1,0:T(8,128)(2,1)S(1)} collective-permute-done((bf16[32,4096]{1,0:T(8,128)(2,1)S(1)}, bf16[32,4096]{1,0:T(8,128)(2,1)S(1)}, u32[]{:S(2)}, u32[]{:S(2)}) %collective-permute-start.16) | collective-permute-done | bytes 262176 | tf_op jit(solution)/shard_map/ppermute | solution.py:129
  78.9 4.2 %collective-permute-start.14 = (bf16[128,4096]{1,0:T(8,128)(2,1)S(1)}, bf16[128,4096]{1,0:T(8,128)(2,1)S(1)}, u32[]{:S(2)}, u32[]{:S(2)}) collective-permute-start(bf16[128,4096]{1,0:T(8,128)(2,1)S(1)} %bitcast.27), channel_id=1, source_target_pairs={{0,32},{32,0},{1,33},{33,1},{2,34},{34,2},{3,35},{35,3},{4,36},{36... | collective-permute-start | bytes 3145736 | tf_op jit(solution)/shard_map/ppermute | solution.py:134
  83.1 1.9 %collective-permute-start.19 = (bf16[2,32,4096]{2,1,0:T(8,128)(2,1)S(1)}, bf16[2,32,4096]{2,1,0:T(8,128)(2,1)S(1)}, u32[]{:S(2)}, u32[]{:S(2)}) collective-permute-start(bf16[2,32,4096]{2,1,0:T(8,128)(2,1)S(1)} %stack.5.refs_0_), channel_id=1, source_target_pairs={{0,1},{1,0},{2,3},{3,2},{4,5},{5,4},{6,7},{7,6},{8,9},{9,8},{10,11... | collective-permute-start | bytes 1572872 | tf_op jit(solution)/shard_map/ppermute | solution.py:137
  85.1 1.9 %collective-permute-start.18 = (bf16[32,4096]{1,0:T(8,128)(2,1)S(1)}, bf16[32,4096]{1,0:T(8,128)(2,1)S(1)}, u32[]{:S(2)}, u32[]{:S(2)}) collective-permute-start(bf16[32,4096]{1,0:T(8,128)(2,1)S(1)} %collective-permute-done.16.refs_0_), channel_id=1, source_target_pairs={{0,3},{1,30},{2,1},{3,4},{4,7},{5,2},{6,5},{7,8},{8,11},{9,6},{10,... | collective-permute-start | bytes 786440 | tf_op jit(solution)/shard_map/ppermute | solution.py:129
  87.0 0.2 slice_bitcast_fusion.2
  87.2 0.0 copy-start
  87.2 4.2 %collective-permute-start.20 = (bf16[32,4096]{1,0:T(8,128)(2,1)S(1)}, bf16[32,4096]{1,0:T(8,128)(2,1)S(1)}, u32[]{:S(2)}, u32[]{:S(2)}) collective-permute-start(bf16[32,4096]{1,0:T(8,128)(2,1)S(1)} %collective-permute-done.16.refs_0_), channel_id=1, source_target_pairs={{0,2},{1,31},{2,0},{3,5},{4,6},{5,3},{6,4},{7,9},{8,10},{9,7},{10,... | collective-permute-start | bytes 786440 | tf_op jit(solution)/shard_map/ppermute | solution.py:132
  91.4 0.1 slice_bitcast_fusion.6
  91.5 1.1 fusion.8
  92.6 14.3 %collective-permute-done.14.refs_5_ = bf16[128,4096]{1,0:T(8,128)(2,1)S(1)} collective-permute-done((bf16[128,4096]{1,0:T(8,128)(2,1)S(1)}, bf16[128,4096]{1,0:T(8,128)(2,1)S(1)}, u32[]{:S(2)}, u32[]{:S(2)}) %collective-permute-start.14) | collective-permute-done | bytes 1048608 | tf_op jit(solution)/shard_map/ppermute | solution.py:134
  106.9 1.1 fusion.27.early
  108.0 1.3 %finish.1 = f32[512,256]{1,0:T(8,128)S(1)} custom-call(f32[416,256]{1,0:T(8,128)S(1)} %fusion.27.early, bf16[2,32,4096]{2,1,0:T(8,128)(2,1)S(1)} %stack.5.refs_0_, bf16[2,16,4096]{2,1,0:T(8,128)(2,1)S(1)} %bitcast.30, bf16[2,32,4096]{2,1,0:T(8,128)(2,1)S(1)} %collective-permute-done.19.refs_2_, bf16[2,16,4096]{2,1,0:T(8,128)(2,1)S(1)} %bitcast.31, ...), custom_call_target="tpu_custom_call" | custom-call | flops 402653184 | tf_op jit(solution)/shard_map/finish/pallas_call | solution.py:80
  109.3 13.4 %all_to_all.5.got = f32[8,64,256]{2,1,0:T(8,128)S(1)} all-to-all(f32[8,64,256]{2,1,0:T(8,128)S(1)} %bitcast.23), channel_id=1, replica_groups=mesh['layer'=8,'trow'=2,'tcol'=32] {'layer'}, dimensions={0} | all-to-all | bytes 1048576 | tf_op jit(solution)/shard_map/all_to_all | solution.py:149
  122.7 0.7 layer_sum.1
  (11 shorter events, 0.1 us)
Async XLA Ops:
  1.0 14.9 %collective-permute-start = (bf16[32,4096]{1,0:T(8,128)(2,1)S(1)}, bf16[32,4096]{1,0:T(8,128)(2,1)S(1)}, u32[]{:S(2)}, u32[]{:S(2)}) collective-permute-start(bf16[32,4096]{1,0:T(8,128)(2,1)S(1)} %pad_maximum_fusion.refs_0_), channel_id=1, source_target_pairs={{0,3},{1,30},{2,1},{3,4},{4,7},{5,2},{6,5},{7,8},{8,11},{9,6},{10,... | collective-permute-start | bytes 786440 | tf_op jit(solution)/shard_map/ppermute | solution.py:127
  4.3 14.8 %collective-permute-start.1 = (bf16[32,4096]{1,0:T(8,128)(2,1)S(1)}, bf16[32,4096]{1,0:T(8,128)(2,1)S(1)}, u32[]{:S(2)}, u32[]{:S(2)}) collective-permute-start(bf16[32,4096]{1,0:T(8,128)(2,1)S(1)} %pad_maximum_fusion.refs_0_), channel_id=1, source_target_pairs={{0,30},{1,3},{2,4},{3,1},{4,2},{5,7},{6,8},{7,5},{8,6},{9,11},{10,... | collective-permute-start | bytes 786440 | tf_op jit(solution)/shard_map/ppermute | solution.py:127
  15.9 8.9 %collective-permute-start.2 = (bf16[32,4096]{1,0:T(8,128)(2,1)S(1)}, bf16[32,4096]{1,0:T(8,128)(2,1)S(1)}, u32[]{:S(2)}, u32[]{:S(2)}) collective-permute-start(bf16[32,4096]{1,0:T(8,128)(2,1)S(1)} %collective-permute-done.refs_1_), channel_id=1, source_target_pairs={{0,3},{1,30},{2,1},{3,4},{4,7},{5,2},{6,5},{7,8},{8,11},{9,6},{10,... | collective-permute-start | bytes 786440 | tf_op jit(solution)/shard_map/ppermute | solution.py:129
  19.1 8.9 %collective-permute-start.3 = (bf16[32,4096]{1,0:T(8,128)(2,1)S(1)}, bf16[32,4096]{1,0:T(8,128)(2,1)S(1)}, u32[]{:S(2)}, u32[]{:S(2)}) collective-permute-start(bf16[32,4096]{1,0:T(8,128)(2,1)S(1)} %collective-permute-done.1.refs_2_), channel_id=1, source_target_pairs={{0,3},{1,30},{2,1},{3,4},{4,7},{5,2},{6,5},{7,8},{8,11},{9,6},{10,... | collective-permute-start | bytes 786440 | tf_op jit(solution)/shard_map/ppermute | solution.py:131
  24.8 8.9 %collective-permute-start.4 = (bf16[32,4096]{1,0:T(8,128)(2,1)S(1)}, bf16[32,4096]{1,0:T(8,128)(2,1)S(1)}, u32[]{:S(2)}, u32[]{:S(2)}) collective-permute-start(bf16[32,4096]{1,0:T(8,128)(2,1)S(1)} %collective-permute-done.2.refs_3_), channel_id=1, source_target_pairs={{0,3},{1,30},{2,1},{3,4},{4,7},{5,2},{6,5},{7,8},{8,11},{9,6},{10,... | collective-permute-start | bytes 786440 | tf_op jit(solution)/shard_map/ppermute | solution.py:129
  28.0 8.9 %collective-permute-start.5 = (bf16[32,4096]{1,0:T(8,128)(2,1)S(1)}, bf16[32,4096]{1,0:T(8,128)(2,1)S(1)}, u32[]{:S(2)}, u32[]{:S(2)}) collective-permute-start(bf16[32,4096]{1,0:T(8,128)(2,1)S(1)} %collective-permute-done.3.refs_4_), channel_id=1, source_target_pairs={{0,3},{1,30},{2,1},{3,4},{4,7},{5,2},{6,5},{7,8},{8,11},{9,6},{10,... | collective-permute-start | bytes 786440 | tf_op jit(solution)/shard_map/ppermute | solution.py:131
  33.7 8.9 %collective-permute-start.6 = (bf16[32,4096]{1,0:T(8,128)(2,1)S(1)}, bf16[32,4096]{1,0:T(8,128)(2,1)S(1)}, u32[]{:S(2)}, u32[]{:S(2)}) collective-permute-start(bf16[32,4096]{1,0:T(8,128)(2,1)S(1)} %collective-permute-done.4.refs_5_), channel_id=1, source_target_pairs={{0,3},{1,30},{2,1},{3,4},{4,7},{5,2},{6,5},{7,8},{8,11},{9,6},{10,... | collective-permute-start | bytes 786440 | tf_op jit(solution)/shard_map/ppermute | solution.py:129
  36.9 8.9 %collective-permute-start.7 = (bf16[32,4096]{1,0:T(8,128)(2,1)S(1)}, bf16[32,4096]{1,0:T(8,128)(2,1)S(1)}, u32[]{:S(2)}, u32[]{:S(2)}) collective-permute-start(bf16[32,4096]{1,0:T(8,128)(2,1)S(1)} %collective-permute-done.5.refs_6_), channel_id=1, source_target_pairs={{0,3},{1,30},{2,1},{3,4},{4,7},{5,2},{6,5},{7,8},{8,11},{9,6},{10,... | collective-permute-start | bytes 786440 | tf_op jit(solution)/shard_map/ppermute | solution.py:131
  42.6 13.4 %collective-permute-start.8 = (bf16[32,4096]{1,0:T(8,128)(2,1)S(1)}, bf16[32,4096]{1,0:T(8,128)(2,1)S(1)}, u32[]{:S(2)}, u32[]{:S(2)}) collective-permute-start(bf16[32,4096]{1,0:T(8,128)(2,1)S(1)} %collective-permute-done.6.refs_0_), channel_id=1, source_target_pairs={{0,3},{1,30},{2,1},{3,4},{4,7},{5,2},{6,5},{7,8},{8,11},{9,6},{10,... | collective-permute-start | bytes 786440 | tf_op jit(solution)/shard_map/ppermute | solution.py:129
  45.8 13.1 %collective-permute-start.9 = (bf16[32,4096]{1,0:T(8,128)(2,1)S(1)}, bf16[32,4096]{1,0:T(8,128)(2,1)S(1)}, u32[]{:S(2)}, u32[]{:S(2)}) collective-permute-start(bf16[32,4096]{1,0:T(8,128)(2,1)S(1)} %collective-permute-done.7.refs_1_), channel_id=1, source_target_pairs={{0,3},{1,30},{2,1},{3,4},{4,7},{5,2},{6,5},{7,8},{8,11},{9,6},{10,... | collective-permute-start | bytes 786440 | tf_op jit(solution)/shard_map/ppermute | solution.py:131
  47.7 43.8 %collective-permute-start.15 = (bf16[128,4096]{1,0:T(8,128)(2,1)}, bf16[128,4096]{1,0:T(8,128)(2,1)S(1)}, u32[]{:S(2)}, u32[]{:S(2)}) collective-permute-start(bf16[128,4096]{1,0:T(8,128)(2,1)} %bitcast.24), channel_id=1, source_target_pairs={{0,32},{32,0},{1,33},{33,1},{2,34},{34,2},{3,35},{35,3},{4,36},{36... | collective-permute-start | bytes 3145736 | tf_op jit(solution)/shard_map/ppermute | solution.py:135
  51.0 34.1 %collective-permute-start.12 = (bf16[2,112,4096]{2,1,0:T(8,128)(2,1)S(1)}, bf16[2,112,4096]{2,1,0:T(8,128)(2,1)S(1)}, u32[]{:S(2)}, u32[]{:S(2)}) collective-permute-start(bf16[2,112,4096]{2,1,0:T(8,128)(2,1)S(1)} %stack.3), channel_id=1, source_target_pairs={{0,1},{1,0},{2,3},{3,2},{4,5},{5,4},{6,7},{7,6},{8,9},{9,8},{10,11... | collective-permute-start | bytes 5505032 | tf_op jit(solution)/shard_map/ppermute | solution.py:137
  55.9 8.9 %collective-permute-start.10 = (bf16[32,4096]{1,0:T(8,128)(2,1)S(1)}, bf16[32,4096]{1,0:T(8,128)(2,1)S(1)}, u32[]{:S(2)}, u32[]{:S(2)}) collective-permute-start(bf16[32,4096]{1,0:T(8,128)(2,1)S(1)} %collective-permute-done.8.refs_2_), channel_id=1, source_target_pairs={{0,3},{1,30},{2,1},{3,4},{4,7},{5,2},{6,5},{7,8},{8,11},{9,6},{10,... | collective-permute-start | bytes 786440 | tf_op jit(solution)/shard_map/ppermute | solution.py:129
  58.9 8.9 %collective-permute-start.11 = (bf16[32,4096]{1,0:T(8,128)(2,1)S(1)}, bf16[32,4096]{1,0:T(8,128)(2,1)S(1)}, u32[]{:S(2)}, u32[]{:S(2)}) collective-permute-start(bf16[32,4096]{1,0:T(8,128)(2,1)S(1)} %collective-permute-done.9.refs_3_), channel_id=1, source_target_pairs={{0,3},{1,30},{2,1},{3,4},{4,7},{5,2},{6,5},{7,8},{8,11},{9,6},{10,... | collective-permute-start | bytes 786440 | tf_op jit(solution)/shard_map/ppermute | solution.py:131
  67.9 11.0 %copy-start.1 = (bf16[1,128,4096]{2,1,0:T(8,128)(2,1)S(1)}, bf16[1,128,4096]{2,1,0:T(8,128)(2,1)}, u32[]{:S(2)}) copy-start(bf16[1,128,4096]{2,1,0:T(8,128)(2,1)} %param.6) | copy-start | bytes 3145732
  67.9 19.3 %collective-permute-start.13 = (bf16[2,96,4096]{2,1,0:T(8,128)(2,1)S(1)}, bf16[2,96,4096]{2,1,0:T(8,128)(2,1)S(1)}, u32[]{:S(2)}, u32[]{:S(2)}) collective-permute-start(bf16[2,96,4096]{2,1,0:T(8,128)(2,1)S(1)} %stack.4), channel_id=1, source_target_pairs={{0,1},{1,0},{2,3},{3,2},{4,5},{5,4},{6,7},{7,6},{8,9},{9,8},{10,11... | collective-permute-start | bytes 4718600 | tf_op jit(solution)/shard_map/ppermute | solution.py:137
  70.0 8.9 %collective-permute-start.16 = (bf16[32,4096]{1,0:T(8,128)(2,1)S(1)}, bf16[32,4096]{1,0:T(8,128)(2,1)S(1)}, u32[]{:S(2)}, u32[]{:S(2)}) collective-permute-start(bf16[32,4096]{1,0:T(8,128)(2,1)S(1)} %collective-permute-done.10.refs_4_), channel_id=1, source_target_pairs={{0,3},{1,30},{2,1},{3,4},{4,7},{5,2},{6,5},{7,8},{8,11},{9,6},{10,... | collective-permute-start | bytes 786440 | tf_op jit(solution)/shard_map/ppermute | solution.py:129
  71.9 11.2 %collective-permute-start.17 = (bf16[32,4096]{1,0:T(8,128)(2,1)S(1)}, bf16[32,4096]{1,0:T(8,128)(2,1)S(1)}, u32[]{:S(2)}, u32[]{:S(2)}) collective-permute-start(bf16[32,4096]{1,0:T(8,128)(2,1)S(1)} %collective-permute-done.11.refs_5_), channel_id=1, source_target_pairs={{0,3},{1,30},{2,1},{3,4},{4,7},{5,2},{6,5},{7,8},{8,11},{9,6},{10,... | collective-permute-start | bytes 786440 | tf_op jit(solution)/shard_map/ppermute | solution.py:131
  78.9 28.0 %collective-permute-start.14 = (bf16[128,4096]{1,0:T(8,128)(2,1)S(1)}, bf16[128,4096]{1,0:T(8,128)(2,1)S(1)}, u32[]{:S(2)}, u32[]{:S(2)}) collective-permute-start(bf16[128,4096]{1,0:T(8,128)(2,1)S(1)} %bitcast.27), channel_id=1, source_target_pairs={{0,32},{32,0},{1,33},{33,1},{2,34},{34,2},{3,35},{35,3},{4,36},{36... | collective-permute-start | bytes 3145736 | tf_op jit(solution)/shard_map/ppermute | solution.py:134
  83.1 24.9 %collective-permute-start.19 = (bf16[2,32,4096]{2,1,0:T(8,128)(2,1)S(1)}, bf16[2,32,4096]{2,1,0:T(8,128)(2,1)S(1)}, u32[]{:S(2)}, u32[]{:S(2)}) collective-permute-start(bf16[2,32,4096]{2,1,0:T(8,128)(2,1)S(1)} %stack.5.refs_0_), channel_id=1, source_target_pairs={{0,1},{1,0},{2,3},{3,2},{4,5},{5,4},{6,7},{7,6},{8,9},{9,8},{10,11... | collective-permute-start | bytes 1572872 | tf_op jit(solution)/shard_map/ppermute | solution.py:137
  85.1 22.9 %collective-permute-start.18 = (bf16[32,4096]{1,0:T(8,128)(2,1)S(1)}, bf16[32,4096]{1,0:T(8,128)(2,1)S(1)}, u32[]{:S(2)}, u32[]{:S(2)}) collective-permute-start(bf16[32,4096]{1,0:T(8,128)(2,1)S(1)} %collective-permute-done.16.refs_0_), channel_id=1, source_target_pairs={{0,3},{1,30},{2,1},{3,4},{4,7},{5,2},{6,5},{7,8},{8,11},{9,6},{10,... | collective-permute-start | bytes 786440 | tf_op jit(solution)/shard_map/ppermute | solution.py:129
  87.2 4.4 %copy-start = (bf16[1,128,4096]{2,1,0:T(8,128)(2,1)S(1)}, bf16[1,128,4096]{2,1,0:T(8,128)(2,1)}, u32[]{:S(2)}) copy-start(bf16[1,128,4096]{2,1,0:T(8,128)(2,1)} %param.7) | copy-start | bytes 3145732
  87.2 20.8 %collective-permute-start.20 = (bf16[32,4096]{1,0:T(8,128)(2,1)S(1)}, bf16[32,4096]{1,0:T(8,128)(2,1)S(1)}, u32[]{:S(2)}, u32[]{:S(2)}) collective-permute-start(bf16[32,4096]{1,0:T(8,128)(2,1)S(1)} %collective-permute-done.16.refs_0_), channel_id=1, source_target_pairs={{0,2},{1,31},{2,0},{3,5},{4,6},{5,3},{6,4},{7,9},{8,10},{9,7},{10,... | collective-permute-start | bytes 786440 | tf_op jit(solution)/shard_map/ppermute | solution.py:132

commit v6 on v5

--- a/solution.py
+++ b/solution.py
@@ -38,8 +38,24 @@
     )(*parts)
 
 
+def pair_kernel(act, back, out):
+    out[0] = act[...]
+    out[1] = back[...]
+
+
+def pair(act, back):
+    return pl.pallas_call(
+        pair_kernel,
+        out_shape=jax.ShapeDtypeStruct((2, *act.shape), act.dtype),
+        in_specs=[VMEM, VMEM],
+        out_specs=VMEM,
+        compiler_params=pltpu.CompilerParams(vmem_limit_bytes=4 * MIB),
+        name="pair",
+    )(act, back)
+
+
 def finish_kernel(height, depth, early, *refs):
-    stacks, (own_act, other_act, own_back, other_back, out, act, back) = refs[:-7], refs[-7:]
+    stacks, (own, other, out, act, back) = refs[:-5], refs[-5:]
     tcol = lax.axis_index("tcol")
     z, core = lax.shift_right_logical(tcol, 1), lax.rem(tcol, 2)
     planes = out.shape[0] // (2 * height)
@@ -65,17 +81,17 @@
             at += height
     dims = (((1,), (1,)), ((), ()))
 
-    def grams(cols, rows):
-        return [lax.dot_general(c[...], rows[...], dims, preferred_element_type=jnp.float32) for c in cols]
+    def grams(kind, rows):
+        return [lax.dot_general(c[kind], rows[...], dims, preferred_element_type=jnp.float32) for c in (own, other)]
 
-    gram_act, gram_back = grams((own_act, other_act), act), grams((own_back, other_back), back)
+    gram_act, gram_back = grams(0, act), grams(1, back)
     terms = jnp.concatenate([(a * b * (1.0 / depth)).T for a, b in zip(gram_act, gram_back)], axis=1)
     for i, shard in enumerate(late + late):
         put(terms[i * height : (i + 1) * height, :], shard, int(i >= len(late)))
 
 
 def finish(early, stacks, cols, height, planes):
-    width, depth = cols[0].shape
+    width, depth = cols[0].shape[1:]
     late = sum(s.shape[1] for s in stacks)
     return pl.pallas_call(
         functools.partial(finish_kernel, height, depth),
@@ -130,22 +146,23 @@
         if step < half:
             held[1, step] = lax.ppermute(held[1, step - 1], "tcol", along)
     last = [held[0, half], lax.ppermute(held[0, half - 1], "tcol", beside)]
-    across = [(0, 1), (1, 0)]
-    other_act = lax.ppermute(act_cols[0], "trow", across)
-    other_back = lax.ppermute(back_cols[0], "trow", across)
-    mine = [stack([held[shard] for shard in group]) for group in GROUPS]
-    given = [lax.ppermute(rows, "tcol", cores) for rows in mine]
+    own_cols = pair(act_cols[0], back_cols[0])
+    other_cols = lax.ppermute(own_cols, "trow", [(0, 1), (1, 0)])
+    mine, given = [], []
+    for i, group in enumerate(GROUPS):
+        mine.append(stack([held[shard] for shard in group]))
+        given.append(lax.ppermute(mine[i], "tcol", cores))
 
+    cols = jnp.concatenate((own_cols, other_cols), axis=1)
     early = mine[:-1] + given[:-1]
-    rows, cols = jnp.concatenate([s[0] for s in early], axis=0), jnp.concatenate((act_cols[0], other_act), axis=0)
-    gram_act = jnp.einsum("rd,cd->rc", rows, cols, preferred_element_type=jnp.float32)
-    rows, cols = jnp.concatenate([s[1] for s in early], axis=0), jnp.concatenate((back_cols[0], other_back), axis=0)
-    gram_back = jnp.einsum("rd,cd->rc", rows, cols, preferred_element_type=jnp.float32)
+    act, back = (jnp.concatenate([rows[kind] for rows in early], axis=0) for kind in range(2))
+    gram_act = jnp.einsum("rd,cd->rc", act, cols[0], preferred_element_type=jnp.float32)
+    gram_back = jnp.einsum("rd,cd->rc", back, cols[1], preferred_element_type=jnp.float32)
     terms = gram_act * gram_back / depth
     height = act_rows.shape[1]
     last = [s.reshape(2, height, depth) for s in last]
     stacks = (mine[-1], last[0], given[-1], last[1])
-    terms = finish(terms, stacks, (act_cols[0], other_act, back_cols[0], other_back), height, planes)
+    terms = finish(terms, stacks, (own_cols, other_cols), height, planes)
     got = lax.all_to_all(terms.reshape(layers, -1, terms.shape[-1]), "layer", 0, 0, tiled=True)
     return layer_sum(got)
 

time: 125 us -> 122 us (0.976)
  the two profiles are of different devices: /device:TPU:24 before, /device:TPU:1 now
where the time goes in v6:
time: 122 us; the launch traced here: 121 us
  starting transfers between devices  77.8 us (64%)
  waiting for transfers between devices  20.5 us (17%)
  blocking collectives  13.9 us (11%)
  local copies, waits for them, and re-layouts  3.11 us (3%)
  Pallas kernels  2.36 us (2%)
  matrix products  2.16 us (2%)
    ppermute x7, starting transfers between devices, local(): held[0, step] = lax.ppermute(held[0, step - 1], 'tcol', along)  30.5 us
    ppermute x6, starting transfers between devices, local(): held[1, step] = lax.ppermute(held[1, step - 1], 'tcol', along)  16.6 us
    all_to_all x1, blocking collectives, local(): lax.all_to_all(terms.reshape(layers, -1, terms.shape[-1]), 'layer', 0, 0,...  13.9 us
    ppermute x1, starting transfers between devices, local(): lax.ppermute(own, 'tcol', along)  12.5 us
    ppermute x3, starting transfers between devices, local(): given.append(lax.ppermute(mine[i], 'tcol', cores))  8.08 us
    ppermute x1, waiting for transfers between devices, local(): other_cols = lax.ppermute(own_cols, 'trow', [(0, 1), (1, 0)])  6.68 us
    ppermute x7, waiting for transfers between devices, local(): held[0, step] = lax.ppermute(held[0, step - 1], 'tcol', along)  6.64 us
    ppermute x6, waiting for transfers between devices, local(): held[1, step] = lax.ppermute(held[1, step - 1], 'tcol', along)  5.76 us
  transfers between devices with their start and end apart: 20, of which 9 were waited for; matrix products, arithmetic and copies ran while one was open for 2% of the time, Pallas kernels for 0%

profile of v6, /device:TPU:1, one launch (start us, length us, event | category | flops | bytes accessed | tf_op | source)
XLA Modules:
  0.0 121.0 jit_solution(7136359598803310552)
XLA Ops:
  0.0 1.0 pad_maximum_fusion.1.refs_0_
  1.0 12.5 %collective-permute-start = (bf16[32,4096]{1,0:T(8,128)(2,1)S(1)}, bf16[32,4096]{1,0:T(8,128)(2,1)S(1)}, u32[]{:S(2)}, u32[]{:S(2)}) collective-permute-start(bf16[32,4096]{1,0:T(8,128)(2,1)S(1)} %pad_maximum_fusion.1.refs_0_), channel_id=1, source_target_pairs={{0,3},{1,30},{2,1},{3,4},{4,7},{5,2},{6,5},{7,8},{8,11},{9,6},{10,... | collective-permute-start | bytes 786440 | tf_op jit(solution)/shard_map/ppermute | solution.py:143
  13.5 1.9 %collective-permute-start.1 = (bf16[32,4096]{1,0:T(8,128)(2,1)S(1)}, bf16[32,4096]{1,0:T(8,128)(2,1)S(1)}, u32[]{:S(2)}, u32[]{:S(2)}) collective-permute-start(bf16[32,4096]{1,0:T(8,128)(2,1)S(1)} %pad_maximum_fusion.1.refs_0_), channel_id=1, source_target_pairs={{0,30},{1,3},{2,4},{3,1},{4,2},{5,7},{6,8},{7,5},{8,6},{9,11},{10,... | collective-permute-start | bytes 786440 | tf_op jit(solution)/shard_map/ppermute | solution.py:143
  15.4 1.4 %collective-permute-done.refs_1_ = bf16[32,4096]{1,0:T(8,128)(2,1)S(1)} collective-permute-done((bf16[32,4096]{1,0:T(8,128)(2,1)S(1)}, bf16[32,4096]{1,0:T(8,128)(2,1)S(1)}, u32[]{:S(2)}, u32[]{:S(2)}) %collective-permute-start) | collective-permute-done | bytes 262176 | tf_op jit(solution)/shard_map/ppermute | solution.py:143
  16.8 5.6 %collective-permute-start.2 = (bf16[32,4096]{1,0:T(8,128)(2,1)S(1)}, bf16[32,4096]{1,0:T(8,128)(2,1)S(1)}, u32[]{:S(2)}, u32[]{:S(2)}) collective-permute-start(bf16[32,4096]{1,0:T(8,128)(2,1)S(1)} %collective-permute-done.refs_1_), channel_id=1, source_target_pairs={{0,3},{1,30},{2,1},{3,4},{4,7},{5,2},{6,5},{7,8},{8,11},{9,6},{10,... | collective-permute-start | bytes 786440 | tf_op jit(solution)/shard_map/ppermute | solution.py:145
  22.4 2.9 %collective-permute-start.3 = (bf16[32,4096]{1,0:T(8,128)(2,1)S(1)}, bf16[32,4096]{1,0:T(8,128)(2,1)S(1)}, u32[]{:S(2)}, u32[]{:S(2)}) collective-permute-start(bf16[32,4096]{1,0:T(8,128)(2,1)S(1)} %collective-permute-done.1.refs_2_), channel_id=1, source_target_pairs={{0,3},{1,30},{2,1},{3,4},{4,7},{5,2},{6,5},{7,8},{8,11},{9,6},{10,... | collective-permute-start | bytes 786440 | tf_op jit(solution)/shard_map/ppermute | solution.py:147
  25.3 0.4 collective-permute-done.2.refs_3_
  25.7 5.6 %collective-permute-start.4 = (bf16[32,4096]{1,0:T(8,128)(2,1)S(1)}, bf16[32,4096]{1,0:T(8,128)(2,1)S(1)}, u32[]{:S(2)}, u32[]{:S(2)}) collective-permute-start(bf16[32,4096]{1,0:T(8,128)(2,1)S(1)} %collective-permute-done.2.refs_3_), channel_id=1, source_target_pairs={{0,3},{1,30},{2,1},{3,4},{4,7},{5,2},{6,5},{7,8},{8,11},{9,6},{10,... | collective-permute-start | bytes 786440 | tf_op jit(solution)/shard_map/ppermute | solution.py:145
  31.3 0.0 collective-permute-done.3.refs_4_
  31.3 2.9 %collective-permute-start.5 = (bf16[32,4096]{1,0:T(8,128)(2,1)S(1)}, bf16[32,4096]{1,0:T(8,128)(2,1)S(1)}, u32[]{:S(2)}, u32[]{:S(2)}) collective-permute-start(bf16[32,4096]{1,0:T(8,128)(2,1)S(1)} %collective-permute-done.3.refs_4_), channel_id=1, source_target_pairs={{0,3},{1,30},{2,1},{3,4},{4,7},{5,2},{6,5},{7,8},{8,11},{9,6},{10,... | collective-permute-start | bytes 786440 | tf_op jit(solution)/shard_map/ppermute | solution.py:147
  34.2 0.4 collective-permute-done.4.refs_5_
  34.6 5.6 %collective-permute-start.6 = (bf16[32,4096]{1,0:T(8,128)(2,1)S(1)}, bf16[32,4096]{1,0:T(8,128)(2,1)S(1)}, u32[]{:S(2)}, u32[]{:S(2)}) collective-permute-start(bf16[32,4096]{1,0:T(8,128)(2,1)S(1)} %collective-permute-done.4.refs_5_), channel_id=1, source_target_pairs={{0,3},{1,30},{2,1},{3,4},{4,7},{5,2},{6,5},{7,8},{8,11},{9,6},{10,... | collective-permute-start | bytes 786440 | tf_op jit(solution)/shard_map/ppermute | solution.py:145
  40.2 0.0 collective-permute-done.5.refs_6_
  40.2 2.9 %collective-permute-start.7 = (bf16[32,4096]{1,0:T(8,128)(2,1)S(1)}, bf16[32,4096]{1,0:T(8,128)(2,1)S(1)}, u32[]{:S(2)}, u32[]{:S(2)}) collective-permute-start(bf16[32,4096]{1,0:T(8,128)(2,1)S(1)} %collective-permute-done.5.refs_6_), channel_id=1, source_target_pairs={{0,3},{1,30},{2,1},{3,4},{4,7},{5,2},{6,5},{7,8},{8,11},{9,6},{10,... | collective-permute-start | bytes 786440 | tf_op jit(solution)/shard_map/ppermute | solution.py:147
  43.1 0.4 collective-permute-done.6.refs_0_
  43.5 5.6 %collective-permute-start.8 = (bf16[32,4096]{1,0:T(8,128)(2,1)S(1)}, bf16[32,4096]{1,0:T(8,128)(2,1)S(1)}, u32[]{:S(2)}, u32[]{:S(2)}) collective-permute-start(bf16[32,4096]{1,0:T(8,128)(2,1)S(1)} %collective-permute-done.6.refs_0_), channel_id=1, source_target_pairs={{0,3},{1,30},{2,1},{3,4},{4,7},{5,2},{6,5},{7,8},{8,11},{9,6},{10,... | collective-permute-start | bytes 786440 | tf_op jit(solution)/shard_map/ppermute | solution.py:145
  49.1 2.9 %collective-permute-start.9 = (bf16[32,4096]{1,0:T(8,128)(2,1)S(1)}, bf16[32,4096]{1,0:T(8,128)(2,1)S(1)}, u32[]{:S(2)}, u32[]{:S(2)}) collective-permute-start(bf16[32,4096]{1,0:T(8,128)(2,1)S(1)} %collective-permute-done.7.refs_1_), channel_id=1, source_target_pairs={{0,3},{1,30},{2,1},{3,4},{4,7},{5,2},{6,5},{7,8},{8,11},{9,6},{10,... | collective-permute-start | bytes 786440 | tf_op jit(solution)/shard_map/ppermute | solution.py:147
  52.0 0.0 copy-start
  52.0 1.2 %copy-done = bf16[1,128,4096]{2,1,0:T(8,128)(2,1)S(1)} copy-done((bf16[1,128,4096]{2,1,0:T(8,128)(2,1)S(1)}, bf16[1,128,4096]{2,1,0:T(8,128)(2,1)}, u32[]{:S(2)}) %copy-start) | copy-done | bytes 1048600
  53.2 1.2 %copy-done.1 = bf16[1,128,4096]{2,1,0:T(8,128)(2,1)S(1)} copy-done((bf16[1,128,4096]{2,1,0:T(8,128)(2,1)S(1)}, bf16[1,128,4096]{2,1,0:T(8,128)(2,1)}, u32[]{:S(2)}) %copy-start.1) | copy-done | bytes 1048600
  54.5 0.1 pair.1.refs_4_
  54.6 4.8 %collective-permute-start.14 = (bf16[2,128,4096]{2,1,0:T(8,128)(2,1)S(1)}, bf16[2,128,4096]{2,1,0:T(8,128)(2,1)S(1)}, u32[]{:S(2)}, u32[]{:S(2)}) collective-permute-start(bf16[2,128,4096]{2,1,0:T(8,128)(2,1)S(1)} %pair.1.refs_4_), channel_id=1, source_target_pairs={{0,32},{32,0},{1,33},{33,1},{2,34},{34,2},{3,35},{35,3},{4,36},{36... | collective-permute-start | bytes 6291464 | tf_op jit(solution)/shard_map/ppermute | solution.py:150
  59.4 0.1 stack.3
  59.6 1.9 %collective-permute-start.12 = (bf16[2,112,4096]{2,1,0:T(8,128)(2,1)S(1)}, bf16[2,112,4096]{2,1,0:T(8,128)(2,1)S(1)}, u32[]{:S(2)}, u32[]{:S(2)}) collective-permute-start(bf16[2,112,4096]{2,1,0:T(8,128)(2,1)S(1)} %stack.3), channel_id=1, source_target_pairs={{0,1},{1,0},{2,3},{3,2},{4,5},{5,4},{6,7},{7,6},{8,9},{9,8},{10,11... | collective-permute-start | bytes 5505032 | tf_op jit(solution)/shard_map/ppermute | solution.py:154
  61.5 0.0 collective-permute-done.8.refs_2_
  61.5 2.2 %collective-permute-start.10 = (bf16[32,4096]{1,0:T(8,128)(2,1)S(1)}, bf16[32,4096]{1,0:T(8,128)(2,1)S(1)}, u32[]{:S(2)}, u32[]{:S(2)}) collective-permute-start(bf16[32,4096]{1,0:T(8,128)(2,1)S(1)} %collective-permute-done.8.refs_2_), channel_id=1, source_target_pairs={{0,3},{1,30},{2,1},{3,4},{4,7},{5,2},{6,5},{7,8},{8,11},{9,6},{10,... | collective-permute-start | bytes 786440 | tf_op jit(solution)/shard_map/ppermute | solution.py:145
  63.7 2.5 %collective-permute-start.11 = (bf16[32,4096]{1,0:T(8,128)(2,1)S(1)}, bf16[32,4096]{1,0:T(8,128)(2,1)S(1)}, u32[]{:S(2)}, u32[]{:S(2)}) collective-permute-start(bf16[32,4096]{1,0:T(8,128)(2,1)S(1)} %collective-permute-done.9.refs_3_), channel_id=1, source_target_pairs={{0,3},{1,30},{2,1},{3,4},{4,7},{5,2},{6,5},{7,8},{8,11},{9,6},{10,... | collective-permute-start | bytes 786440 | tf_op jit(solution)/shard_map/ppermute | solution.py:147
  66.2 0.2 slice_bitcast_fusion.3
  66.4 3.1 %collective-permute-done.10.refs_4_ = bf16[32,4096]{1,0:T(8,128)(2,1)S(1)} collective-permute-done((bf16[32,4096]{1,0:T(8,128)(2,1)S(1)}, bf16[32,4096]{1,0:T(8,128)(2,1)S(1)}, u32[]{:S(2)}, u32[]{:S(2)}) %collective-permute-start.10) | collective-permute-done | bytes 262176 | tf_op jit(solution)/shard_map/ppermute | solution.py:145
  69.5 2.8 %collective-permute-done.11.refs_5_ = bf16[32,4096]{1,0:T(8,128)(2,1)S(1)} collective-permute-done((bf16[32,4096]{1,0:T(8,128)(2,1)S(1)}, bf16[32,4096]{1,0:T(8,128)(2,1)S(1)}, u32[]{:S(2)}, u32[]{:S(2)}) %collective-permute-start.11) | collective-permute-done | bytes 262176 | tf_op jit(solution)/shard_map/ppermute | solution.py:147
  72.3 0.1 stack.4
  72.4 3.5 %collective-permute-start.13 = (bf16[2,96,4096]{2,1,0:T(8,128)(2,1)S(1)}, bf16[2,96,4096]{2,1,0:T(8,128)(2,1)S(1)}, u32[]{:S(2)}, u32[]{:S(2)}) collective-permute-start(bf16[2,96,4096]{2,1,0:T(8,128)(2,1)S(1)} %stack.4), channel_id=1, source_target_pairs={{0,1},{1,0},{2,3},{3,2},{4,5},{5,4},{6,7},{7,6},{8,9},{9,8},{10,11... | collective-permute-start | bytes 4718600 | tf_op jit(solution)/shard_map/ppermute | solution.py:154
  75.9 2.9 %collective-permute-start.15 = (bf16[32,4096]{1,0:T(8,128)(2,1)S(1)}, bf16[32,4096]{1,0:T(8,128)(2,1)S(1)}, u32[]{:S(2)}, u32[]{:S(2)}) collective-permute-start(bf16[32,4096]{1,0:T(8,128)(2,1)S(1)} %collective-permute-done.10.refs_4_), channel_id=1, source_target_pairs={{0,3},{1,30},{2,1},{3,4},{4,7},{5,2},{6,5},{7,8},{8,11},{9,6},{10,... | collective-permute-start | bytes 786440 | tf_op jit(solution)/shard_map/ppermute | solution.py:145
  78.8 2.4 %collective-permute-start.16 = (bf16[32,4096]{1,0:T(8,128)(2,1)S(1)}, bf16[32,4096]{1,0:T(8,128)(2,1)S(1)}, u32[]{:S(2)}, u32[]{:S(2)}) collective-permute-start(bf16[32,4096]{1,0:T(8,128)(2,1)S(1)} %collective-permute-done.11.refs_5_), channel_id=1, source_target_pairs={{0,3},{1,30},{2,1},{3,4},{4,7},{5,2},{6,5},{7,8},{8,11},{9,6},{10,... | collective-permute-start | bytes 786440 | tf_op jit(solution)/shard_map/ppermute | solution.py:147
  81.2 0.1 slice_bitcast_fusion.7
  81.4 2.5 %collective-permute-done.15.refs_0_ = bf16[32,4096]{1,0:T(8,128)(2,1)S(1)} collective-permute-done((bf16[32,4096]{1,0:T(8,128)(2,1)S(1)}, bf16[32,4096]{1,0:T(8,128)(2,1)S(1)}, u32[]{:S(2)}, u32[]{:S(2)}) %collective-permute-start.15) | collective-permute-done | bytes 262176 | tf_op jit(solution)/shard_map/ppermute | solution.py:145
  83.8 2.9 %collective-permute-done.16.refs_1_ = bf16[32,4096]{1,0:T(8,128)(2,1)S(1)} collective-permute-done((bf16[32,4096]{1,0:T(8,128)(2,1)S(1)}, bf16[32,4096]{1,0:T(8,128)(2,1)S(1)}, u32[]{:S(2)}, u32[]{:S(2)}) %collective-permute-start.16) | collective-permute-done | bytes 262176 | tf_op jit(solution)/shard_map/ppermute | solution.py:147
  86.8 2.7 %collective-permute-start.18 = (bf16[2,32,4096]{2,1,0:T(8,128)(2,1)S(1)}, bf16[2,32,4096]{2,1,0:T(8,128)(2,1)S(1)}, u32[]{:S(2)}, u32[]{:S(2)}) collective-permute-start(bf16[2,32,4096]{2,1,0:T(8,128)(2,1)S(1)} %stack.5.refs_0_), channel_id=1, source_target_pairs={{0,1},{1,0},{2,3},{3,2},{4,5},{5,4},{6,7},{7,6},{8,9},{9,8},{10,11... | collective-permute-start | bytes 1572872 | tf_op jit(solution)/shard_map/ppermute | solution.py:154
  89.5 3.1 %collective-permute-start.17 = (bf16[32,4096]{1,0:T(8,128)(2,1)S(1)}, bf16[32,4096]{1,0:T(8,128)(2,1)S(1)}, u32[]{:S(2)}, u32[]{:S(2)}) collective-permute-start(bf16[32,4096]{1,0:T(8,128)(2,1)S(1)} %collective-permute-done.15.refs_0_), channel_id=1, source_target_pairs={{0,3},{1,30},{2,1},{3,4},{4,7},{5,2},{6,5},{7,8},{8,11},{9,6},{10,... | collective-permute-start | bytes 786440 | tf_op jit(solution)/shard_map/ppermute | solution.py:145
  92.6 3.3 %collective-permute-start.19 = (bf16[32,4096]{1,0:T(8,128)(2,1)S(1)}, bf16[32,4096]{1,0:T(8,128)(2,1)S(1)}, u32[]{:S(2)}, u32[]{:S(2)}) collective-permute-start(bf16[32,4096]{1,0:T(8,128)(2,1)S(1)} %collective-permute-done.15.refs_0_), channel_id=1, source_target_pairs={{0,2},{1,31},{2,0},{3,5},{4,6},{5,3},{6,4},{7,9},{8,10},{9,7},{10,... | collective-permute-start | bytes 786440 | tf_op jit(solution)/shard_map/ppermute | solution.py:148
  95.9 0.2 slice_bitcast_fusion.2
  96.2 0.1 slice_bitcast_fusion.6
  96.3 6.7 %collective-permute-done.14.refs_5_ = bf16[2,128,4096]{2,1,0:T(8,128)(2,1)S(1)} collective-permute-done((bf16[2,128,4096]{2,1,0:T(8,128)(2,1)S(1)}, bf16[2,128,4096]{2,1,0:T(8,128)(2,1)S(1)}, u32[]{:S(2)}, u32[]{:S(2)}) %collective-permute-start.14) | collective-permute-done | bytes 2097184 | tf_op jit(solution)/shard_map/ppermute | solution.py:150
  103.0 1.1 fusion.8
  104.1 1.1 fusion.27.early
  105.2 1.3 %finish.1 = f32[512,256]{1,0:T(8,128)S(1)} custom-call(f32[416,256]{1,0:T(8,128)S(1)} %fusion.27.early, bf16[2,32,4096]{2,1,0:T(8,128)(2,1)S(1)} %stack.5.refs_0_, bf16[2,16,4096]{2,1,0:T(8,128)(2,1)S(1)} %bitcast.36, bf16[2,32,4096]{2,1,0:T(8,128)(2,1)S(1)} %collective-permute-done.18.refs_2_, bf16[2,16,4096]{2,1,0:T(8,128)(2,1)S(1)} %bitcast.37, ...), custom_call_target="tpu_custom_call" | custom-call | flops 402653184 | tf_op jit(solution)/shard_map/finish/pallas_call | solution.py:96
  106.5 13.9 %all_to_all.5.got = f32[8,64,256]{2,1,0:T(8,128)S(1)} all-to-all(f32[8,64,256]{2,1,0:T(8,128)S(1)} %bitcast.33), channel_id=1, replica_groups=mesh['layer'=8,'trow'=2,'tcol'=32] {'layer'}, dimensions={0} | all-to-all | bytes 1048576 | tf_op jit(solution)/shard_map/all_to_all | solution.py:166
  120.4 0.7 layer_sum.1
  (10 shorter events, 0.1 us)
Async XLA Ops:
  1.0 15.8 %collective-permute-start = (bf16[32,4096]{1,0:T(8,128)(2,1)S(1)}, bf16[32,4096]{1,0:T(8,128)(2,1)S(1)}, u32[]{:S(2)}, u32[]{:S(2)}) collective-permute-start(bf16[32,4096]{1,0:T(8,128)(2,1)S(1)} %pad_maximum_fusion.1.refs_0_), channel_id=1, source_target_pairs={{0,3},{1,30},{2,1},{3,4},{4,7},{5,2},{6,5},{7,8},{8,11},{9,6},{10,... | collective-permute-start | bytes 786440 | tf_op jit(solution)/shard_map/ppermute | solution.py:143
  13.5 8.9 %collective-permute-start.1 = (bf16[32,4096]{1,0:T(8,128)(2,1)S(1)}, bf16[32,4096]{1,0:T(8,128)(2,1)S(1)}, u32[]{:S(2)}, u32[]{:S(2)}) collective-permute-start(bf16[32,4096]{1,0:T(8,128)(2,1)S(1)} %pad_maximum_fusion.1.refs_0_), channel_id=1, source_target_pairs={{0,30},{1,3},{2,4},{3,1},{4,2},{5,7},{6,8},{7,5},{8,6},{9,11},{10,... | collective-permute-start | bytes 786440 | tf_op jit(solution)/shard_map/ppermute | solution.py:143
  16.8 8.9 %collective-permute-start.2 = (bf16[32,4096]{1,0:T(8,128)(2,1)S(1)}, bf16[32,4096]{1,0:T(8,128)(2,1)S(1)}, u32[]{:S(2)}, u32[]{:S(2)}) collective-permute-start(bf16[32,4096]{1,0:T(8,128)(2,1)S(1)} %collective-permute-done.refs_1_), channel_id=1, source_target_pairs={{0,3},{1,30},{2,1},{3,4},{4,7},{5,2},{6,5},{7,8},{8,11},{9,6},{10,... | collective-permute-start | bytes 786440 | tf_op jit(solution)/shard_map/ppermute | solution.py:145
  22.4 8.9 %collective-permute-start.3 = (bf16[32,4096]{1,0:T(8,128)(2,1)S(1)}, bf16[32,4096]{1,0:T(8,128)(2,1)S(1)}, u32[]{:S(2)}, u32[]{:S(2)}) collective-permute-start(bf16[32,4096]{1,0:T(8,128)(2,1)S(1)} %collective-permute-done.1.refs_2_), channel_id=1, source_target_pairs={{0,3},{1,30},{2,1},{3,4},{4,7},{5,2},{6,5},{7,8},{8,11},{9,6},{10,... | collective-permute-start | bytes 786440 | tf_op jit(solution)/shard_map/ppermute | solution.py:147
  25.7 8.9 %collective-permute-start.4 = (bf16[32,4096]{1,0:T(8,128)(2,1)S(1)}, bf16[32,4096]{1,0:T(8,128)(2,1)S(1)}, u32[]{:S(2)}, u32[]{:S(2)}) collective-permute-start(bf16[32,4096]{1,0:T(8,128)(2,1)S(1)} %collective-permute-done.2.refs_3_), channel_id=1, source_target_pairs={{0,3},{1,30},{2,1},{3,4},{4,7},{5,2},{6,5},{7,8},{8,11},{9,6},{10,... | collective-permute-start | bytes 786440 | tf_op jit(solution)/shard_map/ppermute | solution.py:145
  31.3 8.9 %collective-permute-start.5 = (bf16[32,4096]{1,0:T(8,128)(2,1)S(1)}, bf16[32,4096]{1,0:T(8,128)(2,1)S(1)}, u32[]{:S(2)}, u32[]{:S(2)}) collective-permute-start(bf16[32,4096]{1,0:T(8,128)(2,1)S(1)} %collective-permute-done.3.refs_4_), channel_id=1, source_target_pairs={{0,3},{1,30},{2,1},{3,4},{4,7},{5,2},{6,5},{7,8},{8,11},{9,6},{10,... | collective-permute-start | bytes 786440 | tf_op jit(solution)/shard_map/ppermute | solution.py:147
  34.6 8.9 %collective-permute-start.6 = (bf16[32,4096]{1,0:T(8,128)(2,1)S(1)}, bf16[32,4096]{1,0:T(8,128)(2,1)S(1)}, u32[]{:S(2)}, u32[]{:S(2)}) collective-permute-start(bf16[32,4096]{1,0:T(8,128)(2,1)S(1)} %collective-permute-done.4.refs_5_), channel_id=1, source_target_pairs={{0,3},{1,30},{2,1},{3,4},{4,7},{5,2},{6,5},{7,8},{8,11},{9,6},{10,... | collective-permute-start | bytes 786440 | tf_op jit(solution)/shard_map/ppermute | solution.py:145
  40.2 8.9 %collective-permute-start.7 = (bf16[32,4096]{1,0:T(8,128)(2,1)S(1)}, bf16[32,4096]{1,0:T(8,128)(2,1)S(1)}, u32[]{:S(2)}, u32[]{:S(2)}) collective-permute-start(bf16[32,4096]{1,0:T(8,128)(2,1)S(1)} %collective-permute-done.5.refs_6_), channel_id=1, source_target_pairs={{0,3},{1,30},{2,1},{3,4},{4,7},{5,2},{6,5},{7,8},{8,11},{9,6},{10,... | collective-permute-start | bytes 786440 | tf_op jit(solution)/shard_map/ppermute | solution.py:147
  43.5 18.0 %collective-permute-start.8 = (bf16[32,4096]{1,0:T(8,128)(2,1)S(1)}, bf16[32,4096]{1,0:T(8,128)(2,1)S(1)}, u32[]{:S(2)}, u32[]{:S(2)}) collective-permute-start(bf16[32,4096]{1,0:T(8,128)(2,1)S(1)} %collective-permute-done.6.refs_0_), channel_id=1, source_target_pairs={{0,3},{1,30},{2,1},{3,4},{4,7},{5,2},{6,5},{7,8},{8,11},{9,6},{10,... | collective-permute-start | bytes 786440 | tf_op jit(solution)/shard_map/ppermute | solution.py:145
  49.1 14.6 %collective-permute-start.9 = (bf16[32,4096]{1,0:T(8,128)(2,1)S(1)}, bf16[32,4096]{1,0:T(8,128)(2,1)S(1)}, u32[]{:S(2)}, u32[]{:S(2)}) collective-permute-start(bf16[32,4096]{1,0:T(8,128)(2,1)S(1)} %collective-permute-done.7.refs_1_), channel_id=1, source_target_pairs={{0,3},{1,30},{2,1},{3,4},{4,7},{5,2},{6,5},{7,8},{8,11},{9,6},{10,... | collective-permute-start | bytes 786440 | tf_op jit(solution)/shard_map/ppermute | solution.py:147
  52.0 1.2 %copy-start = (bf16[1,128,4096]{2,1,0:T(8,128)(2,1)S(1)}, bf16[1,128,4096]{2,1,0:T(8,128)(2,1)}, u32[]{:S(2)}) copy-start(bf16[1,128,4096]{2,1,0:T(8,128)(2,1)} %param.6) | copy-start | bytes 3145732
  53.2 1.2 %copy-start.1 = (bf16[1,128,4096]{2,1,0:T(8,128)(2,1)S(1)}, bf16[1,128,4096]{2,1,0:T(8,128)(2,1)}, u32[]{:S(2)}) copy-start(bf16[1,128,4096]{2,1,0:T(8,128)(2,1)} %param.7) | copy-start | bytes 3145732
  54.6 48.4 %collective-permute-start.14 = (bf16[2,128,4096]{2,1,0:T(8,128)(2,1)S(1)}, bf16[2,128,4096]{2,1,0:T(8,128)(2,1)S(1)}, u32[]{:S(2)}, u32[]{:S(2)}) collective-permute-start(bf16[2,128,4096]{2,1,0:T(8,128)(2,1)S(1)} %pair.1.refs_4_), channel_id=1, source_target_pairs={{0,32},{32,0},{1,33},{33,1},{2,34},{34,2},{3,35},{35,3},{4,36},{36... | collective-permute-start | bytes 6291464 | tf_op jit(solution)/shard_map/ppermute | solution.py:150
  59.6 33.0 %collective-permute-start.12 = (bf16[2,112,4096]{2,1,0:T(8,128)(2,1)S(1)}, bf16[2,112,4096]{2,1,0:T(8,128)(2,1)S(1)}, u32[]{:S(2)}, u32[]{:S(2)}) collective-permute-start(bf16[2,112,4096]{2,1,0:T(8,128)(2,1)S(1)} %stack.3), channel_id=1, source_target_pairs={{0,1},{1,0},{2,3},{3,2},{4,5},{5,4},{6,7},{7,6},{8,9},{9,8},{10,11... | collective-permute-start | bytes 5505032 | tf_op jit(solution)/shard_map/ppermute | solution.py:154
  61.5 8.0 %collective-permute-start.10 = (bf16[32,4096]{1,0:T(8,128)(2,1)S(1)}, bf16[32,4096]{1,0:T(8,128)(2,1)S(1)}, u32[]{:S(2)}, u32[]{:S(2)}) collective-permute-start(bf16[32,4096]{1,0:T(8,128)(2,1)S(1)} %collective-permute-done.8.refs_2_), channel_id=1, source_target_pairs={{0,3},{1,30},{2,1},{3,4},{4,7},{5,2},{6,5},{7,8},{8,11},{9,6},{10,... | collective-permute-start | bytes 786440 | tf_op jit(solution)/shard_map/ppermute | solution.py:145
  63.7 8.6 %collective-permute-start.11 = (bf16[32,4096]{1,0:T(8,128)(2,1)S(1)}, bf16[32,4096]{1,0:T(8,128)(2,1)S(1)}, u32[]{:S(2)}, u32[]{:S(2)}) collective-permute-start(bf16[32,4096]{1,0:T(8,128)(2,1)S(1)} %collective-permute-done.9.refs_3_), channel_id=1, source_target_pairs={{0,3},{1,30},{2,1},{3,4},{4,7},{5,2},{6,5},{7,8},{8,11},{9,6},{10,... | collective-permute-start | bytes 786440 | tf_op jit(solution)/shard_map/ppermute | solution.py:147
  72.4 23.8 %collective-permute-start.13 = (bf16[2,96,4096]{2,1,0:T(8,128)(2,1)S(1)}, bf16[2,96,4096]{2,1,0:T(8,128)(2,1)S(1)}, u32[]{:S(2)}, u32[]{:S(2)}) collective-permute-start(bf16[2,96,4096]{2,1,0:T(8,128)(2,1)S(1)} %stack.4), channel_id=1, source_target_pairs={{0,1},{1,0},{2,3},{3,2},{4,5},{5,4},{6,7},{7,6},{8,9},{9,8},{10,11... | collective-permute-start | bytes 4718600 | tf_op jit(solution)/shard_map/ppermute | solution.py:154
  75.9 8.0 %collective-permute-start.15 = (bf16[32,4096]{1,0:T(8,128)(2,1)S(1)}, bf16[32,4096]{1,0:T(8,128)(2,1)S(1)}, u32[]{:S(2)}, u32[]{:S(2)}) collective-permute-start(bf16[32,4096]{1,0:T(8,128)(2,1)S(1)} %collective-permute-done.10.refs_4_), channel_id=1, source_target_pairs={{0,3},{1,30},{2,1},{3,4},{4,7},{5,2},{6,5},{7,8},{8,11},{9,6},{10,... | collective-permute-start | bytes 786440 | tf_op jit(solution)/shard_map/ppermute | solution.py:145
  78.8 8.0 %collective-permute-start.16 = (bf16[32,4096]{1,0:T(8,128)(2,1)S(1)}, bf16[32,4096]{1,0:T(8,128)(2,1)S(1)}, u32[]{:S(2)}, u32[]{:S(2)}) collective-permute-start(bf16[32,4096]{1,0:T(8,128)(2,1)S(1)} %collective-permute-done.11.refs_5_), channel_id=1, source_target_pairs={{0,3},{1,30},{2,1},{3,4},{4,7},{5,2},{6,5},{7,8},{8,11},{9,6},{10,... | collective-permute-start | bytes 786440 | tf_op jit(solution)/shard_map/ppermute | solution.py:147
  86.8 18.4 %collective-permute-start.18 = (bf16[2,32,4096]{2,1,0:T(8,128)(2,1)S(1)}, bf16[2,32,4096]{2,1,0:T(8,128)(2,1)S(1)}, u32[]{:S(2)}, u32[]{:S(2)}) collective-permute-start(bf16[2,32,4096]{2,1,0:T(8,128)(2,1)S(1)} %stack.5.refs_0_), channel_id=1, source_target_pairs={{0,1},{1,0},{2,3},{3,2},{4,5},{5,4},{6,7},{7,6},{8,9},{9,8},{10,11... | collective-permute-start | bytes 1572872 | tf_op jit(solution)/shard_map/ppermute | solution.py:154
  89.5 15.6 %collective-permute-start.17 = (bf16[32,4096]{1,0:T(8,128)(2,1)S(1)}, bf16[32,4096]{1,0:T(8,128)(2,1)S(1)}, u32[]{:S(2)}, u32[]{:S(2)}) collective-permute-start(bf16[32,4096]{1,0:T(8,128)(2,1)S(1)} %collective-permute-done.15.refs_0_), channel_id=1, source_target_pairs={{0,3},{1,30},{2,1},{3,4},{4,7},{5,2},{6,5},{7,8},{8,11},{9,6},{10,... | collective-permute-start | bytes 786440 | tf_op jit(solution)/shard_map/ppermute | solution.py:145
  92.6 12.6 %collective-permute-start.19 = (bf16[32,4096]{1,0:T(8,128)(2,1)S(1)}, bf16[32,4096]{1,0:T(8,128)(2,1)S(1)}, u32[]{:S(2)}, u32[]{:S(2)}) collective-permute-start(bf16[32,4096]{1,0:T(8,128)(2,1)S(1)} %collective-permute-done.15.refs_0_), channel_id=1, source_target_pairs={{0,2},{1,31},{2,0},{3,5},{4,6},{5,3},{6,4},{7,9},{8,10},{9,7},{10,... | collective-permute-start | bytes 786440 | tf_op jit(solution)/shard_map/ppermute | solution.py:148

commit v7 on v5

--- a/solution.py
+++ b/solution.py
@@ -12,8 +12,8 @@
 VMEM = pl.BlockSpec(memory_space=pltpu.VMEM)
 GROUPS = (
     ((0, 0), (0, 1), (1, 1), (0, 2), (1, 2), (0, 3), (1, 3)),
-    ((0, 4), (1, 4), (0, 5), (1, 5), (0, 6), (1, 6)),
-    ((0, 7), (1, 7)),
+    ((0, 4), (1, 4), (0, 5), (1, 5)),
+    ((0, 6), (1, 6), (0, 7), (1, 7)),
 )
 
 
@@ -39,7 +39,8 @@
 
 
 def finish_kernel(height, depth, early, *refs):
-    stacks, (own_act, other_act, own_back, other_back, out, act, back) = refs[:-7], refs[-7:]
+    stacks = refs[:-7]
+    own_act, other_act, own_back, other_back, out, act, back = refs[-7:]
     tcol = lax.axis_index("tcol")
     z, core = lax.shift_right_logical(tcol, 1), lax.rem(tcol, 2)
     planes = out.shape[0] // (2 * height)
@@ -133,14 +134,17 @@
     across = [(0, 1), (1, 0)]
     other_act = lax.ppermute(act_cols[0], "trow", across)
     other_back = lax.ppermute(back_cols[0], "trow", across)
-    mine = [stack([held[shard] for shard in group]) for group in GROUPS]
-    given = [lax.ppermute(rows, "tcol", cores) for rows in mine]
+    mine, given = [], []
+    for i, group in enumerate(GROUPS):
+        mine.append(stack([held[shard] for shard in group]))
+        given.append(lax.ppermute(mine[i], "tcol", cores))
 
+    cols_act = jnp.concatenate((act_cols[0], other_act), axis=0)
+    cols_back = jnp.concatenate((back_cols[0], other_back), axis=0)
     early = mine[:-1] + given[:-1]
-    rows, cols = jnp.concatenate([s[0] for s in early], axis=0), jnp.concatenate((act_cols[0], other_act), axis=0)
-    gram_act = jnp.einsum("rd,cd->rc", rows, cols, preferred_element_type=jnp.float32)
-    rows, cols = jnp.concatenate([s[1] for s in early], axis=0), jnp.concatenate((back_cols[0], other_back), axis=0)
-    gram_back = jnp.einsum("rd,cd->rc", rows, cols, preferred_element_type=jnp.float32)
+    act, back = (jnp.concatenate([rows[kind] for rows in early], axis=0) for kind in range(2))
+    gram_act = jnp.einsum("rd,cd->rc", act, cols_act, preferred_element_type=jnp.float32)
+    gram_back = jnp.einsum("rd,cd->rc", back, cols_back, preferred_element_type=jnp.float32)
     terms = gram_act * gram_back / depth
     height = act_rows.shape[1]
     last = [s.reshape(2, height, depth) for s in last]

time: 125 us -> 122 us (0.976)
  the two profiles are of different devices: /device:TPU:24 before, /device:TPU:32 now
where the time goes in v7:
time: 122 us; the launch traced here: 121 us
  starting transfers between devices  78.8 us (65%)
  waiting for transfers between devices  22.2 us (18%)
  blocking collectives  13.8 us (11%)
  Pallas kernels  2.74 us (2%)
  matrix products  1.89 us (2%)
    ppermute x7, starting transfers between devices, local(): held[0, step] = lax.ppermute(held[0, step - 1], 'tcol', along)  28.9 us
    ppermute x6, starting transfers between devices, local(): held[1, step] = lax.ppermute(held[1, step - 1], 'tcol', along)  26 us
    ppermute x1, waiting for transfers between devices, local(): other_act = lax.ppermute(act_cols[0], 'trow', across)  15.5 us
    all_to_all x1, blocking collectives, local(): lax.all_to_all(terms.reshape(layers, -1, terms.shape[-1]), 'layer', 0, 0,...  13.8 us
    ppermute x3, starting transfers between devices, local(): given.append(lax.ppermute(mine[i], 'tcol', cores))  6.78 us
    ppermute x1, starting transfers between devices, local(): lax.ppermute(own, 'tcol', aslant)  5.17 us
    ppermute x1, starting transfers between devices, local(): other_back = lax.ppermute(back_cols[0], 'trow', across)  5.1 us
    ppermute x7, waiting for transfers between devices, local(): held[0, step] = lax.ppermute(held[0, step - 1], 'tcol', along)  4.24 us
  transfers between devices with their start and end apart: 21, of which 8 were waited for; matrix products, arithmetic and copies ran while one was open for 2% of the time, Pallas kernels for 0%

profile of v7, /device:TPU:32, one launch (start us, length us, event | category | flops | bytes accessed | tf_op | source)
XLA Modules:
  0.0 121.1 jit_solution(16032856019863960208)
XLA Ops:
  0.0 1.0 pad_maximum_fusion.refs_0_
  1.0 1.9 %collective-permute-start = (bf16[32,4096]{1,0:T(8,128)(2,1)S(1)}, bf16[32,4096]{1,0:T(8,128)(2,1)S(1)}, u32[]{:S(2)}, u32[]{:S(2)}) collective-permute-start(bf16[32,4096]{1,0:T(8,128)(2,1)S(1)} %pad_maximum_fusion.refs_0_), channel_id=1, source_target_pairs={{0,3},{1,30},{2,1},{3,4},{4,7},{5,2},{6,5},{7,8},{8,11},{9,6},{10,... | collective-permute-start | bytes 786440 | tf_op jit(solution)/shard_map/ppermute | solution.py:128
  2.9 5.2 %collective-permute-start.1 = (bf16[32,4096]{1,0:T(8,128)(2,1)S(1)}, bf16[32,4096]{1,0:T(8,128)(2,1)S(1)}, u32[]{:S(2)}, u32[]{:S(2)}) collective-permute-start(bf16[32,4096]{1,0:T(8,128)(2,1)S(1)} %pad_maximum_fusion.refs_0_), channel_id=1, source_target_pairs={{0,30},{1,3},{2,4},{3,1},{4,2},{5,7},{6,8},{7,5},{8,6},{9,11},{10,... | collective-permute-start | bytes 786440 | tf_op jit(solution)/shard_map/ppermute | solution.py:128
  8.1 0.6 collective-permute-done.refs_1_
  8.7 8.7 %collective-permute-start.2 = (bf16[32,4096]{1,0:T(8,128)(2,1)S(1)}, bf16[32,4096]{1,0:T(8,128)(2,1)S(1)}, u32[]{:S(2)}, u32[]{:S(2)}) collective-permute-start(bf16[32,4096]{1,0:T(8,128)(2,1)S(1)} %collective-permute-done.refs_1_), channel_id=1, source_target_pairs={{0,3},{1,30},{2,1},{3,4},{4,7},{5,2},{6,5},{7,8},{8,11},{9,6},{10,... | collective-permute-start | bytes 786440 | tf_op jit(solution)/shard_map/ppermute | solution.py:130
  17.4 5.6 %collective-permute-start.3 = (bf16[32,4096]{1,0:T(8,128)(2,1)S(1)}, bf16[32,4096]{1,0:T(8,128)(2,1)S(1)}, u32[]{:S(2)}, u32[]{:S(2)}) collective-permute-start(bf16[32,4096]{1,0:T(8,128)(2,1)S(1)} %collective-permute-done.1.refs_2_), channel_id=1, source_target_pairs={{0,3},{1,30},{2,1},{3,4},{4,7},{5,2},{6,5},{7,8},{8,11},{9,6},{10,... | collective-permute-start | bytes 786440 | tf_op jit(solution)/shard_map/ppermute | solution.py:132
  23.0 0.0 collective-permute-done.2.refs_3_
  23.1 3.3 %collective-permute-start.4 = (bf16[32,4096]{1,0:T(8,128)(2,1)S(1)}, bf16[32,4096]{1,0:T(8,128)(2,1)S(1)}, u32[]{:S(2)}, u32[]{:S(2)}) collective-permute-start(bf16[32,4096]{1,0:T(8,128)(2,1)S(1)} %collective-permute-done.2.refs_3_), channel_id=1, source_target_pairs={{0,3},{1,30},{2,1},{3,4},{4,7},{5,2},{6,5},{7,8},{8,11},{9,6},{10,... | collective-permute-start | bytes 786440 | tf_op jit(solution)/shard_map/ppermute | solution.py:130
  26.3 0.6 collective-permute-done.3.refs_4_
  26.9 5.0 %collective-permute-start.5 = (bf16[32,4096]{1,0:T(8,128)(2,1)S(1)}, bf16[32,4096]{1,0:T(8,128)(2,1)S(1)}, u32[]{:S(2)}, u32[]{:S(2)}) collective-permute-start(bf16[32,4096]{1,0:T(8,128)(2,1)S(1)} %collective-permute-done.3.refs_4_), channel_id=1, source_target_pairs={{0,3},{1,30},{2,1},{3,4},{4,7},{5,2},{6,5},{7,8},{8,11},{9,6},{10,... | collective-permute-start | bytes 786440 | tf_op jit(solution)/shard_map/ppermute | solution.py:132
  31.9 3.3 %collective-permute-start.6 = (bf16[32,4096]{1,0:T(8,128)(2,1)S(1)}, bf16[32,4096]{1,0:T(8,128)(2,1)S(1)}, u32[]{:S(2)}, u32[]{:S(2)}) collective-permute-start(bf16[32,4096]{1,0:T(8,128)(2,1)S(1)} %collective-permute-done.4.refs_5_), channel_id=1, source_target_pairs={{0,3},{1,30},{2,1},{3,4},{4,7},{5,2},{6,5},{7,8},{8,11},{9,6},{10,... | collective-permute-start | bytes 786440 | tf_op jit(solution)/shard_map/ppermute | solution.py:130
  35.2 0.6 collective-permute-done.5.refs_6_
  35.8 5.0 %collective-permute-start.7 = (bf16[32,4096]{1,0:T(8,128)(2,1)S(1)}, bf16[32,4096]{1,0:T(8,128)(2,1)S(1)}, u32[]{:S(2)}, u32[]{:S(2)}) collective-permute-start(bf16[32,4096]{1,0:T(8,128)(2,1)S(1)} %collective-permute-done.5.refs_6_), channel_id=1, source_target_pairs={{0,3},{1,30},{2,1},{3,4},{4,7},{5,2},{6,5},{7,8},{8,11},{9,6},{10,... | collective-permute-start | bytes 786440 | tf_op jit(solution)/shard_map/ppermute | solution.py:132
  40.8 0.0 collective-permute-done.6.refs_0_
  40.8 3.3 %collective-permute-start.8 = (bf16[32,4096]{1,0:T(8,128)(2,1)S(1)}, bf16[32,4096]{1,0:T(8,128)(2,1)S(1)}, u32[]{:S(2)}, u32[]{:S(2)}) collective-permute-start(bf16[32,4096]{1,0:T(8,128)(2,1)S(1)} %collective-permute-done.6.refs_0_), channel_id=1, source_target_pairs={{0,3},{1,30},{2,1},{3,4},{4,7},{5,2},{6,5},{7,8},{8,11},{9,6},{10,... | collective-permute-start | bytes 786440 | tf_op jit(solution)/shard_map/ppermute | solution.py:130
  44.1 0.6 collective-permute-done.7.refs_1_
  44.7 5.0 %collective-permute-start.9 = (bf16[32,4096]{1,0:T(8,128)(2,1)S(1)}, bf16[32,4096]{1,0:T(8,128)(2,1)S(1)}, u32[]{:S(2)}, u32[]{:S(2)}) collective-permute-start(bf16[32,4096]{1,0:T(8,128)(2,1)S(1)} %collective-permute-done.7.refs_1_), channel_id=1, source_target_pairs={{0,3},{1,30},{2,1},{3,4},{4,7},{5,2},{6,5},{7,8},{8,11},{9,6},{10,... | collective-permute-start | bytes 786440 | tf_op jit(solution)/shard_map/ppermute | solution.py:132
  49.7 5.1 %collective-permute-start.13 = (bf16[128,4096]{1,0:T(8,128)(2,1)}, bf16[128,4096]{1,0:T(8,128)(2,1)S(1)}, u32[]{:S(2)}, u32[]{:S(2)}) collective-permute-start(bf16[128,4096]{1,0:T(8,128)(2,1)} %bitcast.24), channel_id=1, source_target_pairs={{0,32},{32,0},{1,33},{33,1},{2,34},{34,2},{3,35},{35,3},{4,36},{36... | collective-permute-start | bytes 3145736 | tf_op jit(solution)/shard_map/ppermute | solution.py:136
  54.8 0.1 stack.3
  55.0 1.9 %collective-permute-start.10 = (bf16[2,112,4096]{2,1,0:T(8,128)(2,1)S(1)}, bf16[2,112,4096]{2,1,0:T(8,128)(2,1)S(1)}, u32[]{:S(2)}, u32[]{:S(2)}) collective-permute-start(bf16[2,112,4096]{2,1,0:T(8,128)(2,1)S(1)} %stack.3), channel_id=1, source_target_pairs={{0,1},{1,0},{2,3},{3,2},{4,5},{5,4},{6,7},{7,6},{8,9},{9,8},{10,11... | collective-permute-start | bytes 5505032 | tf_op jit(solution)/shard_map/ppermute | solution.py:140
  56.9 0.0 collective-permute-done.9.refs_3_
  56.9 0.1 stack.4
  57.0 2.4 %collective-permute-start.11 = (bf16[2,64,4096]{2,1,0:T(8,128)(2,1)S(1)}, bf16[2,64,4096]{2,1,0:T(8,128)(2,1)S(1)}, u32[]{:S(2)}, u32[]{:S(2)}) collective-permute-start(bf16[2,64,4096]{2,1,0:T(8,128)(2,1)S(1)} %stack.4), channel_id=1, source_target_pairs={{0,1},{1,0},{2,3},{3,2},{4,5},{5,4},{6,7},{7,6},{8,9},{9,8},{10,11... | collective-permute-start | bytes 3145736 | tf_op jit(solution)/shard_map/ppermute | solution.py:140
  59.4 2.6 %collective-permute-start.14 = (bf16[32,4096]{1,0:T(8,128)(2,1)S(1)}, bf16[32,4096]{1,0:T(8,128)(2,1)S(1)}, u32[]{:S(2)}, u32[]{:S(2)}) collective-permute-start(bf16[32,4096]{1,0:T(8,128)(2,1)S(1)} %collective-permute-done.8.refs_2_), channel_id=1, source_target_pairs={{0,3},{1,30},{2,1},{3,4},{4,7},{5,2},{6,5},{7,8},{8,11},{9,6},{10,... | collective-permute-start | bytes 786440 | tf_op jit(solution)/shard_map/ppermute | solution.py:130
  62.0 2.2 %collective-permute-start.15 = (bf16[32,4096]{1,0:T(8,128)(2,1)S(1)}, bf16[32,4096]{1,0:T(8,128)(2,1)S(1)}, u32[]{:S(2)}, u32[]{:S(2)}) collective-permute-start(bf16[32,4096]{1,0:T(8,128)(2,1)S(1)} %collective-permute-done.9.refs_3_), channel_id=1, source_target_pairs={{0,3},{1,30},{2,1},{3,4},{4,7},{5,2},{6,5},{7,8},{8,11},{9,6},{10,... | collective-permute-start | bytes 786440 | tf_op jit(solution)/shard_map/ppermute | solution.py:132
  64.3 0.1 slice_bitcast_fusion.3
  64.4 0.0 copy-start.1
  64.4 2.7 %collective-permute-done.14.refs_0_ = bf16[32,4096]{1,0:T(8,128)(2,1)S(1)} collective-permute-done((bf16[32,4096]{1,0:T(8,128)(2,1)S(1)}, bf16[32,4096]{1,0:T(8,128)(2,1)S(1)}, u32[]{:S(2)}, u32[]{:S(2)}) %collective-permute-start.14) | collective-permute-done | bytes 262176 | tf_op jit(solution)/shard_map/ppermute | solution.py:130
  67.1 2.9 %collective-permute-start.16 = (bf16[32,4096]{1,0:T(8,128)(2,1)S(1)}, bf16[32,4096]{1,0:T(8,128)(2,1)S(1)}, u32[]{:S(2)}, u32[]{:S(2)}) collective-permute-start(bf16[32,4096]{1,0:T(8,128)(2,1)S(1)} %collective-permute-done.14.refs_0_), channel_id=1, source_target_pairs={{0,3},{1,30},{2,1},{3,4},{4,7},{5,2},{6,5},{7,8},{8,11},{9,6},{10,... | collective-permute-start | bytes 786440 | tf_op jit(solution)/shard_map/ppermute | solution.py:130
  70.0 0.0 collective-permute-done.15.refs_1_
  70.0 3.1 %collective-permute-start.17 = (bf16[32,4096]{1,0:T(8,128)(2,1)S(1)}, bf16[32,4096]{1,0:T(8,128)(2,1)S(1)}, u32[]{:S(2)}, u32[]{:S(2)}) collective-permute-start(bf16[32,4096]{1,0:T(8,128)(2,1)S(1)} %collective-permute-done.15.refs_1_), channel_id=1, source_target_pairs={{0,3},{1,30},{2,1},{3,4},{4,7},{5,2},{6,5},{7,8},{8,11},{9,6},{10,... | collective-permute-start | bytes 786440 | tf_op jit(solution)/shard_map/ppermute | solution.py:132
  73.2 0.1 slice_bitcast_fusion.7
  73.2 1.5 %collective-permute-done.16.refs_2_ = bf16[32,4096]{1,0:T(8,128)(2,1)S(1)} collective-permute-done((bf16[32,4096]{1,0:T(8,128)(2,1)S(1)}, bf16[32,4096]{1,0:T(8,128)(2,1)S(1)}, u32[]{:S(2)}, u32[]{:S(2)}) %collective-permute-start.16) | collective-permute-done | bytes 262176 | tf_op jit(solution)/shard_map/ppermute | solution.py:130
  74.8 2.9 %collective-permute-start.12 = (bf16[128,4096]{1,0:T(8,128)(2,1)S(1)}, bf16[128,4096]{1,0:T(8,128)(2,1)S(1)}, u32[]{:S(2)}, u32[]{:S(2)}) collective-permute-start(bf16[128,4096]{1,0:T(8,128)(2,1)S(1)} %bitcast.27), channel_id=1, source_target_pairs={{0,32},{32,0},{1,33},{33,1},{2,34},{34,2},{3,35},{35,3},{4,36},{36... | collective-permute-start | bytes 3145736 | tf_op jit(solution)/shard_map/ppermute | solution.py:135
  77.7 0.1 collective-permute-done.17.refs_3_
  77.7 0.1 stack.5.refs_0_
  77.8 2.5 %collective-permute-start.19 = (bf16[2,64,4096]{2,1,0:T(8,128)(2,1)S(1)}, bf16[2,64,4096]{2,1,0:T(8,128)(2,1)S(1)}, u32[]{:S(2)}, u32[]{:S(2)}) collective-permute-start(bf16[2,64,4096]{2,1,0:T(8,128)(2,1)S(1)} %stack.5.refs_0_), channel_id=1, source_target_pairs={{0,1},{1,0},{2,3},{3,2},{4,5},{5,4},{6,7},{7,6},{8,9},{9,8},{10,11... | collective-permute-start | bytes 3145736 | tf_op jit(solution)/shard_map/ppermute | solution.py:140
  80.3 4.8 %collective-permute-start.18 = (bf16[32,4096]{1,0:T(8,128)(2,1)S(1)}, bf16[32,4096]{1,0:T(8,128)(2,1)S(1)}, u32[]{:S(2)}, u32[]{:S(2)}) collective-permute-start(bf16[32,4096]{1,0:T(8,128)(2,1)S(1)} %collective-permute-done.16.refs_2_), channel_id=1, source_target_pairs={{0,3},{1,30},{2,1},{3,4},{4,7},{5,2},{6,5},{7,8},{8,11},{9,6},{10,... | collective-permute-start | bytes 786440 | tf_op jit(solution)/shard_map/ppermute | solution.py:130
  85.1 0.1 slice_bitcast_fusion.6
  85.2 0.0 copy-start
  85.2 2.1 %collective-permute-start.20 = (bf16[32,4096]{1,0:T(8,128)(2,1)S(1)}, bf16[32,4096]{1,0:T(8,128)(2,1)S(1)}, u32[]{:S(2)}, u32[]{:S(2)}) collective-permute-start(bf16[32,4096]{1,0:T(8,128)(2,1)S(1)} %collective-permute-done.16.refs_2_), channel_id=1, source_target_pairs={{0,2},{1,31},{2,0},{3,5},{4,6},{5,3},{6,4},{7,9},{8,10},{9,7},{10,... | collective-permute-start | bytes 786440 | tf_op jit(solution)/shard_map/ppermute | solution.py:133
  87.3 0.1 slice_bitcast_fusion.2
  87.4 0.9 fusion.8
  88.4 15.5 %collective-permute-done.12.refs_5_ = bf16[128,4096]{1,0:T(8,128)(2,1)S(1)} collective-permute-done((bf16[128,4096]{1,0:T(8,128)(2,1)S(1)}, bf16[128,4096]{1,0:T(8,128)(2,1)S(1)}, u32[]{:S(2)}, u32[]{:S(2)}) %collective-permute-start.12) | collective-permute-done | bytes 1048608 | tf_op jit(solution)/shard_map/ppermute | solution.py:135
  103.8 0.9 fusion.27.early
  104.8 1.8 %finish.1 = f32[512,256]{1,0:T(8,128)S(1)} custom-call(f32[352,256]{1,0:T(8,128)S(1)} %fusion.27.early, bf16[2,64,4096]{2,1,0:T(8,128)(2,1)S(1)} %stack.5.refs_0_, bf16[2,16,4096]{2,1,0:T(8,128)(2,1)S(1)} %bitcast.30, bf16[2,64,4096]{2,1,0:T(8,128)(2,1)S(1)} %collective-permute-done.19.refs_2_, bf16[2,16,4096]{2,1,0:T(8,128)(2,1)S(1)} %bitcast.31, ...), custom_call_target="tpu_custom_call" | custom-call | flops 671088640 | tf_op jit(solution)/shard_map/finish/pallas_call | solution.py:81
  106.6 13.8 %all_to_all.5.got = f32[8,64,256]{2,1,0:T(8,128)S(1)} all-to-all(f32[8,64,256]{2,1,0:T(8,128)S(1)} %bitcast.23), channel_id=1, replica_groups=mesh['layer'=8,'trow'=2,'tcol'=32] {'layer'}, dimensions={0} | all-to-all | bytes 1048576 | tf_op jit(solution)/shard_map/all_to_all | solution.py:153
  120.5 0.7 layer_sum.1
  (11 shorter events, 0.0 us)
Async XLA Ops:
  1.0 7.7 %collective-permute-start = (bf16[32,4096]{1,0:T(8,128)(2,1)S(1)}, bf16[32,4096]{1,0:T(8,128)(2,1)S(1)}, u32[]{:S(2)}, u32[]{:S(2)}) collective-permute-start(bf16[32,4096]{1,0:T(8,128)(2,1)S(1)} %pad_maximum_fusion.refs_0_), channel_id=1, source_target_pairs={{0,3},{1,30},{2,1},{3,4},{4,7},{5,2},{6,5},{7,8},{8,11},{9,6},{10,... | collective-permute-start | bytes 786440 | tf_op jit(solution)/shard_map/ppermute | solution.py:128
  2.9 14.5 %collective-permute-start.1 = (bf16[32,4096]{1,0:T(8,128)(2,1)S(1)}, bf16[32,4096]{1,0:T(8,128)(2,1)S(1)}, u32[]{:S(2)}, u32[]{:S(2)}) collective-permute-start(bf16[32,4096]{1,0:T(8,128)(2,1)S(1)} %pad_maximum_fusion.refs_0_), channel_id=1, source_target_pairs={{0,30},{1,3},{2,4},{3,1},{4,2},{5,7},{6,8},{7,5},{8,6},{9,11},{10,... | collective-permute-start | bytes 786440 | tf_op jit(solution)/shard_map/ppermute | solution.py:128
  8.7 14.4 %collective-permute-start.2 = (bf16[32,4096]{1,0:T(8,128)(2,1)S(1)}, bf16[32,4096]{1,0:T(8,128)(2,1)S(1)}, u32[]{:S(2)}, u32[]{:S(2)}) collective-permute-start(bf16[32,4096]{1,0:T(8,128)(2,1)S(1)} %collective-permute-done.refs_1_), channel_id=1, source_target_pairs={{0,3},{1,30},{2,1},{3,4},{4,7},{5,2},{6,5},{7,8},{8,11},{9,6},{10,... | collective-permute-start | bytes 786440 | tf_op jit(solution)/shard_map/ppermute | solution.py:130
  17.4 9.5 %collective-permute-start.3 = (bf16[32,4096]{1,0:T(8,128)(2,1)S(1)}, bf16[32,4096]{1,0:T(8,128)(2,1)S(1)}, u32[]{:S(2)}, u32[]{:S(2)}) collective-permute-start(bf16[32,4096]{1,0:T(8,128)(2,1)S(1)} %collective-permute-done.1.refs_2_), channel_id=1, source_target_pairs={{0,3},{1,30},{2,1},{3,4},{4,7},{5,2},{6,5},{7,8},{8,11},{9,6},{10,... | collective-permute-start | bytes 786440 | tf_op jit(solution)/shard_map/ppermute | solution.py:132
  23.1 8.9 %collective-permute-start.4 = (bf16[32,4096]{1,0:T(8,128)(2,1)S(1)}, bf16[32,4096]{1,0:T(8,128)(2,1)S(1)}, u32[]{:S(2)}, u32[]{:S(2)}) collective-permute-start(bf16[32,4096]{1,0:T(8,128)(2,1)S(1)} %collective-permute-done.2.refs_3_), channel_id=1, source_target_pairs={{0,3},{1,30},{2,1},{3,4},{4,7},{5,2},{6,5},{7,8},{8,11},{9,6},{10,... | collective-permute-start | bytes 786440 | tf_op jit(solution)/shard_map/ppermute | solution.py:130
  26.9 8.9 %collective-permute-start.5 = (bf16[32,4096]{1,0:T(8,128)(2,1)S(1)}, bf16[32,4096]{1,0:T(8,128)(2,1)S(1)}, u32[]{:S(2)}, u32[]{:S(2)}) collective-permute-start(bf16[32,4096]{1,0:T(8,128)(2,1)S(1)} %collective-permute-done.3.refs_4_), channel_id=1, source_target_pairs={{0,3},{1,30},{2,1},{3,4},{4,7},{5,2},{6,5},{7,8},{8,11},{9,6},{10,... | collective-permute-start | bytes 786440 | tf_op jit(solution)/shard_map/ppermute | solution.py:132
  31.9 8.9 %collective-permute-start.6 = (bf16[32,4096]{1,0:T(8,128)(2,1)S(1)}, bf16[32,4096]{1,0:T(8,128)(2,1)S(1)}, u32[]{:S(2)}, u32[]{:S(2)}) collective-permute-start(bf16[32,4096]{1,0:T(8,128)(2,1)S(1)} %collective-permute-done.4.refs_5_), channel_id=1, source_target_pairs={{0,3},{1,30},{2,1},{3,4},{4,7},{5,2},{6,5},{7,8},{8,11},{9,6},{10,... | collective-permute-start | bytes 786440 | tf_op jit(solution)/shard_map/ppermute | solution.py:130
  35.8 8.9 %collective-permute-start.7 = (bf16[32,4096]{1,0:T(8,128)(2,1)S(1)}, bf16[32,4096]{1,0:T(8,128)(2,1)S(1)}, u32[]{:S(2)}, u32[]{:S(2)}) collective-permute-start(bf16[32,4096]{1,0:T(8,128)(2,1)S(1)} %collective-permute-done.5.refs_6_), channel_id=1, source_target_pairs={{0,3},{1,30},{2,1},{3,4},{4,7},{5,2},{6,5},{7,8},{8,11},{9,6},{10,... | collective-permute-start | bytes 786440 | tf_op jit(solution)/shard_map/ppermute | solution.py:132
  40.8 16.1 %collective-permute-start.8 = (bf16[32,4096]{1,0:T(8,128)(2,1)S(1)}, bf16[32,4096]{1,0:T(8,128)(2,1)S(1)}, u32[]{:S(2)}, u32[]{:S(2)}) collective-permute-start(bf16[32,4096]{1,0:T(8,128)(2,1)S(1)} %collective-permute-done.6.refs_0_), channel_id=1, source_target_pairs={{0,3},{1,30},{2,1},{3,4},{4,7},{5,2},{6,5},{7,8},{8,11},{9,6},{10,... | collective-permute-start | bytes 786440 | tf_op jit(solution)/shard_map/ppermute | solution.py:130
  44.7 12.2 %collective-permute-start.9 = (bf16[32,4096]{1,0:T(8,128)(2,1)S(1)}, bf16[32,4096]{1,0:T(8,128)(2,1)S(1)}, u32[]{:S(2)}, u32[]{:S(2)}) collective-permute-start(bf16[32,4096]{1,0:T(8,128)(2,1)S(1)} %collective-permute-done.7.refs_1_), channel_id=1, source_target_pairs={{0,3},{1,30},{2,1},{3,4},{4,7},{5,2},{6,5},{7,8},{8,11},{9,6},{10,... | collective-permute-start | bytes 786440 | tf_op jit(solution)/shard_map/ppermute | solution.py:132
  49.7 37.7 %collective-permute-start.13 = (bf16[128,4096]{1,0:T(8,128)(2,1)}, bf16[128,4096]{1,0:T(8,128)(2,1)S(1)}, u32[]{:S(2)}, u32[]{:S(2)}) collective-permute-start(bf16[128,4096]{1,0:T(8,128)(2,1)} %bitcast.24), channel_id=1, source_target_pairs={{0,32},{32,0},{1,33},{33,1},{2,34},{34,2},{3,35},{35,3},{4,36},{36... | collective-permute-start | bytes 3145736 | tf_op jit(solution)/shard_map/ppermute | solution.py:136
  55.0 30.2 %collective-permute-start.10 = (bf16[2,112,4096]{2,1,0:T(8,128)(2,1)S(1)}, bf16[2,112,4096]{2,1,0:T(8,128)(2,1)S(1)}, u32[]{:S(2)}, u32[]{:S(2)}) collective-permute-start(bf16[2,112,4096]{2,1,0:T(8,128)(2,1)S(1)} %stack.3), channel_id=1, source_target_pairs={{0,1},{1,0},{2,3},{3,2},{4,5},{5,4},{6,7},{7,6},{8,9},{9,8},{10,11... | collective-permute-start | bytes 5505032 | tf_op jit(solution)/shard_map/ppermute | solution.py:140
  57.0 23.3 %collective-permute-start.11 = (bf16[2,64,4096]{2,1,0:T(8,128)(2,1)S(1)}, bf16[2,64,4096]{2,1,0:T(8,128)(2,1)S(1)}, u32[]{:S(2)}, u32[]{:S(2)}) collective-permute-start(bf16[2,64,4096]{2,1,0:T(8,128)(2,1)S(1)} %stack.4), channel_id=1, source_target_pairs={{0,1},{1,0},{2,3},{3,2},{4,5},{5,4},{6,7},{7,6},{8,9},{9,8},{10,11... | collective-permute-start | bytes 3145736 | tf_op jit(solution)/shard_map/ppermute | solution.py:140
  59.4 7.7 %collective-permute-start.14 = (bf16[32,4096]{1,0:T(8,128)(2,1)S(1)}, bf16[32,4096]{1,0:T(8,128)(2,1)S(1)}, u32[]{:S(2)}, u32[]{:S(2)}) collective-permute-start(bf16[32,4096]{1,0:T(8,128)(2,1)S(1)} %collective-permute-done.8.refs_2_), channel_id=1, source_target_pairs={{0,3},{1,30},{2,1},{3,4},{4,7},{5,2},{6,5},{7,8},{8,11},{9,6},{10,... | collective-permute-start | bytes 786440 | tf_op jit(solution)/shard_map/ppermute | solution.py:130
  62.0 8.0 %collective-permute-start.15 = (bf16[32,4096]{1,0:T(8,128)(2,1)S(1)}, bf16[32,4096]{1,0:T(8,128)(2,1)S(1)}, u32[]{:S(2)}, u32[]{:S(2)}) collective-permute-start(bf16[32,4096]{1,0:T(8,128)(2,1)S(1)} %collective-permute-done.9.refs_3_), channel_id=1, source_target_pairs={{0,3},{1,30},{2,1},{3,4},{4,7},{5,2},{6,5},{7,8},{8,11},{9,6},{10,... | collective-permute-start | bytes 786440 | tf_op jit(solution)/shard_map/ppermute | solution.py:132
  64.4 10.4 %copy-start.1 = (bf16[1,128,4096]{2,1,0:T(8,128)(2,1)S(1)}, bf16[1,128,4096]{2,1,0:T(8,128)(2,1)}, u32[]{:S(2)}) copy-start(bf16[1,128,4096]{2,1,0:T(8,128)(2,1)} %param.6) | copy-start | bytes 3145732
  67.1 7.7 %collective-permute-start.16 = (bf16[32,4096]{1,0:T(8,128)(2,1)S(1)}, bf16[32,4096]{1,0:T(8,128)(2,1)S(1)}, u32[]{:S(2)}, u32[]{:S(2)}) collective-permute-start(bf16[32,4096]{1,0:T(8,128)(2,1)S(1)} %collective-permute-done.14.refs_0_), channel_id=1, source_target_pairs={{0,3},{1,30},{2,1},{3,4},{4,7},{5,2},{6,5},{7,8},{8,11},{9,6},{10,... | collective-permute-start | bytes 786440 | tf_op jit(solution)/shard_map/ppermute | solution.py:130
  70.0 7.7 %collective-permute-start.17 = (bf16[32,4096]{1,0:T(8,128)(2,1)S(1)}, bf16[32,4096]{1,0:T(8,128)(2,1)S(1)}, u32[]{:S(2)}, u32[]{:S(2)}) collective-permute-start(bf16[32,4096]{1,0:T(8,128)(2,1)S(1)} %collective-permute-done.15.refs_1_), channel_id=1, source_target_pairs={{0,3},{1,30},{2,1},{3,4},{4,7},{5,2},{6,5},{7,8},{8,11},{9,6},{10,... | collective-permute-start | bytes 786440 | tf_op jit(solution)/shard_map/ppermute | solution.py:132
  74.8 29.1 %collective-permute-start.12 = (bf16[128,4096]{1,0:T(8,128)(2,1)S(1)}, bf16[128,4096]{1,0:T(8,128)(2,1)S(1)}, u32[]{:S(2)}, u32[]{:S(2)}) collective-permute-start(bf16[128,4096]{1,0:T(8,128)(2,1)S(1)} %bitcast.27), channel_id=1, source_target_pairs={{0,32},{32,0},{1,33},{33,1},{2,34},{34,2},{3,35},{35,3},{4,36},{36... | collective-permute-start | bytes 3145736 | tf_op jit(solution)/shard_map/ppermute | solution.py:135
  77.8 27.0 %collective-permute-start.19 = (bf16[2,64,4096]{2,1,0:T(8,128)(2,1)S(1)}, bf16[2,64,4096]{2,1,0:T(8,128)(2,1)S(1)}, u32[]{:S(2)}, u32[]{:S(2)}) collective-permute-start(bf16[2,64,4096]{2,1,0:T(8,128)(2,1)S(1)} %stack.5.refs_0_), channel_id=1, source_target_pairs={{0,1},{1,0},{2,3},{3,2},{4,5},{5,4},{6,7},{7,6},{8,9},{9,8},{10,11... | collective-permute-start | bytes 3145736 | tf_op jit(solution)/shard_map/ppermute | solution.py:140
  80.3 24.5 %collective-permute-start.18 = (bf16[32,4096]{1,0:T(8,128)(2,1)S(1)}, bf16[32,4096]{1,0:T(8,128)(2,1)S(1)}, u32[]{:S(2)}, u32[]{:S(2)}) collective-permute-start(bf16[32,4096]{1,0:T(8,128)(2,1)S(1)} %collective-permute-done.16.refs_2_), channel_id=1, source_target_pairs={{0,3},{1,30},{2,1},{3,4},{4,7},{5,2},{6,5},{7,8},{8,11},{9,6},{10,... | collective-permute-start | bytes 786440 | tf_op jit(solution)/shard_map/ppermute | solution.py:130
  85.2 2.2 %copy-start = (bf16[1,128,4096]{2,1,0:T(8,128)(2,1)S(1)}, bf16[1,128,4096]{2,1,0:T(8,128)(2,1)}, u32[]{:S(2)}) copy-start(bf16[1,128,4096]{2,1,0:T(8,128)(2,1)} %param.7) | copy-start | bytes 3145732
  85.2 19.6 %collective-permute-start.20 = (bf16[32,4096]{1,0:T(8,128)(2,1)S(1)}, bf16[32,4096]{1,0:T(8,128)(2,1)S(1)}, u32[]{:S(2)}, u32[]{:S(2)}) collective-permute-start(bf16[32,4096]{1,0:T(8,128)(2,1)S(1)} %collective-permute-done.16.refs_2_), channel_id=1, source_target_pairs={{0,2},{1,31},{2,0},{3,5},{4,6},{5,3},{6,4},{7,9},{8,10},{9,7},{10,... | collective-permute-start | bytes 786440 | tf_op jit(solution)/shard_map/ppermute | solution.py:133

commit v8 on v7

--- a/solution.py
+++ b/solution.py
@@ -12,8 +12,8 @@
 VMEM = pl.BlockSpec(memory_space=pltpu.VMEM)
 GROUPS = (
     ((0, 0), (0, 1), (1, 1), (0, 2), (1, 2), (0, 3), (1, 3)),
-    ((0, 4), (1, 4), (0, 5), (1, 5)),
-    ((0, 6), (1, 6), (0, 7), (1, 7)),
+    ((0, 4), (1, 4), (0, 5), (1, 5), (0, 6), (1, 6)),
+    ((0, 7), (1, 7)),
 )
 
 
@@ -38,8 +38,9 @@
     )(*parts)
 
 
-def finish_kernel(height, depth, early, *refs):
-    stacks = refs[:-7]
+def finish_kernel(height, depth, *refs):
+    n_early = len(GROUPS) - 1
+    early, stacks = refs[:n_early], refs[n_early:-7]
     own_act, other_act, own_back, other_back, out, act, back = refs[-7:]
     tcol = lax.axis_index("tcol")
     z, core = lax.shift_right_logical(tcol, 1), lax.rem(tcol, 2)
@@ -53,9 +54,9 @@
         at = pl.multiple_of((lax.rem(plane + planes, planes) * 2 + on) * height, height)
         out[pl.ds(at, height), :] = rows
 
-    first = [shard for group in GROUPS[:-1] for shard in group]
-    for i, shard in enumerate(first + first):
-        put(early[i * height : (i + 1) * height, :], shard, int(i >= len(first)))
+    for terms, group in zip(early, GROUPS):
+        for i, shard in enumerate(group + group):
+            put(terms[i * height : (i + 1) * height, :], shard, int(i >= len(group)))
 
     late = list(GROUPS[-1]) + [(0, planes // 2)]
     at = 0
@@ -80,14 +81,14 @@
     late = sum(s.shape[1] for s in stacks)
     return pl.pallas_call(
         functools.partial(finish_kernel, height, depth),
-        out_shape=jax.ShapeDtypeStruct((2 * planes * height, 2 * width), early.dtype),
-        in_specs=[VMEM] * (1 + len(stacks) + len(cols)),
+        out_shape=jax.ShapeDtypeStruct((2 * planes * height, 2 * width), early[0].dtype),
+        in_specs=[VMEM] * (len(early) + len(stacks) + len(cols)),
         out_specs=VMEM,
         scratch_shapes=[pltpu.VMEM((late, depth), cols[0].dtype)] * 2,
         compiler_params=pltpu.CompilerParams(vmem_limit_bytes=12 * MIB),
         cost_estimate=pl.CostEstimate(flops=8 * late * width * depth, bytes_accessed=0, transcendentals=0),
         name="finish",
-    )(early, *stacks, *cols)
+    )(*early, *stacks, *cols)
 
 
 def sum_kernel(got, out):
@@ -141,11 +142,13 @@
 
     cols_act = jnp.concatenate((act_cols[0], other_act), axis=0)
     cols_back = jnp.concatenate((back_cols[0], other_back), axis=0)
-    early = mine[:-1] + given[:-1]
-    act, back = (jnp.concatenate([rows[kind] for rows in early], axis=0) for kind in range(2))
-    gram_act = jnp.einsum("rd,cd->rc", act, cols_act, preferred_element_type=jnp.float32)
-    gram_back = jnp.einsum("rd,cd->rc", back, cols_back, preferred_element_type=jnp.float32)
-    terms = gram_act * gram_back / depth
+    terms = []
+    for i in range(len(GROUPS) - 1):
+        rows = jnp.concatenate((mine[i][0], given[i][0]), axis=0)
+        gram_act = jnp.einsum("rd,cd->rc", rows, cols_act, preferred_element_type=jnp.float32)
+        rows = jnp.concatenate((mine[i][1], given[i][1]), axis=0)
+        gram_back = jnp.einsum("rd,cd->rc", rows, cols_back, preferred_element_type=jnp.float32)
+        terms.append(gram_act * gram_back / depth)
     height = act_rows.shape[1]
     last = [s.reshape(2, height, depth) for s in last]
     stacks = (mine[-1], last[0], given[-1], last[1])

time: 122 us -> 127 us (1.041)
  the two profiles are of different devices: /device:TPU:32 before, /device:TPU:24 now
where the time goes in v8:
time: 127 us; the launch traced here: 125 us
  starting transfers between devices  61.3 us (48%)
  waiting for transfers between devices  42.8 us (34%)
  blocking collectives  13.4 us (11%)
  matrix products  3.28 us (3%)
  Pallas kernels  2.22 us (2%)
    ppermute x7, waiting for transfers between devices, local(): held[0, step] = lax.ppermute(held[0, step - 1], 'tcol', along)  18.8 us
    ppermute x1, waiting for transfers between devices, local(): other_act = lax.ppermute(act_cols[0], 'trow', across)  14.7 us
    ppermute x7, starting transfers between devices, local(): held[0, step] = lax.ppermute(held[0, step - 1], 'tcol', along)  14.4 us
    all_to_all x1, blocking collectives, local(): lax.all_to_all(terms.reshape(layers, -1, terms.shape[-1]), 'layer', 0, 0,...  13.4 us
    ppermute x6, starting transfers between devices, local(): held[1, step] = lax.ppermute(held[1, step - 1], 'tcol', along)  12.7 us
    ppermute x1, starting transfers between devices, local(): lax.ppermute(own, 'tcol', aslant)  10.5 us
    ppermute x3, starting transfers between devices, local(): given.append(lax.ppermute(mine[i], 'tcol', cores))  9.06 us
    ppermute x6, waiting for transfers between devices, local(): held[1, step] = lax.ppermute(held[1, step - 1], 'tcol', along)  6.85 us
  transfers between devices with their start and end apart: 21, of which 12 were waited for; matrix products, arithmetic and copies ran while one was open for 3% of the time, Pallas kernels for 0%

profile of v8, /device:TPU:24, one launch (start us, length us, event | category | flops | bytes accessed | tf_op | source)
XLA Modules:
  0.0 124.9 jit_solution(11317256907423251247)
XLA Ops:
  0.0 1.0 pad_maximum_fusion.14.refs_0_
  1.0 3.3 %collective-permute-start = (bf16[32,4096]{1,0:T(8,128)(2,1)S(1)}, bf16[32,4096]{1,0:T(8,128)(2,1)S(1)}, u32[]{:S(2)}, u32[]{:S(2)}) collective-permute-start(bf16[32,4096]{1,0:T(8,128)(2,1)S(1)} %pad_maximum_fusion.14.refs_0_), channel_id=1, source_target_pairs={{0,3},{1,30},{2,1},{3,4},{4,7},{5,2},{6,5},{7,8},{8,11},{9,6},{10,... | collective-permute-start | bytes 786440 | tf_op jit(solution)/shard_map/ppermute | solution.py:129
  4.3 10.5 %collective-permute-start.1 = (bf16[32,4096]{1,0:T(8,128)(2,1)S(1)}, bf16[32,4096]{1,0:T(8,128)(2,1)S(1)}, u32[]{:S(2)}, u32[]{:S(2)}) collective-permute-start(bf16[32,4096]{1,0:T(8,128)(2,1)S(1)} %pad_maximum_fusion.14.refs_0_), channel_id=1, source_target_pairs={{0,30},{1,3},{2,4},{3,1},{4,2},{5,7},{6,8},{7,5},{8,6},{9,11},{10,... | collective-permute-start | bytes 786440 | tf_op jit(solution)/shard_map/ppermute | solution.py:129
  14.8 1.1 collective-permute-done.refs_1_
  15.9 1.9 %collective-permute-start.2 = (bf16[32,4096]{1,0:T(8,128)(2,1)S(1)}, bf16[32,4096]{1,0:T(8,128)(2,1)S(1)}, u32[]{:S(2)}, u32[]{:S(2)}) collective-permute-start(bf16[32,4096]{1,0:T(8,128)(2,1)S(1)} %collective-permute-done.refs_1_), channel_id=1, source_target_pairs={{0,3},{1,30},{2,1},{3,4},{4,7},{5,2},{6,5},{7,8},{8,11},{9,6},{10,... | collective-permute-start | bytes 786440 | tf_op jit(solution)/shard_map/ppermute | solution.py:131
  17.8 1.3 %collective-permute-done.1.refs_2_ = bf16[32,4096]{1,0:T(8,128)(2,1)S(1)} collective-permute-done((bf16[32,4096]{1,0:T(8,128)(2,1)S(1)}, bf16[32,4096]{1,0:T(8,128)(2,1)S(1)}, u32[]{:S(2)}, u32[]{:S(2)}) %collective-permute-start.1) | collective-permute-done | bytes 262176 | tf_op jit(solution)/shard_map/ppermute | solution.py:129
  19.1 2.3 %collective-permute-start.3 = (bf16[32,4096]{1,0:T(8,128)(2,1)S(1)}, bf16[32,4096]{1,0:T(8,128)(2,1)S(1)}, u32[]{:S(2)}, u32[]{:S(2)}) collective-permute-start(bf16[32,4096]{1,0:T(8,128)(2,1)S(1)} %collective-permute-done.1.refs_2_), channel_id=1, source_target_pairs={{0,3},{1,30},{2,1},{3,4},{4,7},{5,2},{6,5},{7,8},{8,11},{9,6},{10,... | collective-permute-start | bytes 786440 | tf_op jit(solution)/shard_map/ppermute | solution.py:133
  21.4 3.3 %collective-permute-done.2.refs_3_ = bf16[32,4096]{1,0:T(8,128)(2,1)S(1)} collective-permute-done((bf16[32,4096]{1,0:T(8,128)(2,1)S(1)}, bf16[32,4096]{1,0:T(8,128)(2,1)S(1)}, u32[]{:S(2)}, u32[]{:S(2)}) %collective-permute-start.2) | collective-permute-done | bytes 262176 | tf_op jit(solution)/shard_map/ppermute | solution.py:131
  24.8 1.9 %collective-permute-start.4 = (bf16[32,4096]{1,0:T(8,128)(2,1)S(1)}, bf16[32,4096]{1,0:T(8,128)(2,1)S(1)}, u32[]{:S(2)}, u32[]{:S(2)}) collective-permute-start(bf16[32,4096]{1,0:T(8,128)(2,1)S(1)} %collective-permute-done.2.refs_3_), channel_id=1, source_target_pairs={{0,3},{1,30},{2,1},{3,4},{4,7},{5,2},{6,5},{7,8},{8,11},{9,6},{10,... | collective-permute-start | bytes 786440 | tf_op jit(solution)/shard_map/ppermute | solution.py:131
  26.7 1.3 %collective-permute-done.3.refs_4_ = bf16[32,4096]{1,0:T(8,128)(2,1)S(1)} collective-permute-done((bf16[32,4096]{1,0:T(8,128)(2,1)S(1)}, bf16[32,4096]{1,0:T(8,128)(2,1)S(1)}, u32[]{:S(2)}, u32[]{:S(2)}) %collective-permute-start.3) | collective-permute-done | bytes 262176 | tf_op jit(solution)/shard_map/ppermute | solution.py:133
  28.0 1.9 %collective-permute-start.5 = (bf16[32,4096]{1,0:T(8,128)(2,1)S(1)}, bf16[32,4096]{1,0:T(8,128)(2,1)S(1)}, u32[]{:S(2)}, u32[]{:S(2)}) collective-permute-start(bf16[32,4096]{1,0:T(8,128)(2,1)S(1)} %collective-permute-done.3.refs_4_), channel_id=1, source_target_pairs={{0,3},{1,30},{2,1},{3,4},{4,7},{5,2},{6,5},{7,8},{8,11},{9,6},{10,... | collective-permute-start | bytes 786440 | tf_op jit(solution)/shard_map/ppermute | solution.py:133
  29.9 3.8 %collective-permute-done.4.refs_5_ = bf16[32,4096]{1,0:T(8,128)(2,1)S(1)} collective-permute-done((bf16[32,4096]{1,0:T(8,128)(2,1)S(1)}, bf16[32,4096]{1,0:T(8,128)(2,1)S(1)}, u32[]{:S(2)}, u32[]{:S(2)}) %collective-permute-start.4) | collective-permute-done | bytes 262176 | tf_op jit(solution)/shard_map/ppermute | solution.py:131
  33.7 1.9 %collective-permute-start.9 = (bf16[32,4096]{1,0:T(8,128)(2,1)S(1)}, bf16[32,4096]{1,0:T(8,128)(2,1)S(1)}, u32[]{:S(2)}, u32[]{:S(2)}) collective-permute-start(bf16[32,4096]{1,0:T(8,128)(2,1)S(1)} %collective-permute-done.4.refs_5_), channel_id=1, source_target_pairs={{0,3},{1,30},{2,1},{3,4},{4,7},{5,2},{6,5},{7,8},{8,11},{9,6},{10,... | collective-permute-start | bytes 786440 | tf_op jit(solution)/shard_map/ppermute | solution.py:131
  35.6 1.3 %collective-permute-done.5.refs_6_ = bf16[32,4096]{1,0:T(8,128)(2,1)S(1)} collective-permute-done((bf16[32,4096]{1,0:T(8,128)(2,1)S(1)}, bf16[32,4096]{1,0:T(8,128)(2,1)S(1)}, u32[]{:S(2)}, u32[]{:S(2)}) %collective-permute-start.5) | collective-permute-done | bytes 262176 | tf_op jit(solution)/shard_map/ppermute | solution.py:133
  36.9 1.9 %collective-permute-start.10 = (bf16[32,4096]{1,0:T(8,128)(2,1)S(1)}, bf16[32,4096]{1,0:T(8,128)(2,1)S(1)}, u32[]{:S(2)}, u32[]{:S(2)}) collective-permute-start(bf16[32,4096]{1,0:T(8,128)(2,1)S(1)} %collective-permute-done.5.refs_6_), channel_id=1, source_target_pairs={{0,3},{1,30},{2,1},{3,4},{4,7},{5,2},{6,5},{7,8},{8,11},{9,6},{10,... | collective-permute-start | bytes 786440 | tf_op jit(solution)/shard_map/ppermute | solution.py:133
  38.8 3.8 %collective-permute-done.9.refs_0_ = bf16[32,4096]{1,0:T(8,128)(2,1)S(1)} collective-permute-done((bf16[32,4096]{1,0:T(8,128)(2,1)S(1)}, bf16[32,4096]{1,0:T(8,128)(2,1)S(1)}, u32[]{:S(2)}, u32[]{:S(2)}) %collective-permute-start.9) | collective-permute-done | bytes 262176 | tf_op jit(solution)/shard_map/ppermute | solution.py:131
  42.6 1.9 %collective-permute-start.11 = (bf16[32,4096]{1,0:T(8,128)(2,1)S(1)}, bf16[32,4096]{1,0:T(8,128)(2,1)S(1)}, u32[]{:S(2)}, u32[]{:S(2)}) collective-permute-start(bf16[32,4096]{1,0:T(8,128)(2,1)S(1)} %collective-permute-done.9.refs_0_), channel_id=1, source_target_pairs={{0,3},{1,30},{2,1},{3,4},{4,7},{5,2},{6,5},{7,8},{8,11},{9,6},{10,... | collective-permute-start | bytes 786440 | tf_op jit(solution)/shard_map/ppermute | solution.py:131
  44.5 1.3 %collective-permute-done.10.refs_1_ = bf16[32,4096]{1,0:T(8,128)(2,1)S(1)} collective-permute-done((bf16[32,4096]{1,0:T(8,128)(2,1)S(1)}, bf16[32,4096]{1,0:T(8,128)(2,1)S(1)}, u32[]{:S(2)}, u32[]{:S(2)}) %collective-permute-start.10) | collective-permute-done | bytes 262176 | tf_op jit(solution)/shard_map/ppermute | solution.py:133
  45.8 1.9 %collective-permute-start.12 = (bf16[32,4096]{1,0:T(8,128)(2,1)S(1)}, bf16[32,4096]{1,0:T(8,128)(2,1)S(1)}, u32[]{:S(2)}, u32[]{:S(2)}) collective-permute-start(bf16[32,4096]{1,0:T(8,128)(2,1)S(1)} %collective-permute-done.10.refs_1_), channel_id=1, source_target_pairs={{0,3},{1,30},{2,1},{3,4},{4,7},{5,2},{6,5},{7,8},{8,11},{9,6},{10,... | collective-permute-start | bytes 786440 | tf_op jit(solution)/shard_map/ppermute | solution.py:133
  47.7 3.1 %collective-permute-start.8 = (bf16[128,4096]{1,0:T(8,128)(2,1)}, bf16[128,4096]{1,0:T(8,128)(2,1)S(1)}, u32[]{:S(2)}, u32[]{:S(2)}) collective-permute-start(bf16[128,4096]{1,0:T(8,128)(2,1)} %bitcast.24), channel_id=1, source_target_pairs={{0,32},{32,0},{1,33},{33,1},{2,34},{34,2},{3,35},{35,3},{4,36},{36... | collective-permute-start | bytes 3145736 | tf_op jit(solution)/shard_map/ppermute | solution.py:137
  50.8 0.1 stack.3
  51.0 5.0 %collective-permute-start.6 = (bf16[2,112,4096]{2,1,0:T(8,128)(2,1)S(1)}, bf16[2,112,4096]{2,1,0:T(8,128)(2,1)S(1)}, u32[]{:S(2)}, u32[]{:S(2)}) collective-permute-start(bf16[2,112,4096]{2,1,0:T(8,128)(2,1)S(1)} %stack.3), channel_id=1, source_target_pairs={{0,1},{1,0},{2,3},{3,2},{4,5},{5,4},{6,7},{7,6},{8,9},{9,8},{10,11... | collective-permute-start | bytes 5505032 | tf_op jit(solution)/shard_map/ppermute | solution.py:141
  55.9 2.9 %collective-permute-start.13 = (bf16[32,4096]{1,0:T(8,128)(2,1)S(1)}, bf16[32,4096]{1,0:T(8,128)(2,1)S(1)}, u32[]{:S(2)}, u32[]{:S(2)}) collective-permute-start(bf16[32,4096]{1,0:T(8,128)(2,1)S(1)} %collective-permute-done.11.refs_2_), channel_id=1, source_target_pairs={{0,3},{1,30},{2,1},{3,4},{4,7},{5,2},{6,5},{7,8},{8,11},{9,6},{10,... | collective-permute-start | bytes 786440 | tf_op jit(solution)/shard_map/ppermute | solution.py:131
  58.9 1.9 %collective-permute-start.14 = (bf16[32,4096]{1,0:T(8,128)(2,1)S(1)}, bf16[32,4096]{1,0:T(8,128)(2,1)S(1)}, u32[]{:S(2)}, u32[]{:S(2)}) collective-permute-start(bf16[32,4096]{1,0:T(8,128)(2,1)S(1)} %collective-permute-done.12.refs_3_), channel_id=1, source_target_pairs={{0,3},{1,30},{2,1},{3,4},{4,7},{5,2},{6,5},{7,8},{8,11},{9,6},{10,... | collective-permute-start | bytes 786440 | tf_op jit(solution)/shard_map/ppermute | solution.py:133
  60.8 0.2 slice_bitcast_fusion.3
  61.0 3.9 %collective-permute-done.13.refs_4_ = bf16[32,4096]{1,0:T(8,128)(2,1)S(1)} collective-permute-done((bf16[32,4096]{1,0:T(8,128)(2,1)S(1)}, bf16[32,4096]{1,0:T(8,128)(2,1)S(1)}, u32[]{:S(2)}, u32[]{:S(2)}) %collective-permute-start.13) | collective-permute-done | bytes 262176 | tf_op jit(solution)/shard_map/ppermute | solution.py:131
  64.8 2.9 %collective-permute-done.14.refs_5_ = bf16[32,4096]{1,0:T(8,128)(2,1)S(1)} collective-permute-done((bf16[32,4096]{1,0:T(8,128)(2,1)S(1)}, bf16[32,4096]{1,0:T(8,128)(2,1)S(1)}, u32[]{:S(2)}, u32[]{:S(2)}) %collective-permute-start.14) | collective-permute-done | bytes 262176 | tf_op jit(solution)/shard_map/ppermute | solution.py:133
  67.8 0.1 stack.4
  67.9 0.0 copy-start.1
  67.9 2.1 %collective-permute-start.15 = (bf16[2,96,4096]{2,1,0:T(8,128)(2,1)S(1)}, bf16[2,96,4096]{2,1,0:T(8,128)(2,1)S(1)}, u32[]{:S(2)}, u32[]{:S(2)}) collective-permute-start(bf16[2,96,4096]{2,1,0:T(8,128)(2,1)S(1)} %stack.4), channel_id=1, source_target_pairs={{0,1},{1,0},{2,3},{3,2},{4,5},{5,4},{6,7},{7,6},{8,9},{9,8},{10,11... | collective-permute-start | bytes 4718600 | tf_op jit(solution)/shard_map/ppermute | solution.py:141
  70.0 1.9 %collective-permute-start.16 = (bf16[32,4096]{1,0:T(8,128)(2,1)S(1)}, bf16[32,4096]{1,0:T(8,128)(2,1)S(1)}, u32[]{:S(2)}, u32[]{:S(2)}) collective-permute-start(bf16[32,4096]{1,0:T(8,128)(2,1)S(1)} %collective-permute-done.13.refs_4_), channel_id=1, source_target_pairs={{0,3},{1,30},{2,1},{3,4},{4,7},{5,2},{6,5},{7,8},{8,11},{9,6},{10,... | collective-permute-start | bytes 786440 | tf_op jit(solution)/shard_map/ppermute | solution.py:131
  71.9 2.7 %collective-permute-start.17 = (bf16[32,4096]{1,0:T(8,128)(2,1)S(1)}, bf16[32,4096]{1,0:T(8,128)(2,1)S(1)}, u32[]{:S(2)}, u32[]{:S(2)}) collective-permute-start(bf16[32,4096]{1,0:T(8,128)(2,1)S(1)} %collective-permute-done.14.refs_5_), channel_id=1, source_target_pairs={{0,3},{1,30},{2,1},{3,4},{4,7},{5,2},{6,5},{7,8},{8,11},{9,6},{10,... | collective-permute-start | bytes 786440 | tf_op jit(solution)/shard_map/ppermute | solution.py:133
  74.6 0.1 slice_bitcast_fusion.7
  74.8 4.1 %collective-permute-done.16.refs_0_ = bf16[32,4096]{1,0:T(8,128)(2,1)S(1)} collective-permute-done((bf16[32,4096]{1,0:T(8,128)(2,1)S(1)}, bf16[32,4096]{1,0:T(8,128)(2,1)S(1)}, u32[]{:S(2)}, u32[]{:S(2)}) %collective-permute-start.16) | collective-permute-done | bytes 262176 | tf_op jit(solution)/shard_map/ppermute | solution.py:131
  78.9 4.2 %collective-permute-start.7 = (bf16[128,4096]{1,0:T(8,128)(2,1)S(1)}, bf16[128,4096]{1,0:T(8,128)(2,1)S(1)}, u32[]{:S(2)}, u32[]{:S(2)}) collective-permute-start(bf16[128,4096]{1,0:T(8,128)(2,1)S(1)} %bitcast.28), channel_id=1, source_target_pairs={{0,32},{32,0},{1,33},{33,1},{2,34},{34,2},{3,35},{35,3},{4,36},{36... | collective-permute-start | bytes 3145736 | tf_op jit(solution)/shard_map/ppermute | solution.py:136
  83.1 2.1 %collective-permute-start.19 = (bf16[2,32,4096]{2,1,0:T(8,128)(2,1)S(1)}, bf16[2,32,4096]{2,1,0:T(8,128)(2,1)S(1)}, u32[]{:S(2)}, u32[]{:S(2)}) collective-permute-start(bf16[2,32,4096]{2,1,0:T(8,128)(2,1)S(1)} %stack.5.refs_2_), channel_id=1, source_target_pairs={{0,1},{1,0},{2,3},{3,2},{4,5},{5,4},{6,7},{7,6},{8,9},{9,8},{10,11... | collective-permute-start | bytes 1572872 | tf_op jit(solution)/shard_map/ppermute | solution.py:141
  85.2 1.9 %collective-permute-start.18 = (bf16[32,4096]{1,0:T(8,128)(2,1)S(1)}, bf16[32,4096]{1,0:T(8,128)(2,1)S(1)}, u32[]{:S(2)}, u32[]{:S(2)}) collective-permute-start(bf16[32,4096]{1,0:T(8,128)(2,1)S(1)} %collective-permute-done.16.refs_0_), channel_id=1, source_target_pairs={{0,3},{1,30},{2,1},{3,4},{4,7},{5,2},{6,5},{7,8},{8,11},{9,6},{10,... | collective-permute-start | bytes 786440 | tf_op jit(solution)/shard_map/ppermute | solution.py:131
  87.1 0.2 slice_bitcast_fusion.2
  87.3 4.0 %collective-permute-start.20 = (bf16[32,4096]{1,0:T(8,128)(2,1)S(1)}, bf16[32,4096]{1,0:T(8,128)(2,1)S(1)}, u32[]{:S(2)}, u32[]{:S(2)}) collective-permute-start(bf16[32,4096]{1,0:T(8,128)(2,1)S(1)} %collective-permute-done.16.refs_0_), channel_id=1, source_target_pairs={{0,2},{1,31},{2,0},{3,5},{4,6},{5,3},{6,4},{7,9},{8,10},{9,7},{10,... | collective-permute-start | bytes 786440 | tf_op jit(solution)/shard_map/ppermute | solution.py:134
  91.4 0.8 fusion.4
  92.2 14.7 %collective-permute-done.7.refs_7_ = bf16[128,4096]{1,0:T(8,128)(2,1)S(1)} collective-permute-done((bf16[128,4096]{1,0:T(8,128)(2,1)S(1)}, bf16[128,4096]{1,0:T(8,128)(2,1)S(1)}, u32[]{:S(2)}, u32[]{:S(2)}) %collective-permute-start.7) | collective-permute-done | bytes 1048608 | tf_op jit(solution)/shard_map/ppermute | solution.py:136
  106.9 0.8 fusion.19.refs_0_
  107.7 0.1 slice_bitcast_fusion.6
  107.9 0.8 fusion.12
  108.7 0.9 fusion.25.refs_1_
  109.6 1.3 %finish.1 = f32[512,256]{1,0:T(8,128)S(1)} custom-call(f32[224,256]{1,0:T(8,128)S(1)} %fusion.19.refs_0_, f32[192,256]{1,0:T(8,128)S(1)} %fusion.25.refs_1_, bf16[2,32,4096]{2,1,0:T(8,128)(2,1)S(1)} %stack.5.refs_2_, bf16[2,16,4096]{2,1,0:T(8,128)(2,1)S(1)} %bitcast.32, bf16[2,32,4096]{2,1,0:T(8,128)(2,1)S(1)} %collective-permute-done.19.refs_4_, ...), custom_call_target="tpu_custom_call" | custom-call | flops 402653184 | tf_op jit(solution)/shard_map/finish/pallas_call | solution.py:82
  110.9 13.4 %all_to_all.5.got = f32[8,64,256]{2,1,0:T(8,128)S(1)} all-to-all(f32[8,64,256]{2,1,0:T(8,128)S(1)} %bitcast.23), channel_id=1, replica_groups=mesh['layer'=8,'trow'=2,'tcol'=32] {'layer'}, dimensions={0} | all-to-all | bytes 1048576 | tf_op jit(solution)/shard_map/all_to_all | solution.py:156
  124.3 0.7 layer_sum.1
  (13 shorter events, 0.1 us)
Async XLA Ops:
  1.0 14.9 %collective-permute-start = (bf16[32,4096]{1,0:T(8,128)(2,1)S(1)}, bf16[32,4096]{1,0:T(8,128)(2,1)S(1)}, u32[]{:S(2)}, u32[]{:S(2)}) collective-permute-start(bf16[32,4096]{1,0:T(8,128)(2,1)S(1)} %pad_maximum_fusion.14.refs_0_), channel_id=1, source_target_pairs={{0,3},{1,30},{2,1},{3,4},{4,7},{5,2},{6,5},{7,8},{8,11},{9,6},{10,... | collective-permute-start | bytes 786440 | tf_op jit(solution)/shard_map/ppermute | solution.py:129
  4.3 14.8 %collective-permute-start.1 = (bf16[32,4096]{1,0:T(8,128)(2,1)S(1)}, bf16[32,4096]{1,0:T(8,128)(2,1)S(1)}, u32[]{:S(2)}, u32[]{:S(2)}) collective-permute-start(bf16[32,4096]{1,0:T(8,128)(2,1)S(1)} %pad_maximum_fusion.14.refs_0_), channel_id=1, source_target_pairs={{0,30},{1,3},{2,4},{3,1},{4,2},{5,7},{6,8},{7,5},{8,6},{9,11},{10,... | collective-permute-start | bytes 786440 | tf_op jit(solution)/shard_map/ppermute | solution.py:129
  15.9 8.9 %collective-permute-start.2 = (bf16[32,4096]{1,0:T(8,128)(2,1)S(1)}, bf16[32,4096]{1,0:T(8,128)(2,1)S(1)}, u32[]{:S(2)}, u32[]{:S(2)}) collective-permute-start(bf16[32,4096]{1,0:T(8,128)(2,1)S(1)} %collective-permute-done.refs_1_), channel_id=1, source_target_pairs={{0,3},{1,30},{2,1},{3,4},{4,7},{5,2},{6,5},{7,8},{8,11},{9,6},{10,... | collective-permute-start | bytes 786440 | tf_op jit(solution)/shard_map/ppermute | solution.py:131
  19.1 8.9 %collective-permute-start.3 = (bf16[32,4096]{1,0:T(8,128)(2,1)S(1)}, bf16[32,4096]{1,0:T(8,128)(2,1)S(1)}, u32[]{:S(2)}, u32[]{:S(2)}) collective-permute-start(bf16[32,4096]{1,0:T(8,128)(2,1)S(1)} %collective-permute-done.1.refs_2_), channel_id=1, source_target_pairs={{0,3},{1,30},{2,1},{3,4},{4,7},{5,2},{6,5},{7,8},{8,11},{9,6},{10,... | collective-permute-start | bytes 786440 | tf_op jit(solution)/shard_map/ppermute | solution.py:133
  24.8 8.9 %collective-permute-start.4 = (bf16[32,4096]{1,0:T(8,128)(2,1)S(1)}, bf16[32,4096]{1,0:T(8,128)(2,1)S(1)}, u32[]{:S(2)}, u32[]{:S(2)}) collective-permute-start(bf16[32,4096]{1,0:T(8,128)(2,1)S(1)} %collective-permute-done.2.refs_3_), channel_id=1, source_target_pairs={{0,3},{1,30},{2,1},{3,4},{4,7},{5,2},{6,5},{7,8},{8,11},{9,6},{10,... | collective-permute-start | bytes 786440 | tf_op jit(solution)/shard_map/ppermute | solution.py:131
  28.0 8.9 %collective-permute-start.5 = (bf16[32,4096]{1,0:T(8,128)(2,1)S(1)}, bf16[32,4096]{1,0:T(8,128)(2,1)S(1)}, u32[]{:S(2)}, u32[]{:S(2)}) collective-permute-start(bf16[32,4096]{1,0:T(8,128)(2,1)S(1)} %collective-permute-done.3.refs_4_), channel_id=1, source_target_pairs={{0,3},{1,30},{2,1},{3,4},{4,7},{5,2},{6,5},{7,8},{8,11},{9,6},{10,... | collective-permute-start | bytes 786440 | tf_op jit(solution)/shard_map/ppermute | solution.py:133
  33.7 8.9 %collective-permute-start.9 = (bf16[32,4096]{1,0:T(8,128)(2,1)S(1)}, bf16[32,4096]{1,0:T(8,128)(2,1)S(1)}, u32[]{:S(2)}, u32[]{:S(2)}) collective-permute-start(bf16[32,4096]{1,0:T(8,128)(2,1)S(1)} %collective-permute-done.4.refs_5_), channel_id=1, source_target_pairs={{0,3},{1,30},{2,1},{3,4},{4,7},{5,2},{6,5},{7,8},{8,11},{9,6},{10,... | collective-permute-start | bytes 786440 | tf_op jit(solution)/shard_map/ppermute | solution.py:131
  36.9 8.9 %collective-permute-start.10 = (bf16[32,4096]{1,0:T(8,128)(2,1)S(1)}, bf16[32,4096]{1,0:T(8,128)(2,1)S(1)}, u32[]{:S(2)}, u32[]{:S(2)}) collective-permute-start(bf16[32,4096]{1,0:T(8,128)(2,1)S(1)} %collective-permute-done.5.refs_6_), channel_id=1, source_target_pairs={{0,3},{1,30},{2,1},{3,4},{4,7},{5,2},{6,5},{7,8},{8,11},{9,6},{10,... | collective-permute-start | bytes 786440 | tf_op jit(solution)/shard_map/ppermute | solution.py:133
  42.6 13.4 %collective-permute-start.11 = (bf16[32,4096]{1,0:T(8,128)(2,1)S(1)}, bf16[32,4096]{1,0:T(8,128)(2,1)S(1)}, u32[]{:S(2)}, u32[]{:S(2)}) collective-permute-start(bf16[32,4096]{1,0:T(8,128)(2,1)S(1)} %collective-permute-done.9.refs_0_), channel_id=1, source_target_pairs={{0,3},{1,30},{2,1},{3,4},{4,7},{5,2},{6,5},{7,8},{8,11},{9,6},{10,... | collective-permute-start | bytes 786440 | tf_op jit(solution)/shard_map/ppermute | solution.py:131
  45.8 13.1 %collective-permute-start.12 = (bf16[32,4096]{1,0:T(8,128)(2,1)S(1)}, bf16[32,4096]{1,0:T(8,128)(2,1)S(1)}, u32[]{:S(2)}, u32[]{:S(2)}) collective-permute-start(bf16[32,4096]{1,0:T(8,128)(2,1)S(1)} %collective-permute-done.10.refs_1_), channel_id=1, source_target_pairs={{0,3},{1,30},{2,1},{3,4},{4,7},{5,2},{6,5},{7,8},{8,11},{9,6},{10,... | collective-permute-start | bytes 786440 | tf_op jit(solution)/shard_map/ppermute | solution.py:133
  47.7 39.6 %collective-permute-start.8 = (bf16[128,4096]{1,0:T(8,128)(2,1)}, bf16[128,4096]{1,0:T(8,128)(2,1)S(1)}, u32[]{:S(2)}, u32[]{:S(2)}) collective-permute-start(bf16[128,4096]{1,0:T(8,128)(2,1)} %bitcast.24), channel_id=1, source_target_pairs={{0,32},{32,0},{1,33},{33,1},{2,34},{34,2},{3,35},{35,3},{4,36},{36... | collective-permute-start | bytes 3145736 | tf_op jit(solution)/shard_map/ppermute | solution.py:137
  51.0 34.2 %collective-permute-start.6 = (bf16[2,112,4096]{2,1,0:T(8,128)(2,1)S(1)}, bf16[2,112,4096]{2,1,0:T(8,128)(2,1)S(1)}, u32[]{:S(2)}, u32[]{:S(2)}) collective-permute-start(bf16[2,112,4096]{2,1,0:T(8,128)(2,1)S(1)} %stack.3), channel_id=1, source_target_pairs={{0,1},{1,0},{2,3},{3,2},{4,5},{5,4},{6,7},{7,6},{8,9},{9,8},{10,11... | collective-permute-start | bytes 5505032 | tf_op jit(solution)/shard_map/ppermute | solution.py:141
  55.9 8.9 %collective-permute-start.13 = (bf16[32,4096]{1,0:T(8,128)(2,1)S(1)}, bf16[32,4096]{1,0:T(8,128)(2,1)S(1)}, u32[]{:S(2)}, u32[]{:S(2)}) collective-permute-start(bf16[32,4096]{1,0:T(8,128)(2,1)S(1)} %collective-permute-done.11.refs_2_), channel_id=1, source_target_pairs={{0,3},{1,30},{2,1},{3,4},{4,7},{5,2},{6,5},{7,8},{8,11},{9,6},{10,... | collective-permute-start | bytes 786440 | tf_op jit(solution)/shard_map/ppermute | solution.py:131
  58.9 8.9 %collective-permute-start.14 = (bf16[32,4096]{1,0:T(8,128)(2,1)S(1)}, bf16[32,4096]{1,0:T(8,128)(2,1)S(1)}, u32[]{:S(2)}, u32[]{:S(2)}) collective-permute-start(bf16[32,4096]{1,0:T(8,128)(2,1)S(1)} %collective-permute-done.12.refs_3_), channel_id=1, source_target_pairs={{0,3},{1,30},{2,1},{3,4},{4,7},{5,2},{6,5},{7,8},{8,11},{9,6},{10,... | collective-permute-start | bytes 786440 | tf_op jit(solution)/shard_map/ppermute | solution.py:133
  67.9 11.0 %copy-start.1 = (bf16[1,128,4096]{2,1,0:T(8,128)(2,1)S(1)}, bf16[1,128,4096]{2,1,0:T(8,128)(2,1)}, u32[]{:S(2)}) copy-start(bf16[1,128,4096]{2,1,0:T(8,128)(2,1)} %param.6) | copy-start | bytes 3145732
  67.9 39.8 %collective-permute-start.15 = (bf16[2,96,4096]{2,1,0:T(8,128)(2,1)S(1)}, bf16[2,96,4096]{2,1,0:T(8,128)(2,1)S(1)}, u32[]{:S(2)}, u32[]{:S(2)}) collective-permute-start(bf16[2,96,4096]{2,1,0:T(8,128)(2,1)S(1)} %stack.4), channel_id=1, source_target_pairs={{0,1},{1,0},{2,3},{3,2},{4,5},{5,4},{6,7},{7,6},{8,9},{9,8},{10,11... | collective-permute-start | bytes 4718600 | tf_op jit(solution)/shard_map/ppermute | solution.py:141
  70.0 8.9 %collective-permute-start.16 = (bf16[32,4096]{1,0:T(8,128)(2,1)S(1)}, bf16[32,4096]{1,0:T(8,128)(2,1)S(1)}, u32[]{:S(2)}, u32[]{:S(2)}) collective-permute-start(bf16[32,4096]{1,0:T(8,128)(2,1)S(1)} %collective-permute-done.13.refs_4_), channel_id=1, source_target_pairs={{0,3},{1,30},{2,1},{3,4},{4,7},{5,2},{6,5},{7,8},{8,11},{9,6},{10,... | collective-permute-start | bytes 786440 | tf_op jit(solution)/shard_map/ppermute | solution.py:131
  71.9 11.2 %collective-permute-start.17 = (bf16[32,4096]{1,0:T(8,128)(2,1)S(1)}, bf16[32,4096]{1,0:T(8,128)(2,1)S(1)}, u32[]{:S(2)}, u32[]{:S(2)}) collective-permute-start(bf16[32,4096]{1,0:T(8,128)(2,1)S(1)} %collective-permute-done.14.refs_5_), channel_id=1, source_target_pairs={{0,3},{1,30},{2,1},{3,4},{4,7},{5,2},{6,5},{7,8},{8,11},{9,6},{10,... | collective-permute-start | bytes 786440 | tf_op jit(solution)/shard_map/ppermute | solution.py:133
  78.9 28.0 %collective-permute-start.7 = (bf16[128,4096]{1,0:T(8,128)(2,1)S(1)}, bf16[128,4096]{1,0:T(8,128)(2,1)S(1)}, u32[]{:S(2)}, u32[]{:S(2)}) collective-permute-start(bf16[128,4096]{1,0:T(8,128)(2,1)S(1)} %bitcast.28), channel_id=1, source_target_pairs={{0,32},{32,0},{1,33},{33,1},{2,34},{34,2},{3,35},{35,3},{4,36},{36... | collective-permute-start | bytes 3145736 | tf_op jit(solution)/shard_map/ppermute | solution.py:136
  83.1 8.2 %copy-start = (bf16[1,128,4096]{2,1,0:T(8,128)(2,1)S(1)}, bf16[1,128,4096]{2,1,0:T(8,128)(2,1)}, u32[]{:S(2)}) copy-start(bf16[1,128,4096]{2,1,0:T(8,128)(2,1)} %param.7) | copy-start | bytes 3145732
  83.1 26.5 %collective-permute-start.19 = (bf16[2,32,4096]{2,1,0:T(8,128)(2,1)S(1)}, bf16[2,32,4096]{2,1,0:T(8,128)(2,1)S(1)}, u32[]{:S(2)}, u32[]{:S(2)}) collective-permute-start(bf16[2,32,4096]{2,1,0:T(8,128)(2,1)S(1)} %stack.5.refs_2_), channel_id=1, source_target_pairs={{0,1},{1,0},{2,3},{3,2},{4,5},{5,4},{6,7},{7,6},{8,9},{9,8},{10,11... | collective-permute-start | bytes 1572872 | tf_op jit(solution)/shard_map/ppermute | solution.py:141
  85.2 24.4 %collective-permute-start.18 = (bf16[32,4096]{1,0:T(8,128)(2,1)S(1)}, bf16[32,4096]{1,0:T(8,128)(2,1)S(1)}, u32[]{:S(2)}, u32[]{:S(2)}) collective-permute-start(bf16[32,4096]{1,0:T(8,128)(2,1)S(1)} %collective-permute-done.16.refs_0_), channel_id=1, source_target_pairs={{0,3},{1,30},{2,1},{3,4},{4,7},{5,2},{6,5},{7,8},{8,11},{9,6},{10,... | collective-permute-start | bytes 786440 | tf_op jit(solution)/shard_map/ppermute | solution.py:131
  87.3 22.3 %collective-permute-start.20 = (bf16[32,4096]{1,0:T(8,128)(2,1)S(1)}, bf16[32,4096]{1,0:T(8,128)(2,1)S(1)}, u32[]{:S(2)}, u32[]{:S(2)}) collective-permute-start(bf16[32,4096]{1,0:T(8,128)(2,1)S(1)} %collective-permute-done.16.refs_0_), channel_id=1, source_target_pairs={{0,2},{1,31},{2,0},{3,5},{4,6},{5,3},{6,4},{7,9},{8,10},{9,7},{10,... | collective-permute-start | bytes 786440 | tf_op jit(solution)/shard_map/ppermute | solution.py:134
